TPU v7x, 32 devices: a whole 2x2x4 slice. The times are simulated.
32 devices in a mesh: dp: 32 (over z, y, x, core).
Axes of the slice: x: 2, y: 2, z: 4, core: 2. Of those that a mesh axis runs over, the one named last changes fastest.
Arguments:
- tokens: bfloat16 [32768, 1024], P('dp'), may hold values from -6 to 6
- segment_ids: int32 [64, 512], P('dp'), may hold values from 0 to 15, never falling along the last dimension, each value on 1 to 256 neighbouring positions
- out_grad: bfloat16 [32768, 1024], P('dp'), may hold values from -6 to 6
- qkv_master: float32 [3145728], P('dp'), may hold values from -0.1875 to 0.1875
- qkv_first: float32 [3145728], P('dp'), may hold values from -320 to 320
- qkv_second: float32 [3145728], P('dp'), may hold values from 327.68 to 32768
- proj_master: float32 [1048576], P('dp'), may hold values from -1 to 1
- proj_first: float32 [1048576], P('dp'), may hold values from -320 to 320
- proj_second: float32 [1048576], P('dp'), may hold values from 327.68 to 32768
- up_master: float32 [4194304], P('dp'), may hold values from -0.1875 to 0.1875
- up_first: float32 [4194304], P('dp'), may hold values from -320 to 320
- up_second: float32 [4194304], P('dp'), may hold values from 327.68 to 32768
- down_master: float32 [4194304], P('dp'), may hold values from -0.09375 to 0.09375
- down_first: float32 [4194304], P('dp'), may hold values from -320 to 320
- down_second: float32 [4194304], P('dp'), may hold values from 327.68 to 32768
- vector_master: float32 [12288], P('dp'), may hold values from -1.5 to 1.5, as said below
- vector_first: float32 [12288], P('dp'), may hold values from -320 to 320
- vector_second: float32 [12288], P('dp'), may hold values from 327.68 to 32768
Outputs:
- layer_out: bfloat16 [32768, 1024], P('dp')
- input_grad: bfloat16 [32768, 1024], P('dp')
- qkv_grad: float32 [3145728], P('dp')
- qkv_first_new: float32 [3145728], P('dp')
- qkv_second_new: float32 [3145728], P('dp')
- qkv_master_new: float32 [3145728], P('dp')
- qkv_copy: bfloat16 [3145728], P('dp')
- proj_grad: float32 [1048576], P('dp')
- proj_first_new: float32 [1048576], P('dp')
- proj_second_new: float32 [1048576], P('dp')
- proj_master_new: float32 [1048576], P('dp')
- proj_copy: bfloat16 [1048576], P('dp')
- up_grad: float32 [4194304], P('dp')
- up_first_new: float32 [4194304], P('dp')
- up_second_new: float32 [4194304], P('dp')
- up_master_new: float32 [4194304], P('dp')
- up_copy: bfloat16 [4194304], P('dp')
- down_grad: float32 [4194304], P('dp')
- down_first_new: float32 [4194304], P('dp')
- down_second_new: float32 [4194304], P('dp')
- down_master_new: float32 [4194304], P('dp')
- down_copy: bfloat16 [4194304], P('dp')
- vector_grad: float32 [12288], P('dp')
- vector_first_new: float32 [12288], P('dp')
- vector_second_new: float32 [12288], P('dp')
- vector_master_new: float32 [12288], P('dp')
- vector_copy: bfloat16 [12288], P('dp')
Inputs may be any that keep to these rules, and one draw needn't show every extreme that they name: `segment_ids`: ids never fall along a sequence; tokens attend only to tokens of the same id. `vector_master`: the two norm gains lie in 0.5 to 1.5.
All inputs are finite; a program needn't handle non-finite values.
Results may differ from a plain program's by a relative error of at most 0.012.
The roundings to bfloat16 on the way count: a program that leaves them out, or rounds other values in their place, can miss the bound.
Values may be sent and summed in bfloat16 or wider, within the bound.
A program may use at most 256 MiB of HBM per device.

v0:
```python
import jax
import jax.numpy as jnp
from jax import lax
from jax.sharding import PartitionSpec as P

D = 1024
HEADS = 16
HEAD_DIM = 64
FF = 4096
MB = 2
STEP = 3


NORM_EPS = 1e-05
BETA_FIRST = 0.5
BETA_SECOND = 0.5
ADAM_EPS = 1e-08
WEIGHT_DECAY = 0.01
MASK_FILL = -1000000000.0
RATES = (0.01, 0.03, 0.01, 0.005, 0.05)


def layer_norm(hidden, gain, shift):
    center = hidden - jnp.mean(hidden, axis=-1, keepdims=True)
    spread = jnp.mean(center * center, axis=-1, keepdims=True)
    return center * lax.rsqrt(spread + NORM_EPS) * gain + shift


def gelu_exact(values):
    return jax.nn.gelu(values, approximate=False)


def split_vector(vector):
    return (
        vector[0:D],
        vector[D : 2 * D],
        vector[2 * D : 3 * D],
        vector[3 * D : 4 * D],
        vector[4 * D : 5 * D],
        vector[5 * D : 5 * D + FF],
        vector[5 * D + FF : 6 * D + FF],
        vector[6 * D + FF : 7 * D + FF],
        vector[7 * D + FF : 8 * D + FF],
    )


def weight_grad(left_rows, right_rows):
    return lax.dot_general(
        left_rows, right_rows, (((0,), (0,)), ((), ())), preferred_element_type=jnp.float32
    )


def back_product(grad_rows, matrix):
    return lax.dot_general(
        grad_rows, matrix, (((1,), (1,)), ((), ())), preferred_element_type=jnp.float32
    )


def doc_scores(query_rows, key_rows, doc_ids):
    score_scale = HEAD_DIM ** (-0.5)
    scores = (
        jnp.einsum("qhd,khd->hqk", query_rows, key_rows, preferred_element_type=jnp.float32)
        * score_scale
    )
    same_doc = (doc_ids[:, None] == doc_ids[None, :])[None]
    return jnp.where(same_doc, scores, MASK_FILL)


def attend_one(query_rows, key_rows, value_rows, doc_ids):
    scores = doc_scores(query_rows, key_rows, doc_ids)
    row_max = jnp.max(scores, axis=-1, keepdims=True)
    row_total = jnp.sum(jnp.exp(scores - row_max), axis=-1, keepdims=True)
    log_total = row_max + jnp.log(row_total)
    probs_low = jnp.exp(scores - log_total).astype(jnp.bfloat16)
    attended = jnp.einsum("hqk,khd->qhd", probs_low, value_rows, preferred_element_type=jnp.float32)
    return (attended, log_total)


def attend_back(query_rows, key_rows, value_rows, doc_ids, log_total, attended_grad):
    score_scale = HEAD_DIM ** (-0.5)
    probs = jnp.exp(doc_scores(query_rows, key_rows, doc_ids) - log_total)
    probs_low = probs.astype(jnp.bfloat16)
    value_grad = jnp.einsum(
        "hqk,qhd->khd", probs_low, attended_grad, preferred_element_type=jnp.float32
    )
    prob_grad = jnp.einsum(
        "qhd,khd->hqk", attended_grad, value_rows, preferred_element_type=jnp.float32
    )
    row_dot = jnp.sum(probs * prob_grad, axis=-1, keepdims=True)
    score_grad = (probs * (prob_grad - row_dot)).astype(jnp.bfloat16)
    query_grad = (
        jnp.einsum("hqk,khd->qhd", score_grad, key_rows, preferred_element_type=jnp.float32)
        * score_scale
    )
    key_grad = (
        jnp.einsum("hqk,qhd->khd", score_grad, query_rows, preferred_element_type=jnp.float32)
        * score_scale
    )
    return jnp.stack([query_grad, key_grad, value_grad], axis=1).astype(jnp.bfloat16)


def forward_micro(token_rows, doc_ids, weights):
    qkv_weight, proj_weight, up_weight, down_weight, vector = weights
    (
        bias_query,
        bias_value,
        bias_proj,
        gain_first,
        shift_first,
        bias_up,
        bias_down,
        gain_second,
        shift_second,
    ) = split_vector(vector.astype(jnp.float32))
    seq_count, length = doc_ids.shape
    bias_all = jnp.concatenate([bias_query, jnp.zeros_like(bias_query), bias_value])
    packed = (
        jnp.dot(token_rows, qkv_weight, preferred_element_type=jnp.float32) + bias_all
    ).astype(jnp.bfloat16)
    heads_view = packed.reshape(seq_count, length, 3, HEADS, HEAD_DIM)
    attended, log_total = lax.map(
        lambda pieces: attend_one(*pieces),
        (heads_view[:, :, 0], heads_view[:, :, 1], heads_view[:, :, 2], doc_ids),
    )
    attended = attended.reshape(seq_count * length, D).astype(jnp.bfloat16)
    branch = jnp.dot(attended, proj_weight, preferred_element_type=jnp.float32) + bias_proj
    residual = token_rows.astype(jnp.float32) + branch
    normed = layer_norm(residual, gain_first, shift_first)
    normed_low = normed.astype(jnp.bfloat16)
    upward = jnp.dot(normed_low, up_weight, preferred_element_type=jnp.float32) + bias_up
    activated = gelu_exact(upward).astype(jnp.bfloat16)
    downward = jnp.dot(activated, down_weight, preferred_element_type=jnp.float32) + bias_down
    second_in = normed + downward
    output = layer_norm(second_in, gain_second, shift_second)
    saved = (packed, log_total, attended, residual, normed_low, upward, activated, second_in)
    return (output.astype(jnp.bfloat16), saved)


def backward_micro(token_rows, doc_ids, weights, saved, cotangent):
    qkv_weight, proj_weight, up_weight, down_weight, vector = weights
    (
        bias_query,
        bias_value,
        bias_proj,
        gain_first,
        shift_first,
        bias_up,
        bias_down,
        gain_second,
        shift_second,
    ) = split_vector(vector.astype(jnp.float32))
    packed, log_total, attended, residual, normed_low, upward, activated, second_in = saved
    seq_count, length = doc_ids.shape
    unused_second, second_pull = jax.vjp(layer_norm, second_in, gain_second, shift_second)
    second_grad, gain_second_grad, shift_second_grad = second_pull(cotangent.astype(jnp.float32))
    down_rows_grad = second_grad.astype(jnp.bfloat16)
    down_weight_grad = weight_grad(activated, down_rows_grad)
    bias_down_grad = jnp.sum(down_rows_grad.astype(jnp.float32), axis=0)
    activated_grad = back_product(down_rows_grad, down_weight)
    unused_gelu, gelu_pull = jax.vjp(gelu_exact, upward)
    upward_grad = gelu_pull(activated_grad)[0].astype(jnp.bfloat16)
    up_weight_grad = weight_grad(normed_low, upward_grad)
    bias_up_grad = jnp.sum(upward_grad.astype(jnp.float32), axis=0)
    normed_grad = back_product(upward_grad, up_weight) + second_grad
    unused_first, first_pull = jax.vjp(layer_norm, residual, gain_first, shift_first)
    residual_grad, gain_first_grad, shift_first_grad = first_pull(normed_grad)
    branch_grad = residual_grad.astype(jnp.bfloat16)
    proj_weight_grad = weight_grad(attended, branch_grad)
    bias_proj_grad = jnp.sum(branch_grad.astype(jnp.float32), axis=0)
    attended_grad = back_product(branch_grad, proj_weight).astype(jnp.bfloat16)
    heads_view = packed.reshape(seq_count, length, 3, HEADS, HEAD_DIM)
    packed_grad = lax.map(
        lambda pieces: attend_back(*pieces),
        (
            heads_view[:, :, 0],
            heads_view[:, :, 1],
            heads_view[:, :, 2],
            doc_ids,
            log_total,
            attended_grad.reshape(seq_count, length, HEADS, HEAD_DIM),
        ),
    )
    packed_grad = packed_grad.reshape(seq_count * length, 3 * D)
    qkv_weight_grad = weight_grad(token_rows, packed_grad)
    packed_sums = jnp.sum(packed_grad.astype(jnp.float32), axis=0)
    input_part = (back_product(packed_grad, qkv_weight) + residual_grad).astype(jnp.bfloat16)
    vector_grad = jnp.concatenate(
        [
            packed_sums[0:D],
            packed_sums[2 * D : 3 * D],
            bias_proj_grad,
            gain_first_grad,
            shift_first_grad,
            bias_up_grad,
            bias_down_grad,
            gain_second_grad,
            shift_second_grad,
        ]
    )
    return (
        input_part,
        (
            qkv_weight_grad.reshape(-1),
            proj_weight_grad.reshape(-1),
            up_weight_grad.reshape(-1),
            down_weight_grad.reshape(-1),
            vector_grad,
        ),
    )


def adam_update(master, moment_one, moment_two, grad, rate):
    one_new = BETA_FIRST * moment_one + (1.0 - BETA_FIRST) * grad
    two_new = BETA_SECOND * moment_two + (1.0 - BETA_SECOND) * grad * grad
    one_hat = one_new / (1.0 - BETA_FIRST**STEP)
    two_hat = two_new / (1.0 - BETA_SECOND**STEP)
    master_new = master - rate * (one_hat / (jnp.sqrt(two_hat) + ADAM_EPS) + WEIGHT_DECAY * master)
    return (grad, one_new, two_new, master_new, master_new.astype(jnp.bfloat16))


def shaped(flat_parts):
    matrix_shapes = ((D, 3 * D), (D, D), (D, FF), (FF, D), (-1,))
    return tuple(
        (
            flat_piece.reshape(matrix_shape)
            for flat_piece, matrix_shape in zip(flat_parts, matrix_shapes)
        )
    )


def by_owner(flat_parts, devices):
    return tuple((flat_piece.reshape(devices, -1) for flat_piece in flat_parts))


def body(
    tokens,
    segment_ids,
    out_grad,
    qkv_master,
    qkv_first,
    qkv_second,
    proj_master,
    proj_first,
    proj_second,
    up_master,
    up_first,
    up_second,
    down_master,
    down_first,
    down_second,
    vector_master,
    vector_first,
    vector_second,
):
    masters = (qkv_master, proj_master, up_master, down_master, vector_master)
    lowered = tuple((master.astype(jnp.bfloat16) for master in masters))
    seq_dev, length = segment_ids.shape
    per_micro = seq_dev // MB
    rows_micro = per_micro * length
    devices = lax.axis_size("dp")
    accumulated = tuple(
        (jnp.zeros((master.shape[0] * devices,), jnp.float32) for master in masters)
    )
    owned = tuple((jnp.zeros_like(master) for master in masters))
    layer_parts = []
    input_parts = []
    for micro_index in range(MB):
        weights = shaped(
            (
                lax.all_gather(lowered[0], "dp", axis=0, tiled=True),
                lax.all_gather(lowered[1], "dp", axis=0, tiled=True),
                lax.all_gather(lowered[2], "dp", axis=0, tiled=True),
                lax.all_gather(lowered[3], "dp", axis=0, tiled=True),
                lax.all_gather(lowered[4], "dp", axis=0, tiled=True),
            )
        )
        token_rows = tokens[micro_index * rows_micro : (micro_index + 1) * rows_micro]
        doc_ids = segment_ids[micro_index * per_micro : (micro_index + 1) * per_micro]
        cotangent = out_grad[micro_index * rows_micro : (micro_index + 1) * rows_micro]
        output, saved = forward_micro(token_rows, doc_ids, weights)
        layer_parts.append(output)
        gathered_back = (
            lax.all_gather(lowered[0], "dp", axis=0, tiled=True),
            lax.all_gather(lowered[1], "dp", axis=0, tiled=True),
            lax.all_gather(lowered[2], "dp", axis=0, tiled=True),
            lax.all_gather(lowered[3], "dp", axis=0, tiled=True),
            lax.all_gather(lowered[4], "dp", axis=0, tiled=True),
        )
        back_weights = shaped(gathered_back)
        input_part, weight_grads = backward_micro(
            token_rows, doc_ids, back_weights, saved, cotangent
        )
        input_parts.append(input_part)
        accumulated = tuple(
            (earlier + latest for earlier, latest in zip(accumulated, weight_grads))
        )
    rows_total = by_owner(accumulated, devices)
    shares = (
        lax.psum_scatter(rows_total[0], "dp", scatter_dimension=0, tiled=True),
        lax.psum_scatter(rows_total[1], "dp", scatter_dimension=0, tiled=True),
        lax.psum_scatter(rows_total[2], "dp", scatter_dimension=0, tiled=True),
        lax.psum_scatter(rows_total[3], "dp", scatter_dimension=0, tiled=True),
        lax.psum_scatter(rows_total[4], "dp", scatter_dimension=0, tiled=True),
    )
    owned = tuple((share.reshape(-1) for share in shares))
    layer_out = jnp.concatenate(layer_parts, axis=0)
    input_grad = jnp.concatenate(input_parts, axis=0)
    qkv_out = adam_update(qkv_master, qkv_first, qkv_second, owned[0], RATES[0])
    proj_out = adam_update(proj_master, proj_first, proj_second, owned[1], RATES[1])
    up_out = adam_update(up_master, up_first, up_second, owned[2], RATES[2])
    down_out = adam_update(down_master, down_first, down_second, owned[3], RATES[3])
    vector_out = adam_update(vector_master, vector_first, vector_second, owned[4], RATES[4])
    return (
        layer_out,
        input_grad,
        qkv_out[0],
        qkv_out[1],
        qkv_out[2],
        qkv_out[3],
        qkv_out[4],
        proj_out[0],
        proj_out[1],
        proj_out[2],
        proj_out[3],
        proj_out[4],
        up_out[0],
        up_out[1],
        up_out[2],
        up_out[3],
        up_out[4],
        down_out[0],
        down_out[1],
        down_out[2],
        down_out[3],
        down_out[4],
        vector_out[0],
        vector_out[1],
        vector_out[2],
        vector_out[3],
        vector_out[4],
    )


def solution(mesh):
    in_specs = (
        P("dp", None),
        P("dp", None),
        P("dp", None),
        P("dp"),
        P("dp"),
        P("dp"),
        P("dp"),
        P("dp"),
        P("dp"),
        P("dp"),
        P("dp"),
        P("dp"),
        P("dp"),
        P("dp"),
        P("dp"),
        P("dp"),
        P("dp"),
        P("dp"),
    )
    out_specs = (
        P("dp", None),
        P("dp", None),
        P("dp"),
        P("dp"),
        P("dp"),
        P("dp"),
        P("dp"),
        P("dp"),
        P("dp"),
        P("dp"),
        P("dp"),
        P("dp"),
        P("dp"),
        P("dp"),
        P("dp"),
        P("dp"),
        P("dp"),
        P("dp"),
        P("dp"),
        P("dp"),
        P("dp"),
        P("dp"),
        P("dp"),
        P("dp"),
        P("dp"),
        P("dp"),
        P("dp"),
    )
    return jax.shard_map(body, mesh=mesh, in_specs=in_specs, out_specs=out_specs, check_vma=False)
```

profile of v0, /device:TPU:0, one launch (start us, length us, event | category | flops | bytes accessed | tf_op | source)
XLA Modules:
  0.0 1352.3 jit_solution(124589989344429256)
XLA Ops:
  10.6 1.8 convert_element_type.213
  12.5 1.8 convert_element_type.215
  15.0 43.5 %all-gather = bf16[32,1,384]{2,1,0:T(2,128)(2,1)S(1)} all-gather(bf16[1,1,384]{2,1,0:T(2,128)(2,1)S(1)} %reshape.400), channel_id=1, replica_groups=mesh['dp'=32] {'dp'}, dimensions={0}, use_global_device_ids=true | all-gather | bytes 25344 | tf_op jit(solution)/shard_map/all_gather | solution.py:274
  61.1 9.3 all-gather.8.cloned.1.call-done
  70.4 4.2 reshape.391
  74.6 67.3 %all-gather.6.cloned.1.call-done = bf16[3145728]{0:T(1024)(128)(2,1)} async-done(((bf16[98304]{0:T(1024)(128)(2,1)}), bf16[3145728]{0:T(1024)(128)(2,1)}) %all-gather.6.cloned.1.call-update) | async-done | bytes 6291472 | tf_op jit(solution)/shard_map/all_gather | solution.py:270
  141.9 10.4 reshape.389
  152.3 7.8 add_convert_fusion.2
  160.1 4.9 add_convert_fusion.3
  164.9 3.2 copy.78
  168.1 8.4 fusion.1
  176.6 9.2 exponential_reduce_fusion
  185.9 8.8 convolution_convert_fusion
  196.5 4.7 copy.76
  201.2 10.0 fusion
  211.3 9.3 exponential_reduce_fusion.1
  220.7 10.4 convolution_convert_fusion.1
  234.2 13.3 reshape.392
  247.6 8.0 fusion.57
  255.5 3.3 copy-done.95
  258.8 48.7 %multiply_convert_fusion.3 = (bf16[512,4096]{1,0:T(8,128)(2,1)}, f32[512,4096]{1,0:T(8,128)}, bf16[512,4096]{1,0:T(8,128)(2,1)}, f32[512,4096]{1,0:T(8,128)}, f32[512,4096]{1,0:T(8,128)}) fusion(f32[4096]{0:T(1024)S(1)} %slice.143, f32[512,4096]{1,0:T(8,128)S(1)} %fusion.57, bf16[1024,4096]{1,0:T(8,128)(2,1)S(1)} %copy-done.13, ...), kind=kOutput, calls=%fused_computation.36 | convolution fusion | flops 4574412800 | bytes 52457472 | tf_op jit(solution)/shard_map/dot_general | solution.py:130
  307.5 13.3 reshape.393
  320.9 8.8 fusion.85
  330.1 4.8 fusion.86
  335.3 2.4 convert_reduce_fusion.4
  337.7 3.1 fusion.76
  341.9 6.8 fusion.87
  349.5 27.4 %convert_reduce_fusion.1 = (f32[4096]{0:T(1024)}, bf16[512,4096]{1,0:T(8,128)(2,1)}, f32[4096]{0:T(1024)}, bf16[512,4096]{1,0:T(8,128)(2,1)}) fusion(f32[512,4096]{1,0:T(8,128)} %get-tuple-element.184, f32[512,4096]{1,0:T(8,128)} %get-tuple-element.223, f32[4096]{0:T(1024)S(1)} %slice.143, f32[512,4096]{1,0:T(8,128)} %fusion.87, ...), kind=kOutput, calls=%fused_computation.20 | convolution fusion | flops 4366262272 | bytes 59817984 | tf_op jit(solution)/shard_map/dot_general | solution.py:54
  376.9 9.8 add_add_fusion.8
  386.8 10.7 multiply_reduce_fusion.3
  397.6 2.3 fusion.73
  403.1 2.3 convolution_convert_fusion.2
  407.0 9.6 convolution_bitcast_fusion
  416.6 12.0 multiply_reduce_fusion
  428.6 12.2 multiply_convert_fusion
  440.8 3.6 multiply_bitcast_fusion
  444.4 2.5 multiply_bitcast_fusion.1
  448.7 2.3 convolution_convert_fusion.3
  452.5 8.1 convolution_bitcast_fusion.1
  460.7 12.2 multiply_reduce_fusion.1
  472.9 12.2 multiply_convert_fusion.1
  485.1 2.6 multiply_bitcast_fusion.2
  489.3 3.3 fusion.88
  493.5 8.5 fusion.59
  502.0 8.1 fusion.89
  512.6 3.4 fusion.32
  518.4 6.4 add_bitcast_fusion
  524.8 12.6 copy.88
  537.4 10.0 add.329
  547.3 5.7 convolution_add_fusion.2
  553.0 5.0 add.336
  558.0 12.9 convolution_add_fusion
  570.8 12.2 add.343
  583.0 13.0 convolution_add_fusion.1
  596.0 12.1 add.349
  609.1 41.1 %all-reduce.4 = f32[32,384]{1,0:T(8,128)S(1)} all-reduce(f32[32,384]{1,0:T(8,128)S(1)} %add.355), channel_id=6, replica_groups=mesh['dp'=32] {'dp'}, use_global_device_ids=true, to_apply=%region_42.43.clone | all-reduce | flops 12288 | bytes 98304
  650.4 7.3 add_convert_fusion.4
  657.8 7.0 add_convert_fusion.5
  664.8 2.5 pad_maximum_fusion
  668.0 661.7 %all-reduce.8.cloned.1.call-done = (f32[32,98304]{1,0:T(8,128)}, f32[32,32768]{1,0:T(8,128)}, f32[32,131072]{1,0:T(8,128)}, f32[32,131072]{1,0:T(8,128)}) async-done(((f32[32,98304]{1,0:T(8,128)}, f32[32,32768]{1,0:T(8,128)}, f32[32,131072]{1,0:T(8,128)}, f32[32,131072]{1,0:T(8,128)}), (f32[32,98304]{1,0:T(8,128)}, f32[32,32768]{1,0:T(8,128)}, f32[32,131072]{1,0:T(8,128)}, ...) | async-done | bytes 50331664
  1329.7 2.2 constant_dynamic-slice_fusion.3
  1333.3 4.2 constant_dynamic-slice_fusion
  1337.6 2.8 fusion.71
  1340.4 1.8 fusion.69
  (278 shorter events, 35.6 us)
Async XLA Ops:
  7.2 63.2 %all-gather.8.cloned.1.call-start = ((), (), s32[]{:S(2)}) async-start(), calls=%async_computation.1 | async-start | bytes 2162688 | tf_op jit(solution)/shard_map/all_gather | solution.py:271
  8.8 133.1 %all-gather.6.cloned.1.call-start = ((), (), s32[]{:S(2)}) async-start(), calls=%async_computation | async-start | bytes 6488064 | tf_op jit(solution)/shard_map/all_gather | solution.py:270
  10.6 223.6 %all-gather.10.cloned.1.call-start = ((), (), s32[]{:S(2)}) async-start(), calls=%async_computation.2 | async-start | bytes 8650752 | tf_op jit(solution)/shard_map/all_gather | solution.py:272
  12.4 295.1 %all-gather.12.cloned.1.call-start = ((), (), s32[]{:S(2)}) async-start(), calls=%async_computation.3 | async-start | bytes 8650752 | tf_op jit(solution)/shard_map/all_gather | solution.py:273
  14.3 1315.4 %all-reduce.8.cloned.1.call-start = ((), (), s32[]{:S(2)}) async-start(), calls=%async_computation.4 | async-start | bytes 100663296
  61.1 159.6 %copy-start.24 = (pred[512,512]{0,1:T(8,128)(4,1)}, pred[512,512]{0,1:T(8,128)(4,1)S(1)}, u32[]{:S(2)}) copy-start(pred[512,512]{0,1:T(8,128)(4,1)S(1)} %broadcast_compare_fusion.1) | copy-start | bytes 786436
  74.6 77.7 %copy-start.28 = (bf16[1024,1024]{1,0:T(8,128)(2,1)S(1)}, bf16[1024,1024]{1,0:T(8,128)(2,1)}, u32[]{:S(2)}) copy-start(bf16[1024,1024]{1,0:T(8,128)(2,1)} %param.18) | copy-start | bytes 6291460
  152.3 7.8 copy-start.27
  168.1 17.7 %copy-start.1 = (bf16[512,3072]{0,1:T(8,128)(2,1)}, bf16[512,3072]{0,1:T(8,128)(2,1)S(1)}, u32[]{:S(2)}) copy-start(bf16[512,3072]{0,1:T(8,128)(2,1)S(1)} %copy.78) | copy-start | bytes 9437188
  185.8 8.9 copy-start.61
  185.9 8.9 copy-start.5
  185.9 8.9 copy-start.29
  196.5 14.8 %copy-start.64 = (f32[512]{0:T(512)}, f32[512]{0:T(512)S(1)}, u32[]{:S(2)}) copy-start(f32[512]{0:T(512)S(1)} %multiply_reduce_fusion.7) | copy-start | bytes 6148
  220.6 10.4 copy-start.59
  220.6 10.4 copy-start.6
  220.7 10.4 copy-start.30
  231.1 16.5 %copy-start.51 = (bf16[16,64,512]{2,1,0:T(8,128)(2,1)}, bf16[16,64,512]{2,1,0:T(8,128)(2,1)S(1)}, u32[]{:S(2)}) copy-start(bf16[16,64,512]{2,1,0:T(8,128)(2,1)S(1)} %convolution_convert_fusion.1) | copy-start | bytes 3145732
  234.2 13.4 copy-start.66
  247.6 11.3 copy-start.10
  247.6 11.3 copy-start.13
  307.5 13.3 copy-start.85
  320.9 9.2 copy-start.11
  320.9 9.2 copy-start.14
  320.9 9.2 copy-start.92
  330.1 5.2 copy-start.15
  330.1 5.2 copy-start.63
  340.8 7.8 copy-start.21
  340.8 7.8 copy-start.19
  341.9 6.8 copy-start.32
  349.5 27.4 %copy-start.47 = (bf16[512,1024]{1,0:T(8,128)(2,1)}, bf16[512,1024]{1,0:T(8,128)(2,1)S(1)}, u32[]{:S(2)}) copy-start(bf16[512,1024]{1,0:T(8,128)(2,1)S(1)} %get-tuple-element.152) | copy-start | bytes 3145732
  376.9 9.9 copy-start.20
  386.7 10.8 copy-start.67
  386.8 10.8 copy-start.65
  397.5 5.6 copy-start.7
  399.9 5.5 copy-start.81
  402.1 4.8 copy-start.26
  402.1 4.8 copy-start.62
  407.0 9.6 copy-start.2
  447.7 4.8 copy-start.25
  447.7 4.8 copy-start.60
  452.5 8.2 copy-start
  493.5 8.5 copy-start.48
  493.5 8.5 copy-start.93
  537.4 10.0 copy-start.23
  570.8 12.2 copy-start.33
  608.3 42.0 %copy-start.4 = (bf16[512,3,16,64]{0,3,2,1:T(8,128)(2,1)S(1)}, bf16[512,3,16,64]{0,3,2,1:T(8,128)(2,1)}, u32[]{:S(2)}) copy-start(bf16[512,3,16,64]{0,3,2,1:T(8,128)(2,1)} %copy-done.3) | copy-start | bytes 9437188
  608.3 42.0 %copy-start.82 = (f32[512]{0:T(512)S(1)}, f32[512]{0:T(512)}, u32[]{:S(2)}) copy-start(f32[512]{0:T(512)} %copy-done.81) | copy-start | bytes 6148
  650.3 17.0 %copy-start.80 = (f32[384]{0:T(512)}, f32[384]{0:T(512)S(1)}, u32[]{:S(2)}) copy-start(f32[384]{0:T(512)S(1)} %dynamic-slice_reduce_fusion) | copy-start | bytes 4612
  650.3 7.4 copy-start.17
  650.3 7.4 copy-start.40
  650.3 7.4 copy-start.84
  657.7 7.0 copy-start.37
  657.8 7.0 copy-start.38
  664.8 672.8 %copy-start.45 = (f32[98304]{0:T(1024)S(1)}, f32[98304]{0:T(1024)}, u32[]{:S(2)}) copy-start(f32[98304]{0:T(1024)} %param.21) | copy-start | bytes 1179652
  664.8 677.4 %copy-start.43 = (f32[131072]{0:T(1024)S(1)}, f32[131072]{0:T(1024)}, u32[]{:S(2)}) copy-start(f32[131072]{0:T(1024)} %param.27) | copy-start | bytes 1572868
  664.8 677.4 %copy-start.54 = (f32[131072]{0:T(1024)S(1)}, f32[131072]{0:T(1024)}, u32[]{:S(2)}) copy-start(f32[131072]{0:T(1024)} %param.29) | copy-start | bytes 1572868
  664.8 677.4 %copy-start.55 = (f32[131072]{0:T(1024)S(1)}, f32[131072]{0:T(1024)}, u32[]{:S(2)}) copy-start(f32[131072]{0:T(1024)} %param.28) | copy-start | bytes 1572868
  667.3 676.4 %copy-start.44 = (f32[131072]{0:T(1024)S(1)}, f32[131072]{0:T(1024)}, u32[]{:S(2)}) copy-start(f32[131072]{0:T(1024)} %param.30) | copy-start | bytes 1572868
  667.3 676.4 %copy-start.56 = (f32[131072]{0:T(1024)S(1)}, f32[131072]{0:T(1024)}, u32[]{:S(2)}) copy-start(f32[131072]{0:T(1024)} %param.32) | copy-start | bytes 1572868
  667.3 676.4 %copy-start.57 = (f32[131072]{0:T(1024)S(1)}, f32[131072]{0:T(1024)}, u32[]{:S(2)}) copy-start(f32[131072]{0:T(1024)} %param.31) | copy-start | bytes 1572868
  1331.8 13.5 copy-start.46
  1333.3 12.0 copy-start.58
  1337.6 7.7 copy-start.41
  1337.6 7.7 copy-start.42
  (37 other events, 68.4 us)
Sparse Core Ops, SparseCore 0:
  11.4 58.9 all-gather.7
  73.8 67.9 all-gather.5
  145.3 75.5 all-gather.9
  224.2 75.6 all-gather.11
  608.4 721.1 all-reduce.7
where the time goes:
time: 1360 us; the launch traced here: 1350 us
  waiting for transfers between devices  738 us (54%)
  matrix products  310 us (23%)
  local copies, waits for them, and re-layouts  126 us (9%)
  blocking collectives  84.6 us (6%)
  other arithmetic  76.7 us (6%)
  between operations  15.5 us (1%)
    unnamed x6, waiting for transfers between devices  662 us
    dot_general x8, matrix products, back_product(): lax.dot_general(grad_rows, matrix, (((1,), (1,)), ((), ())), preferred_el...  73.6 us
    all_gather x1, waiting for transfers between devices, body(): lax.all_gather(lowered[0], 'dp', axis=0, tiled=True)  67.3 us
    dot_general x8, matrix products, weight_grad(): lax.dot_general(left_rows, right_rows, (((0,), (0,)), ((), ())), preferre...  61.3 us
    dot_general x2, matrix products, forward_micro(): jnp.dot(normed_low, up_weight, preferred_element_type=jnp.float32) + bias_up  56.6 us
    add x6, local copies, waits for them, and re-layouts, body(): earlier + latest  51.8 us
    all_gather x1, blocking collectives, body(): lax.all_gather(lowered[4], 'dp', axis=0, tiled=True)  43.5 us
    reshape x4, local copies, waits for them, and re-layouts, shaped(): flat_piece.reshape(matrix_shape)  41.2 us
  transfers between devices with their start and end apart: 5, of which 3 were waited for; matrix products, arithmetic and copies ran while one was open for 14% of the time, Pallas kernels for 0%

commit v1 on v0

v1 whole, which is shorter than its diff:
```python
import functools

import jax
import jax.numpy as jnp
from jax import lax
from jax.experimental import pallas as pl
from jax.experimental.pallas import tpu as pltpu
from jax.sharding import PartitionSpec as P

D = 1024
HEADS = 16
HEAD_DIM = 64
FF = 4096
STEP = 3
LANES = 128
PAIRS = HEADS * HEAD_DIM // LANES

NORM_EPS = 1e-05
BETA_FIRST = 0.5
BETA_SECOND = 0.5
ADAM_EPS = 1e-08
WEIGHT_DECAY = 0.01
MASK_FILL = -1000000000.0
RATES = (0.01, 0.03, 0.01, 0.005, 0.05)
SCALE = HEAD_DIM ** (-0.5)
HALF_ROOT = 0.7071067811865476
PDF_TOP = 0.3989422804014327

F32 = jnp.float32
BF16 = jnp.bfloat16
MESH = pl.DeviceIdType.MESH


def dot_over(left, right, left_dim, right_dim):
    return lax.dot_general(
        left, right, (((left_dim,), (right_dim,)), ((), ())), preferred_element_type=F32
    )


def depth_of(mesh):
    devices = list(mesh.devices.flat)
    if len(devices) % 8:
        return 0
    try:
        spots = [(*d.coords, d.core_on_chip) for d in devices]
    except AttributeError:
        return 0
    low = [min(s[i] for s in spots) for i in range(4)]
    depth = len(devices) // 8
    for index, (x, y, z, core) in enumerate(spots):
        spot = (((z - low[2]) * 2 + y - low[1]) * 2 + x - low[0]) * 2 + core - low[3]
        if spot != index:
            return 0
    return depth


class Place:
    def __init__(self, depth):
        me = lax.axis_index("dp")
        self.depth = depth
        self.core = me % 2
        self.x = (me // 2) % 2
        self.y = (me // 4) % 2
        self.z = me // 8

    def index(self, z, y, x, core):
        return ((z * 2 + y) * 2 + x) * 2 + core

    def ahead(self, k):
        return (self.z + k) % self.depth

    def back(self, k):
        return (self.z + self.depth - k) % self.depth

    def twin(self):
        return self.index(self.z, self.y, self.x, 1 - self.core)

    def x_mate(self):
        return self.index(self.z, self.y, 1 - self.x, self.core)

    def y_mate(self):
        return self.index(self.z, 1 - self.y, self.x, self.core)

    def z_mate(self, k):
        return self.index(self.ahead(k), self.y, self.x, self.core)

    def greet(self):
        barrier = pltpu.get_barrier_semaphore()
        mates = [self.twin(), self.x_mate(), self.y_mate()]
        mates += [self.z_mate(k) for k in range(1, self.depth)]
        for mate in mates:
            pl.semaphore_signal(barrier, inc=1, device_id=(mate,), device_id_type=MESH)
        pl.semaphore_wait(barrier, len(mates))


def send(source, target, send_sem, recv_sem, device):
    return pltpu.make_async_remote_copy(
        src_ref=source,
        dst_ref=target,
        send_sem=send_sem,
        recv_sem=recv_sem,
        device_id=(device,),
        device_id_type=MESH,
    )


class Gather:
    BY_Z, BY_X, BY_Y, UPPER, LOWER, OWN, FROM_X, FROM_Y, CROSS = range(9)

    def __init__(self, place, blocks, full, send_sems, recv_sems, local_sems):
        self.place = place
        self.blocks = blocks
        self.full = full
        self.sems = (send_sems, recv_sems)
        self.local_sems = local_sems
        self.depth = place.depth

    def home(self, w):
        p = self.place
        return self.full[w].at[p.z, p.y, p.x, p.core]

    def copy(self, w, k, kind):
        p, full = self.place, self.full[w]
        half = self.blocks[w].shape[0] // 2
        sems = [sem.at[w, k, kind] for sem in self.sems]
        zz = p.back(k)
        if kind == self.BY_Z:
            return send(self.blocks[w], self.home(w), *sems, p.z_mate(k))
        if kind in (self.BY_X, self.BY_Y, self.OWN):
            block = full.at[zz, p.y, p.x, p.core]
            source = self.blocks[w] if k == 0 else block
            mate = {self.BY_X: p.x_mate, self.BY_Y: p.y_mate, self.OWN: p.twin}[kind]()
            return send(source, block, *sems, mate)
        if kind == self.UPPER:
            block = full.at[zz, p.y, 1 - p.x, p.core, pl.ds(0, half)]
            return send(block, block, *sems, p.y_mate())
        if kind == self.LOWER:
            block = full.at[zz, 1 - p.y, p.x, p.core, pl.ds(half, half)]
            return send(block, block, *sems, p.x_mate())
        if kind == self.FROM_X:
            block = full.at[zz, p.y, 1 - p.x, p.core]
        elif kind == self.FROM_Y:
            block = full.at[zz, 1 - p.y, p.x, p.core]
        else:
            block = full.at[zz, 1 - p.y, 1 - p.x, p.core]
        return send(block, block, *sems, p.twin())

    def local(self, w):
        return pltpu.make_async_copy(self.blocks[w], self.home(w), self.local_sems.at[w])

    def start(self, w):
        for k in range(1, self.depth):
            self.copy(w, k, self.BY_Z).start()
        self.local(w).start()

    def spread(self, w, k):
        if k:
            self.copy(w, k, self.BY_Z).wait_recv()
        for kind in (self.BY_X, self.BY_Y, self.OWN):
            self.copy(w, k, kind).start()

    def relay(self, w, k):
        self.copy(w, k, self.BY_X).wait_recv()
        self.copy(w, k, self.UPPER).start()
        self.copy(w, k, self.FROM_X).start()
        self.copy(w, k, self.BY_Y).wait_recv()
        self.copy(w, k, self.LOWER).start()
        self.copy(w, k, self.FROM_Y).start()

    def hand_over(self, w, k):
        self.copy(w, k, self.UPPER).wait_recv()
        self.copy(w, k, self.LOWER).wait_recv()
        self.copy(w, k, self.CROSS).start()

    def finish(self, w):
        self.local(w).wait()
        for k in range(self.depth):
            for kind in (self.OWN, self.FROM_X, self.FROM_Y, self.CROSS):
                self.copy(w, k, kind).wait_recv()
            for kind in range(9):
                if kind != self.BY_Z or k:
                    self.copy(w, k, kind).wait_send()

    def step(self, units, t):
        lag = self.depth
        if t < len(units):
            self.spread(*units[t])
        if 0 <= t - lag < len(units):
            self.relay(*units[t - lag])
        if 0 <= t - 2 * lag < len(units):
            self.hand_over(*units[t - 2 * lag])

    def run(self):
        count = len(self.blocks)
        for w in range(count):
            self.start(w)
        units = [(w, k) for w in range(count) for k in range(self.depth)]
        for t in range(len(units) + 2 * self.depth):
            self.step(units, t)
        for w in range(count):
            self.finish(w)


def gather_kernel(depth, count, *refs):
    blocks, full, sems = refs[:count], refs[count : 2 * count], refs[2 * count :]
    place = Place(depth)
    place.greet()
    Gather(place, blocks, full, *sems).run()


def gather_sems(count, depth):
    return [
        pltpu.SemaphoreType.DMA((count, depth, 9)),
        pltpu.SemaphoreType.DMA((count, depth, 9)),
        pltpu.SemaphoreType.DMA((count,)),
    ]


def gather(blocks, depth, collective_id):
    count = len(blocks)
    return pl.pallas_call(
        functools.partial(gather_kernel, depth, count),
        in_specs=[pl.BlockSpec(memory_space=pltpu.VMEM)] * count,
        out_specs=[pl.BlockSpec(memory_space=pl.ANY)] * count,
        out_shape=[jax.ShapeDtypeStruct((depth, 2, 2, 2) + b.shape, b.dtype) for b in blocks],
        scratch_shapes=gather_sems(count, depth),
        compiler_params=pltpu.CompilerParams(
            collective_id=collective_id, has_side_effects=True
        ),
        name="gather",
    )(*blocks)


class Scatter:
    TWIN, UPPER_Y, LOWER_X, UPPER_X, LOWER_Y, BY_Z = range(6)

    def __init__(self, place, grads, out, bufs, send_sems, recv_sems, local_sems):
        self.place = place
        self.grads = grads
        self.out = out
        self.bufs = bufs
        self.sems = (send_sems, recv_sems)
        self.local_sems = local_sems
        self.depth = place.depth
        self.order = list(range(1, self.depth)) + [0]

    def load(self, w, k):
        p = self.place
        return pltpu.make_async_copy(
            self.grads[w].at[p.ahead(k), :, :, p.core],
            self.bufs[w][0].at[k],
            self.local_sems.at[w, k],
        )

    def copy(self, w, k, kind):
        p = self.place
        sums, twin, upper_y, lower_x, upper_x, lower_y, by_z = self.bufs[w]
        half = sums.shape[3] // 2
        sems = [sem.at[w, k, kind] for sem in self.sems]
        top, bottom = pl.ds(0, half), pl.ds(half, half)
        if kind == self.TWIN:
            source = self.grads[w].at[p.ahead(k), :, :, 1 - p.core]
            return send(source, twin.at[k], *sems, p.twin())
        if kind == self.UPPER_Y:
            return send(sums.at[k, 1 - p.y, :, top], upper_y.at[k], *sems, p.y_mate())
        if kind == self.LOWER_X:
            return send(sums.at[k, :, 1 - p.x, bottom], lower_x.at[k], *sems, p.x_mate())
        if kind == self.UPPER_X:
            return send(sums.at[k, p.y, 1 - p.x, top], upper_x.at[k], *sems, p.x_mate())
        if kind == self.LOWER_Y:
            return send(sums.at[k, 1 - p.y, p.x, bottom], lower_y.at[k], *sems, p.y_mate())
        return send(sums.at[k, p.y, p.x], by_z.at[k], *sems, p.z_mate(k))

    @staticmethod
    def add(target, extra):
        total = target[...].astype(F32) + extra[...].astype(F32)
        target[...] = total.astype(target.dtype)

    def start(self, w):
        for k in self.order:
            self.copy(w, k, self.TWIN).start()
            self.load(w, k).start()

    def first(self, w, k):
        sums, twin = self.bufs[w][:2]
        self.load(w, k).wait()
        self.copy(w, k, self.TWIN).wait_recv()

        def body(i, carry):
            self.add(sums.at[k, i // 2, i % 2], twin.at[k, i // 2, i % 2])
            return carry

        lax.fori_loop(0, 4, body, 0)
        self.copy(w, k, self.UPPER_Y).start()
        self.copy(w, k, self.LOWER_X).start()

    def second(self, w, k):
        p = self.place
        sums, _, upper_y, lower_x = self.bufs[w][:4]
        half = sums.shape[3] // 2
        self.copy(w, k, self.UPPER_Y).wait_recv()
        self.copy(w, k, self.LOWER_X).wait_recv()

        def body(i, carry):
            self.add(sums.at[k, p.y, i, pl.ds(0, half)], upper_y.at[k, i])
            self.add(sums.at[k, i, p.x, pl.ds(half, half)], lower_x.at[k, i])
            return carry

        lax.fori_loop(0, 2, body, 0)
        self.copy(w, k, self.UPPER_X).start()
        self.copy(w, k, self.LOWER_Y).start()

    def third(self, w, k):
        p = self.place
        sums, _, _, _, upper_x, lower_y, _ = self.bufs[w]
        half = sums.shape[3] // 2
        self.copy(w, k, self.UPPER_X).wait_recv()
        self.copy(w, k, self.LOWER_Y).wait_recv()
        self.add(sums.at[k, p.y, p.x, pl.ds(0, half)], upper_x.at[k])
        self.add(sums.at[k, p.y, p.x, pl.ds(half, half)], lower_y.at[k])
        if k:
            self.copy(w, k, self.BY_Z).start()

    def finish(self, w):
        p = self.place
        sums, by_z = self.bufs[w][0], self.bufs[w][6]
        for k in range(1, self.depth):
            self.copy(w, k, self.BY_Z).wait_recv()
        total = sums[0, p.y, p.x].astype(F32)
        for k in range(1, self.depth):
            total = total + by_z[k].astype(F32)
        self.out[w][...] = total
        for k in range(self.depth):
            for kind in range(6):
                if kind != self.BY_Z or k:
                    self.copy(w, k, kind).wait_send()

    def step(self, units, t):
        lag = self.depth
        if t < len(units):
            self.first(*units[t])
        if 0 <= t - lag < len(units):
            self.second(*units[t - lag])
        if 0 <= t - 2 * lag < len(units):
            self.third(*units[t - 2 * lag])

    def run(self):
        count = len(self.grads)
        for w in range(count):
            self.start(w)
        units = [(w, k) for w in range(count) for k in self.order]
        for t in range(len(units) + 2 * self.depth):
            self.step(units, t)
        for w in range(count):
            self.finish(w)


def scatter_scratch(grads, depth):
    scratch = []
    for grad in grads:
        rows, columns = grad.shape[-2:]
        half = rows // 2
        shapes = [(depth, 2, 2, rows, columns)] * 2
        shapes += [(depth, 2, half, columns)] * 2 + [(depth, half, columns)] * 2
        shapes += [(depth, rows, columns)]
        scratch += [pltpu.VMEM(shape, grad.dtype) for shape in shapes]
    count = len(grads)
    scratch += [pltpu.SemaphoreType.DMA((count, depth, 6))] * 2
    return scratch + [pltpu.SemaphoreType.DMA((count, depth))]


def scatter_kernel(depth, count, *refs):
    grads, out, rest = refs[:count], refs[count : 2 * count], refs[2 * count :]
    bufs = [rest[7 * w : 7 * w + 7] for w in range(count)]
    place = Place(depth)
    place.greet()
    Scatter(place, grads, out, bufs, *rest[7 * count :]).run()


def scatter(grads, depth, collective_id):
    count = len(grads)
    return pl.pallas_call(
        functools.partial(scatter_kernel, depth, count),
        in_specs=[pl.BlockSpec(memory_space=pl.ANY)] * count,
        out_specs=[pl.BlockSpec(memory_space=pltpu.VMEM)] * count,
        out_shape=[jax.ShapeDtypeStruct(g.shape[-2:], F32) for g in grads],
        scratch_shapes=scatter_scratch(grads, depth),
        compiler_params=pltpu.CompilerParams(
            collective_id=collective_id, has_side_effects=True, vmem_limit_bytes=60 << 20
        ),
        name="scatter",
    )(*grads)


def own_lanes(head):
    lane = lax.broadcasted_iota(jnp.int32, (1, LANES), 1)
    return (lane < HEAD_DIM) == (head == 0)


def mask_once(ids_row, ids_column, mask):
    @pl.when(pl.program_id(1) == 0)
    def _():
        mask[...] = jnp.where(ids_column[0] == ids_row[0], 0.0, MASK_FILL).astype(F32)


def attend_kernel(ids_row, ids_column, qkv, attended, log_total, mask):
    mask_once(ids_row, ids_column, mask)
    query = qkv[:, 0:LANES] * BF16(SCALE)
    key = qkv[:, LANES : 2 * LANES]
    value = qkv[:, 2 * LANES : 3 * LANES]
    length = query.shape[0]
    chunk = length // 2
    outs = []
    for head in range(2):
        own_key = jnp.where(own_lanes(head), key, BF16(0))
        parts = []
        for at in range(0, length, chunk):
            scores = dot_over(own_key, query[at : at + chunk], 1, 1) + mask[:, at : at + chunk]
            top = jnp.max(scores, axis=0, keepdims=True)
            weights = jnp.exp(scores - top)
            total = jnp.sum(weights, axis=0, keepdims=True)
            log_total[0, 0, head : head + 1, at : at + chunk] = top + jnp.log(total)
            probs = (weights * (1.0 / total)).astype(BF16)
            parts.append(dot_over(probs, value, 0, 0))
        outs.append(jnp.concatenate(parts, axis=0))
    attended[...] = jnp.where(own_lanes(0), outs[0], outs[1]).astype(BF16)


def attend_back_kernel(ids_row, ids_column, qkv, attended_grad, log_total, qkv_grad, mask):
    mask_once(ids_row, ids_column, mask)
    query = qkv[:, 0:LANES]
    key = qkv[:, LANES : 2 * LANES]
    value = qkv[:, 2 * LANES : 3 * LANES]
    grad = attended_grad[...]
    scaled = query * BF16(SCALE)
    length = query.shape[0]
    chunk = length // 2
    query_grads, key_grads, value_grads = [], [], []
    for head in range(2):
        own_key = jnp.where(own_lanes(head), key, BF16(0))
        own_value = jnp.where(own_lanes(head), value, BF16(0))
        key_grad = value_grad = None
        parts = []
        for at in range(0, length, chunk):
            piece = slice(at, at + chunk)
            scores = dot_over(own_key, scaled[piece], 1, 1) + mask[:, piece]
            probs = jnp.exp(scores - log_total[0, 0, head : head + 1, piece])
            prob_grad = dot_over(own_value, grad[piece], 1, 1)
            row_dot = jnp.sum(probs * prob_grad, axis=0, keepdims=True)
            score_grad = (probs * (prob_grad - row_dot)).astype(BF16)
            value_part = dot_over(probs.astype(BF16), grad[piece], 1, 0)
            key_part = dot_over(score_grad, query[piece], 1, 0)
            value_grad = value_part if value_grad is None else value_grad + value_part
            key_grad = key_part if key_grad is None else key_grad + key_part
            parts.append(dot_over(score_grad, key, 0, 0))
        query_grads.append(jnp.concatenate(parts, axis=0))
        key_grads.append(key_grad)
        value_grads.append(value_grad)
    first = own_lanes(0)
    qkv_grad[:, 0:LANES] = (jnp.where(first, *query_grads) * SCALE).astype(BF16)
    qkv_grad[:, LANES : 2 * LANES] = (jnp.where(first, *key_grads) * SCALE).astype(BF16)
    qkv_grad[:, 2 * LANES : 3 * LANES] = jnp.where(first, *value_grads).astype(BF16)


def attention_specs(length):
    ids_row = pl.BlockSpec((1, 1, length), lambda b, h: (b, 0, 0))
    ids_column = pl.BlockSpec((1, length, 1), lambda b, h: (b, 0, 0))
    qkv = pl.BlockSpec((length, 3 * LANES), lambda b, h: (b, h))
    one = pl.BlockSpec((length, LANES), lambda b, h: (b, h))
    log_total = pl.BlockSpec((1, 1, 2, length), lambda b, h: (b, h, 0, 0))
    return ids_row, ids_column, qkv, one, log_total


def attend(qkv, doc_ids):
    count, length = doc_ids.shape
    ids_row, ids_column, wide, one, log_total = attention_specs(length)
    return pl.pallas_call(
        attend_kernel,
        grid=(count, PAIRS),
        in_specs=[ids_row, ids_column, wide],
        out_specs=[one, log_total],
        out_shape=[
            jax.ShapeDtypeStruct((count * length, D), BF16),
            jax.ShapeDtypeStruct((count, PAIRS, 2, length), F32),
        ],
        scratch_shapes=[pltpu.VMEM((length, length), F32)],
        name="attend",
    )(doc_ids.reshape(count, 1, length), doc_ids.reshape(count, length, 1), qkv)


def attend_back(qkv, doc_ids, attended_grad, totals):
    count, length = doc_ids.shape
    ids_row, ids_column, wide, one, log_total = attention_specs(length)
    return pl.pallas_call(
        attend_back_kernel,
        grid=(count, PAIRS),
        in_specs=[ids_row, ids_column, wide, one, log_total],
        out_specs=wide,
        out_shape=jax.ShapeDtypeStruct((count * length, 3 * D), BF16),
        scratch_shapes=[pltpu.VMEM((length, length), F32)],
        name="attend_back",
    )(
        doc_ids.reshape(count, 1, length),
        doc_ids.reshape(count, length, 1),
        qkv,
        attended_grad,
        totals,
    )


def split_vector(vector):
    sizes = (D, D, D, D, D, FF, D, D, D)
    parts, at = [], 0
    for size in sizes:
        parts.append(vector[at : at + size])
        at += size
    return parts


def by_pair(columns):
    rows = columns.shape[0]
    return columns.reshape(rows, 3, PAIRS, LANES).swapaxes(1, 2).reshape(rows, 3 * D)


def by_kind(columns):
    rows = columns.shape[0]
    return columns.reshape(rows, PAIRS, 3, LANES).swapaxes(1, 2).reshape(rows, 3 * D)


def normalized(hidden):
    center = hidden - jnp.mean(hidden, axis=-1, keepdims=True)
    root = lax.rsqrt(jnp.mean(center * center, axis=-1, keepdims=True) + NORM_EPS)
    return center * root, root


def norm_back(grad, normed, root, gain):
    scaled = grad * gain
    mean = jnp.mean(scaled, axis=-1, keepdims=True)
    along = jnp.mean(scaled * normed, axis=-1, keepdims=True)
    return root * (scaled - mean - normed * along)


def column_sums(rows):
    return jnp.sum(rows.astype(F32), axis=0)


def times(rows, matrix):
    return jnp.dot(rows, matrix, preferred_element_type=F32)


def weight_grad(left_rows, right_rows, dtype):
    return dot_over(left_rows, right_rows, 0, 0).astype(dtype)


def back_product(grad_rows, matrix):
    return dot_over(grad_rows, matrix, 1, 1)


def layer_step(tokens, doc_ids, cotangent, weights, grad_type):
    qkv_weight, proj_weight, up_weight, down_weight, vector = weights
    (
        bias_query,
        bias_value,
        bias_proj,
        gain_first,
        shift_first,
        bias_up,
        bias_down,
        gain_second,
        shift_second,
    ) = split_vector(vector.astype(F32))
    bias_all = jnp.concatenate([bias_query, jnp.zeros_like(bias_query), bias_value])
    bias_all = by_pair(bias_all[None])[0]
    qkv = (times(tokens, qkv_weight) + bias_all).astype(BF16)
    attended, totals = attend(qkv, doc_ids)
    hidden = tokens.astype(F32) + times(attended, proj_weight) + bias_proj
    normed, root = normalized(hidden)
    branch = normed * gain_first + shift_first
    branch_low = branch.astype(BF16)
    upward = times(branch_low, up_weight) + bias_up
    cdf = 0.5 * (1.0 + lax.erf(upward * HALF_ROOT))
    activated = (upward * cdf).astype(BF16)
    slope = cdf + upward * (PDF_TOP * jnp.exp(-0.5 * upward * upward))
    second_in = branch + times(activated, down_weight) + bias_down
    second_normed, second_root = normalized(second_in)
    output = (second_normed * gain_second + shift_second).astype(BF16)

    cotangent = cotangent.astype(F32)
    gain_second_grad = column_sums(cotangent * second_normed)
    shift_second_grad = column_sums(cotangent)
    second_grad = norm_back(cotangent, second_normed, second_root, gain_second)
    down_rows = second_grad.astype(BF16)
    down_grad = weight_grad(activated, down_rows, grad_type)
    up_rows = (back_product(down_rows, down_weight) * slope).astype(BF16)
    up_grad = weight_grad(branch_low, up_rows, grad_type)
    branch_grad = back_product(up_rows, up_weight) + second_grad
    gain_first_grad = column_sums(branch_grad * normed)
    shift_first_grad = column_sums(branch_grad)
    hidden_grad = norm_back(branch_grad, normed, root, gain_first)
    proj_rows = hidden_grad.astype(BF16)
    proj_grad = weight_grad(attended, proj_rows, grad_type)
    attended_grad = back_product(proj_rows, proj_weight).astype(BF16)
    qkv_rows = attend_back(qkv, doc_ids, attended_grad, totals)
    qkv_grad = weight_grad(tokens, qkv_rows, grad_type)
    qkv_sums = by_kind(column_sums(qkv_rows)[None])[0]
    input_grad = (back_product(qkv_rows, qkv_weight) + hidden_grad).astype(BF16)
    vector_grad = jnp.concatenate(
        [
            qkv_sums[0:D],
            qkv_sums[2 * D : 3 * D],
            column_sums(proj_rows),
            gain_first_grad,
            shift_first_grad,
            column_sums(up_rows),
            column_sums(down_rows),
            gain_second_grad,
            shift_second_grad,
        ]
    )
    return output, input_grad, (qkv_grad, proj_grad, up_grad, down_grad, vector_grad)


def adam_update(master, moment_one, moment_two, grad, rate):
    one_new = BETA_FIRST * moment_one + (1.0 - BETA_FIRST) * grad
    two_new = BETA_SECOND * moment_two + (1.0 - BETA_SECOND) * grad * grad
    one_hat = one_new / (1.0 - BETA_FIRST**STEP)
    two_hat = two_new / (1.0 - BETA_SECOND**STEP)
    master_new = master - rate * (one_hat / (jnp.sqrt(two_hat) + ADAM_EPS) + WEIGHT_DECAY * master)
    return (grad, one_new, two_new, master_new, master_new.astype(BF16))


WIDTHS = (3 * D, D, FF, D)


def gather_weights(masters, devices, depth):
    lowered = [master.astype(BF16) for master in masters]
    blocks = [low.reshape(-1, width) for low, width in zip(lowered, WIDTHS)]
    blocks[0] = by_pair(blocks[0])
    if not depth:
        flat = [lax.all_gather(block, "dp", axis=0, tiled=True) for block in blocks]
        return (*flat, lax.all_gather(lowered[4], "dp", axis=0, tiled=True))
    rows = lowered[4].shape[0] // LANES
    vector = jnp.pad(lowered[4].reshape(rows, LANES), ((0, 32 - rows), (0, 0)))
    full = gather([vector, *blocks], depth, 1)
    matrices = [whole.reshape(-1, width) for whole, width in zip(full[1:], WIDTHS)]
    return (*matrices, full[0].reshape(devices, 32, LANES)[:, :rows].reshape(-1))


def scatter_grads(grads, devices, depth):
    if not depth:
        owned = [
            lax.psum_scatter(
                grad.reshape(devices, -1, grad.shape[-1]), "dp", scatter_dimension=0, tiled=True
            )[0]
            for grad in (*grads[:4], grads[4][None].reshape(-1, 1))
        ]
    else:
        rows = grads[4].shape[0] // devices // LANES
        vector = jnp.pad(grads[4].reshape(devices, rows, LANES), ((0, 0), (0, 16 - rows), (0, 0)))
        shape = (depth, 2, 2, 2)
        blocks = [grad.reshape(*shape, -1, grad.shape[-1]) for grad in grads[:4]]
        owned = scatter([*reversed(blocks), vector.reshape(*shape, 16, LANES)], depth, 2)
        owned = [*reversed(owned[:4]), owned[4][:rows]]
    owned[0] = by_kind(owned[0])
    return [own.reshape(-1) for own in owned]


def body(depth, tokens, segment_ids, out_grad, *states):
    devices = lax.axis_size("dp")
    masters = states[0::3]
    weights = gather_weights(masters, devices, depth)
    grad_type = BF16 if depth else F32
    output, input_grad, grads = layer_step(tokens, segment_ids, out_grad, weights, grad_type)
    owned = scatter_grads(grads, devices, depth)
    outs = [output, input_grad]
    for i in range(5):
        outs += adam_update(*states[3 * i : 3 * i + 3], owned[i], RATES[i])
    return tuple(outs)


def solution(mesh):
    rows = P("dp", None)
    flat = P("dp")
    return jax.shard_map(
        functools.partial(body, depth_of(mesh)),
        mesh=mesh,
        in_specs=(rows,) * 3 + (flat,) * 15,
        out_specs=(rows,) * 2 + (flat,) * 25,
        check_vma=False,
    )
```

time: 1360 us -> 540 us (0.40)
  waiting for transfers between devices: 738 us -> 0 us
  Pallas kernels: 0 us -> 328 us
  matrix products: 310 us -> 146 us
  local copies, waits for them, and re-layouts: 126 us -> 25.8 us
  blocking collectives: 84.6 us -> 0 us
  other arithmetic: 76.7 us -> 29.2 us
  between operations: 15.5 us -> 1.66 us
    unnamed x6 -> x0, waiting for transfers between devices: 662 us -> none
    pallas_call x0 -> x4, Pallas kernels: none -> 328 us  [the longest x1 136 us: scatter(): pl.pallas_call(functools.partial(scatter_kernel, depth, count), in_specs=...]
    dot_general x36 -> x12, matrix products: 310 us -> 146 us  [the longest x8 95.3 us: dot_over(): lax.dot_general(left, right, (((left_dim,), (right_dim,)), ((), ())), pre...]
    all_gather x4 -> x0, waiting for transfers between devices: 76.7 us -> none  [the longest x1 67.3 us: body(): lax.all_gather(lowered[0], 'dp', axis=0, tiled=True)]
    add x6 -> x1, local copies, waits for them, and re-layouts: 51.8 us -> 0.01 us  [layer_step(): qkv = (times(tokens, qkv_weight) + bias_all).astype(BF16)]
    all_gather x1 -> x0, blocking collectives: 43.5 us -> none  [body(): lax.all_gather(lowered[4], 'dp', axis=0, tiled=True)]
    unnamed x1 -> x0, blocking collectives: 41.1 us -> none
    reshape x5 -> x8, local copies, waits for them, and re-layouts: 41.2 us -> 6.75 us  [the longest x3 2.29 us: gather_weights(): blocks = [low.reshape(-1, width) for low, width in zip(lowered, WIDTHS)]]
  transfers between devices with their start and end apart: 5 -> 0, of which waited for: 3 -> 0; matrix products, arithmetic and copies ran while one was open for 14% -> 0% of each run, Pallas kernels for 0% -> 0%
where the time goes in v1:
time: 540 us; the launch traced here: 531 us
  Pallas kernels  328 us (61%)
  matrix products  146 us (27%)
  other arithmetic  29.2 us (5%)
  local copies, waits for them, and re-layouts  25.8 us (5%)
    pallas_call x1, Pallas kernels, scatter(): pl.pallas_call(functools.partial(scatter_kernel, depth, count), in_specs=...  136 us
    pallas_call x1, Pallas kernels, gather(): pl.pallas_call(functools.partial(gather_kernel, depth, count), in_specs=[...  124 us
    dot_general x8, matrix products, dot_over(): lax.dot_general(left, right, (((left_dim,), (right_dim,)), ((), ())), pre...  95.3 us
    dot_general x4, matrix products, times(): return jnp.dot(rows, matrix, preferred_element_type=F32)  50.7 us
    pallas_call x1, Pallas kernels, attend_back(): pl.pallas_call(attend_back_kernel, grid=(count, PAIRS), in_specs=[ids_row...  39.8 us
    pallas_call x1, Pallas kernels, attend(): pl.pallas_call(attend_kernel, grid=(count, PAIRS), in_specs=[ids_row, ids...  28.5 us
    unnamed x83, local copies, waits for them, and re-layouts  17.6 us
    reduce_sum x4, other arithmetic, column_sums(): return jnp.sum(rows.astype(F32), axis=0)  12.3 us

profile of v1, /device:TPU:0, one launch (start us, length us, event | category | flops | bytes accessed | tf_op | source)
XLA Modules:
  0.0 530.9 jit_solution(12828840088598730213)
XLA Ops:
  0.7 0.0 copy-start.23
  0.7 0.8 convert_bitcast_fusion
  1.5 1.3 reshape.178.ids_row
  2.8 0.6 pad.8.refs_0_
  3.4 0.9 convert_element_type.105
  4.3 0.7 reshape.182.refs_2_
  5.0 1.0 convert_element_type.104
  6.0 0.1 copy.66
  6.1 0.8 reshape.181.refs_1_
  7.0 1.1 convert_element_type.106
  8.0 0.8 reshape.183.refs_3_
  8.9 1.1 convert_element_type.107
  9.9 0.8 reshape.184.refs_4_
  10.7 1.0 copy.69.ids_column
  11.8 2.5 copy.71
  14.3 4.1 copy.65
  18.4 123.9 %gather.1 = (bf16[4,2,2,2,32,128]{5,4,3,2,1,0:T(8,128)(2,1)}, bf16[4,2,2,2,32,3072]{5,4,3,2,1,0:T(8,128)(2,1)}, bf16[4,2,2,2,32,1024]{5,4,3,2,1,0:T(8,128)(2,1)}...) custom-call(bf16[32,128]{1,0:T(8,128)(2,1)} %pad.8.refs_0_, ...), custom_call_target="tpu_custom_call" | custom-call | tf_op jit(solution)/shard_map/gather/pallas_call | solution.py:221
  142.3 0.8 slice_convert_fusion
  143.3 11.4 %fusion.6.qkv = bf16[1024,3072]{1,0:T(8,128)(2,1)} fusion(f32[3072]{0:T(1024)S(1)} %add.161, bf16[1024,1024]{1,0:T(8,128)(2,1)S(1)} %copy-done.11, bf16[1024,3072]{1,0:T(8,128)(2,1)} %bitcast.87), kind=kOutput, calls=%fused_computation.14 | convolution fusion | flops 6448742400 | bytes 14692352 | tf_op jit(solution)/shard_map/dot_general | solution.py:548
  154.7 28.5 %attend.1 = (bf16[1024,1024]{1,0:T(8,128)(2,1)}, f32[2,8,2,512]{3,2,1,0:T(2,128)}) custom-call(s32[2,1,512]{2,1,0:T(1,128)} %reshape.178.ids_row, s32[2,512,1]{2,1,0:T(8,128)} %copy.69.ids_column, bf16[1024,3072]{1,0:T(8,128)(2,1)} %fusion.6.qkv), custom_call_target="tpu_custom_call" | custom-call | tf_op jit(solution)/shard_map/attend/pallas_call | solution.py:477
  183.2 4.8 fusion.39
  188.0 0.5 multiply_reduce_fusion.3
  188.5 19.6 %multiply_convert_fusion = (bf16[1024,4096]{1,0:T(8,128)(2,1)}, f32[1024,4096]{1,0:T(8,128)}) fusion(f32[4096]{0:T(1024)S(1)} %slice.66, bf16[1024,4096]{1,0:T(8,128)(2,1)} %bitcast.81, f32[1024,1024]{0,1:T(8,128)S(1)} %get-tuple-element.177, f32[1024]{0:T(1024)S(1)} %get-tuple-element.169, f32[1024]{0:T(1024)S(1)} %get-tuple-element.170, ...), kind=kOutput, calls=%fused_computation.8 | convolution fusion | flops 8620343296 | bytes 37781504 | tf_op jit(solution)/shard_map/dot_general | solution.py:548
  208.1 14.9 %fusion.40 = (f32[1024]{0:T(1024)S(1)}, f32[1024,1024]{0,1:T(8,128)S(1)}) fusion(f32[1024]{0:T(1024)S(1)} %get-tuple-element.168, bf16[1024,4096]{1,0:T(8,128)(2,1)} %get-tuple-element.178, bf16[4096,1024]{1,0:T(8,128)(2,1)} %bitcast.83, f32[1024]{0:T(1024)S(1)} %get-tuple-element.169, f32[1024]{0:T(1024)S(1)} %get-tuple-element.170, ...), kind=kOutput, calls=%fused_computation.98 | convolution fusion | flops 8597273600 | bytes 25190400 | tf_op jit(solution)/shard_map/dot_general | solution.py:548
  223.0 0.0 copy-start.1
  223.0 0.5 multiply_reduce_fusion.2
  223.5 1.1 copy-done.1
  224.6 3.3 fusion.13
  227.9 3.8 convert_reduce_fusion.3
  231.6 18.7 %convert_reduce_fusion = (f32[4096]{0:T(1024)S(1)}, bf16[1024,4096]{1,0:T(8,128)(2,1)}) fusion(f32[1024,4096]{1,0:T(8,128)} %get-tuple-element.179, f32[4096]{0:T(1024)S(1)} %slice.66, bf16[1024,1024]{0,1:T(8,128)(2,1)S(1)} %get-tuple-element.162, bf16[4096,1024]{1,0:T(8,128)(2,1)S(1)} %bitcast.86), kind=kOutput, calls=%fused_computation.7 | convolution fusion | flops 8644456448 | bytes 35684352 | tf_op jit(solution)/shard_map/dot_general | solution.py:35
  250.3 16.1 %multiply_reduce_fusion = (f32[1024]{0:T(1024)S(1)}, f32[1024]{0:T(1024)S(1)}, f32[1024]{0:T(1024)S(1)}, f32[1024]{0:T(1024)S(1)}, f32[1024,1024]{0,1:T(8,128)S(1)}) fusion(f32[1024,1024]{0,1:T(8,128)S(1)} %copy-done.3, f32[1024]{0:T(1024)S(1)} %add_rsqrt_fusion.1, f32[1024]{0:T(1024)S(1)} %broadcast_multiply_fusion.5, f32[1024]{0:T(1024)S(1)} %get-tuple-element.170, ...), kind=kOutput, calls=%fused_computation.27 | convolution fusion | flops 8608804864 | bytes 31506432 | tf_op jit(solution)/shard_map/dot_general | solution.py:35
  266.4 14.8 %convolution_convert_fusion.1 = bf16[4096,1024]{1,0:T(8,128)(2,1)} fusion(bf16[1024,4096]{1,0:T(8,128)(2,1)} %get-tuple-element.178, bf16[1024,1024]{0,1:T(8,128)(2,1)S(1)} %get-tuple-element.162), kind=kOutput, calls=%fused_computation.13 | convolution fusion | flops 8594128896 | bytes 18874368 | tf_op jit(solution)/shard_map/dot_general | solution.py:35
  281.3 1.4 convert_reduce_fusion.4
  282.7 0.0 copy-start.31
  282.7 16.6 %convolution_convert_fusion = bf16[1024,4096]{1,0:T(8,128)(2,1)} fusion(bf16[1024,4096]{1,0:T(8,128)(2,1)} %get-tuple-element.184, f32[1024,1024]{0,1:T(8,128)S(1)} %copy-done.3, f32[1024]{0:T(1024)S(1)} %get-tuple-element.169, f32[1024]{0:T(1024)S(1)} %get-tuple-element.170, f32[1024]{0:T(1024)S(1)} %add_rsqrt_fusion.1, f32[1024]{0:T(1024)S(1)} %broadcast_multiply_fusion.5), kind=kOutput, calls=%fused_computation.12 | convolution fusion | flops 8599371776 | bytes 20987904 | tf_op jit(solution)/shard_map/dot_general | solution.py:35
  299.4 3.7 convolution_convert_fusion.3
  303.1 3.7 convolution_convert_fusion.4.attended_grad
  306.8 39.8 %attend_back.1 = bf16[1024,3072]{1,0:T(8,128)(2,1)} custom-call(s32[2,1,512]{2,1,0:T(1,128)} %reshape.178.ids_row, s32[2,512,1]{2,1,0:T(8,128)} %copy.69.ids_column, bf16[1024,3072]{1,0:T(8,128)(2,1)} %fusion.6.qkv, bf16[1024,1024]{1,0:T(8,128)(2,1)} %convolution_convert_fusion.4.attended_grad, f32[2,8,2,512]{3,2,1,0:T(2,128)} %get-tuple-element.45.log_total), custom_call_target="tpu_custom_call" | custom-call | tf_op jit(solution)/shard_map/attend_back/pallas_call | solution.py:494
  346.6 12.3 %add_convert_fusion.1 = bf16[1024,1024]{0,1:T(8,128)(2,1)} fusion(f32[1024,1024]{0,1:T(8,128)} %copy-done.5, bf16[1024,3072]{1,0:T(8,128)(2,1)} %attend_back.1, bf16[1024,3072]{1,0:T(8,128)(2,1)} %bitcast.88), kind=kOutput, calls=%fused_computation.29 | convolution fusion | flops 6444548096 | bytes 18874368 | tf_op jit(solution)/shard_map/dot_general | solution.py:35
  358.9 4.1 copy.77
  362.9 3.9 convert_reduce_fusion.1
  366.8 0.7 copy-done
  367.6 9.3 %convolution_convert_fusion.2 = bf16[3072,1024]{0,1:T(8,128)(2,1)} fusion(bf16[1024,3072]{1,0:T(8,128)(2,1)S(1)} %copy-done, bf16[1024,1024]{1,0:T(8,128)(2,1)S(1)} %copy-done.12), kind=kOutput, calls=%fused_computation.21 | convolution fusion | flops 6445596672 | bytes 14680064 | tf_op jit(solution)/shard_map/dot_general | solution.py:35
  377.1 0.7 pad.9
  377.8 136.0 %scatter.1 = (f32[128,1024]{1,0:T(8,128)}, f32[32,4096]{1,0:T(8,128)}, f32[32,1024]{1,0:T(8,128)}, f32[32,3072]{1,0:T(8,128)}, f32[16,128]{1,0:T(8,128)}) custom-call(bf16[4,2,2,2,128,1024]{5,4,3,2,1,0:T(8,128)(2,1)} %bitcast.58, bf16[4,2,2,2,32,4096]{5,4,3,2,1,0:T(8,128)(2,1)} %bitcast.59, bf16[4,2,2,2,32,1024]{5,4,3,2,1,0:T(8,128)(2,1)} %bitcast.61, ...), custom_call_target="tpu_custom_call" | custom-call | tf_op jit(solution)/shard_map/scatter/pallas_call | solution.py:382
  513.8 0.0 copy-start.15
  513.8 0.0 copy-start.22
  513.8 0.0 copy-start.6
  513.8 0.0 copy-start.16
  513.8 1.1 copy.82
  514.9 0.0 copy-start.20
  515.0 1.3 fusion.26
  516.3 1.3 reshape.196
  517.6 0.0 copy-start.14
  517.6 1.9 fusion.32
  519.5 1.1 copy.83
  520.7 0.0 copy-start.8
  520.7 0.0 copy-start.18
  520.7 0.1 copy.84
  520.8 0.0 copy-start.9
  520.9 2.7 fusion.34
  523.6 2.7 fusion.28
  526.3 1.5 fusion.30
  527.9 2.6 copy.76
  (82 shorter events, 0.3 us)
Async XLA Ops:
  0.7 10.1 %copy-start.23 = (s32[2,512]{1,0:T(2,128)S(1)}, s32[2,512]{1,0:T(2,128)}, u32[]{:S(2)}) copy-start(s32[2,512]{1,0:T(2,128)} %param.19) | copy-start | bytes 12292
  0.7 11.1 %copy-start.10 = (bf16[1024,1024]{1,0:T(8,128)(2,1)S(1)}, bf16[1024,1024]{1,0:T(8,128)(2,1)}, u32[]{:S(2)}) copy-start(bf16[1024,1024]{1,0:T(8,128)(2,1)} %param.20) | copy-start | bytes 6291460
  14.3 128.9 %copy-start.11 = (bf16[1024,1024]{1,0:T(8,128)(2,1)S(1)}, bf16[1024,1024]{1,0:T(8,128)(2,1)}, u32[]{:S(2)}) copy-start(bf16[1024,1024]{1,0:T(8,128)(2,1)} %param.18) | copy-start | bytes 6291460
  154.7 28.5 %copy-start.13 = (bf16[1024,1024]{0,1:T(8,128)(2,1)S(1)}, bf16[1024,1024]{0,1:T(8,128)(2,1)}, u32[]{:S(2)}) copy-start(bf16[1024,1024]{0,1:T(8,128)(2,1)} %copy.65) | copy-start | bytes 6291460
  188.0 20.1 %copy-start.2 = (f32[1024,1024]{0,1:T(8,128)}, f32[1024,1024]{0,1:T(8,128)S(1)}, u32[]{:S(2)}) copy-start(f32[1024,1024]{0,1:T(8,128)S(1)} %get-tuple-element.177) | copy-start | bytes 12582916
  223.0 1.6 copy-start.1
  224.6 7.0 %slice-start = ((s8[8388608]{0:T(1024)(128)(4,1)}), s8[4194304]{0:T(1024)(128)(4,1)S(1)}, s32[]{:S(2)}) async-start(s8[8388608]{0:T(1024)(128)(4,1)} %bitcast.84), calls=%async_computation | async-start | bytes 8388608
  227.9 3.8 slice-start.1
  231.6 18.7 %copy-start.3 = (f32[1024,1024]{0,1:T(8,128)S(1)}, f32[1024,1024]{0,1:T(8,128)}, u32[]{:S(2)}) copy-start(f32[1024,1024]{0,1:T(8,128)} %copy-done.2) | copy-start | bytes 12582916
  282.7 20.3 %copy-start.5 = (f32[1024,1024]{0,1:T(8,128)}, f32[1024,1024]{0,1:T(8,128)S(1)}, u32[]{:S(2)}) copy-start(f32[1024,1024]{0,1:T(8,128)S(1)} %get-tuple-element.164) | copy-start | bytes 12582916
  282.7 16.6 %copy-start.31 = (bf16[1024,1024]{1,0:T(8,128)(2,1)S(1)}, bf16[1024,1024]{1,0:T(8,128)(2,1)}, u32[]{:S(2)}) copy-start(bf16[1024,1024]{1,0:T(8,128)(2,1)} %get-tuple-element.41) | copy-start | bytes 6291460
  299.4 3.7 copy-start.30
  358.9 7.9 %copy-start.12 = (bf16[1024,1024]{1,0:T(8,128)(2,1)S(1)}, bf16[1024,1024]{1,0:T(8,128)(2,1)}, u32[]{:S(2)}) copy-start(bf16[1024,1024]{1,0:T(8,128)(2,1)} %param.18) | copy-start | bytes 6291460
  362.9 4.6 copy-start
  367.5 9.4 %copy-start.24 = (f32[1024]{0:T(1024)S(1)}, f32[1024]{0:T(1024)}, u32[]{:S(2)}) copy-start(f32[1024]{0:T(1024)} %get-tuple-element.161) | copy-start | bytes 12292
  367.5 9.5 %copy-start.26 = (f32[1024]{0:T(1024)S(1)}, f32[1024]{0:T(1024)}, u32[]{:S(2)}) copy-start(f32[1024]{0:T(1024)} %get-tuple-element.134) | copy-start | bytes 12292
  367.6 9.5 %copy-start.25 = (f32[1024]{0:T(1024)S(1)}, f32[1024]{0:T(1024)}, u32[]{:S(2)}) copy-start(f32[1024]{0:T(1024)} %get-tuple-element.139) | copy-start | bytes 12292
  377.8 137.1 %copy-start.27 = (f32[384]{0:T(512)S(1)}, f32[384]{0:T(512)}, u32[]{:S(2)}) copy-start(f32[384]{0:T(512)} %param.33) | copy-start | bytes 4612
  377.8 137.1 %copy-start.28 = (f32[384]{0:T(512)S(1)}, f32[384]{0:T(512)}, u32[]{:S(2)}) copy-start(f32[384]{0:T(512)} %param.35) | copy-start | bytes 4612
  377.8 137.1 %copy-start.29 = (f32[384]{0:T(512)S(1)}, f32[384]{0:T(512)}, u32[]{:S(2)}) copy-start(f32[384]{0:T(512)} %param.34) | copy-start | bytes 4612
  377.8 139.8 %copy-start.19 = (f32[32768]{0:T(1024)S(1)}, f32[32768]{0:T(1024)}, u32[]{:S(2)}) copy-start(f32[32768]{0:T(1024)} %param.24) | copy-start | bytes 393220
  513.8 6.9 %copy-start.21 = (f32[128,1024]{1,0:T(8,128)S(1)}, f32[128,1024]{1,0:T(8,128)}, u32[]{:S(2)}) copy-start(f32[128,1024]{1,0:T(8,128)} %get-tuple-element.49) | copy-start | bytes 1572868
  513.8 7.1 %copy-start.15 = (f32[98304]{0:T(1024)S(1)}, f32[98304]{0:T(1024)}, u32[]{:S(2)}) copy-start(f32[98304]{0:T(1024)} %param.21) | copy-start | bytes 1179652
  513.8 7.1 %copy-start.22 = (f32[98304]{0:T(1024)S(1)}, f32[98304]{0:T(1024)}, u32[]{:S(2)}) copy-start(f32[98304]{0:T(1024)} %param.23) | copy-start | bytes 1179652
  513.8 9.8 %copy-start.6 = (f32[131072]{0:T(1024)S(1)}, f32[131072]{0:T(1024)}, u32[]{:S(2)}) copy-start(f32[131072]{0:T(1024)} %param.30) | copy-start | bytes 1572868
  513.8 9.8 %copy-start.16 = (f32[131072]{0:T(1024)S(1)}, f32[131072]{0:T(1024)}, u32[]{:S(2)}) copy-start(f32[131072]{0:T(1024)} %param.32) | copy-start | bytes 1572868
  514.9 5.9 %copy-start.20 = (f32[4,8,8,128]{3,1,2,0:T(8,128)}, f32[4,8,8,128]{3,1,2,0:T(8,128)S(1)}, u32[]{:S(2)}) copy-start(f32[4,8,8,128]{3,1,2,0:T(8,128)S(1)} %copy.82) | copy-start | bytes 393220
  517.6 8.7 %copy-start.14 = (f32[32,3,8,128]{3,2,1,0:T(8,128)}, f32[32,3,8,128]{3,2,1,0:T(8,128)S(1)}, u32[]{:S(2)}) copy-start(f32[32,3,8,128]{3,2,1,0:T(8,128)S(1)} %copy.75) | copy-start | bytes 1179652
  520.7 7.2 %copy-start.8 = (f32[4,32,8,128]{3,1,2,0:T(8,128)}, f32[4,32,8,128]{3,1,2,0:T(8,128)S(1)}, u32[]{:S(2)}) copy-start(f32[4,32,8,128]{3,1,2,0:T(8,128)S(1)} %copy.83) | copy-start | bytes 1572868
  520.7 5.6 %copy-start.7 = (f32[131072]{0:T(1024)S(1)}, f32[131072]{0:T(1024)}, u32[]{:S(2)}) copy-start(f32[131072]{0:T(1024)} %param.27) | copy-start | bytes 1572868
  520.7 5.6 %copy-start.17 = (f32[131072]{0:T(1024)S(1)}, f32[131072]{0:T(1024)}, u32[]{:S(2)}) copy-start(f32[131072]{0:T(1024)} %param.29) | copy-start | bytes 1572868
  520.7 5.6 %copy-start.18 = (f32[131072]{0:T(1024)S(1)}, f32[131072]{0:T(1024)}, u32[]{:S(2)}) copy-start(f32[131072]{0:T(1024)} %param.28) | copy-start | bytes 1572868
  520.8 7.0 %copy-start.9 = (f32[16,8,8,128]{3,1,2,0:T(8,128)}, f32[16,8,8,128]{3,1,2,0:T(8,128)S(1)}, u32[]{:S(2)}) copy-start(f32[16,8,8,128]{3,1,2,0:T(8,128)S(1)} %copy.84) | copy-start | bytes 1572868
  523.6 4.2 copy-start.4

commit v2 on v1

--- a/solution.py
+++ b/solution.py
@@ -190,15 +190,23 @@
         if 0 <= t - 2 * lag < len(units):
             self.hand_over(*units[t - 2 * lag])
 
+    def units(self):
+        return [(w, k) for w in range(len(self.blocks)) for k in range(self.depth)]
+
+    def start_all(self):
+        for w in range(len(self.blocks)):
+            self.start(w)
+
+    def finish_all(self):
+        for w in range(len(self.blocks)):
+            self.finish(w)
+
     def run(self):
-        count = len(self.blocks)
-        for w in range(count):
-            self.start(w)
-        units = [(w, k) for w in range(count) for k in range(self.depth)]
+        self.start_all()
+        units = self.units()
         for t in range(len(units) + 2 * self.depth):
             self.step(units, t)
-        for w in range(count):
-            self.finish(w)
+        self.finish_all()
 
 
 def gather_kernel(depth, count, *refs):
@@ -344,15 +352,23 @@
         if 0 <= t - 2 * lag < len(units):
             self.third(*units[t - 2 * lag])
 
+    def units(self):
+        return [(w, k) for w in range(len(self.grads)) for k in self.order]
+
+    def start_all(self):
+        for w in range(len(self.grads)):
+            self.start(w)
+
+    def finish_all(self):
+        for w in range(len(self.grads)):
+            self.finish(w)
+
     def run(self):
-        count = len(self.grads)
-        for w in range(count):
-            self.start(w)
-        units = [(w, k) for w in range(count) for k in self.order]
+        self.start_all()
+        units = self.units()
         for t in range(len(units) + 2 * self.depth):
             self.step(units, t)
-        for w in range(count):
-            self.finish(w)
+        self.finish_all()
 
 
 def scatter_scratch(grads, depth):
@@ -397,25 +413,60 @@
     return (lane < HEAD_DIM) == (head == 0)
 
 
-def mask_once(ids_row, ids_column, mask):
-    @pl.when(pl.program_id(1) == 0)
-    def _():
-        mask[...] = jnp.where(ids_column[0] == ids_row[0], 0.0, MASK_FILL).astype(F32)
-
-
-def attend_kernel(ids_row, ids_column, qkv, attended, log_total, mask):
-    mask_once(ids_row, ids_column, mask)
+def fill_masks(ids_row, ids_column, masks):
+    for b in range(masks.shape[0]):
+        masks[b] = jnp.where(ids_column[b] == ids_row[b], 0.0, MASK_FILL).astype(F32)
+
+
+def at_step(t, work):
+    pl.when(pl.program_id(0) * pl.num_programs(1) + pl.program_id(1) == t)(work)
+
+
+def host(side, steps):
+    units = side.units()
+    count = len(units) + 2 * side.depth
+
+    def open_up():
+        side.place.greet()
+        side.start_all()
+
+    at_step(0, open_up)
+    for t in range(min(count, steps - 1)):
+        at_step(t, functools.partial(side.step, units, t))
+
+    def rest():
+        for t in range(steps - 1, count):
+            side.step(units, t)
+        side.finish_all()
+
+    return lambda: at_step(steps - 1, rest)
+
+
+def attend_kernel(depth, count, steps, *refs):
+    ids_row, ids_column, tokens, weight, bias = refs[:5]
+    blocks, refs = refs[5 : 5 + count], refs[5 + count :]
+    qkv, attended, log_total = refs[:3]
+    full, refs = refs[3 : 3 + count], refs[3 + count :]
+    masks, sems = refs[0], refs[1:]
+    finish = None
+    if count:
+        finish = host(Gather(Place(depth), blocks, full, *sems), steps)
+    at_step(0, lambda: fill_masks(ids_row, ids_column, masks))
+    b = pl.program_id(1)
+    length = masks.shape[1]
+    rows = tokens[pl.ds(pl.multiple_of(b * length, length), length), :]
+    qkv[...] = (dot_over(rows, weight[...], 1, 0) + bias[0]).astype(BF16)
     query = qkv[:, 0:LANES] * BF16(SCALE)
     key = qkv[:, LANES : 2 * LANES]
     value = qkv[:, 2 * LANES : 3 * LANES]
-    length = query.shape[0]
     chunk = length // 2
     outs = []
     for head in range(2):
         own_key = jnp.where(own_lanes(head), key, BF16(0))
         parts = []
         for at in range(0, length, chunk):
-            scores = dot_over(own_key, query[at : at + chunk], 1, 1) + mask[:, at : at + chunk]
+            scores = dot_over(own_key, query[at : at + chunk], 1, 1)
+            scores = scores + masks[b, :, at : at + chunk]
             top = jnp.max(scores, axis=0, keepdims=True)
             weights = jnp.exp(scores - top)
             total = jnp.sum(weights, axis=0, keepdims=True)
@@ -424,10 +475,22 @@
             parts.append(dot_over(probs, value, 0, 0))
         outs.append(jnp.concatenate(parts, axis=0))
     attended[...] = jnp.where(own_lanes(0), outs[0], outs[1]).astype(BF16)
-
-
-def attend_back_kernel(ids_row, ids_column, qkv, attended_grad, log_total, qkv_grad, mask):
-    mask_once(ids_row, ids_column, mask)
+    if finish:
+        finish()
+
+
+def attend_back_kernel(depth, count, steps, *refs):
+    ids_row, ids_column, tokens, qkv, attended_grad, log_total = refs[:6]
+    grads, refs = refs[6 : 6 + count], refs[6 + count :]
+    qkv_grad, weight_grads, sums = refs[:3]
+    out, refs = refs[3 : 3 + count], refs[3 + count :]
+    masks, refs = refs[0], refs[1:]
+    finish = None
+    if count:
+        bufs = [refs[7 * w : 7 * w + 7] for w in range(count)]
+        finish = host(Scatter(Place(depth), grads, out, bufs, *refs[7 * count : -1]), steps)
+    at_step(0, lambda: fill_masks(ids_row, ids_column, masks))
+    b = pl.program_id(1)
     query = qkv[:, 0:LANES]
     key = qkv[:, LANES : 2 * LANES]
     value = qkv[:, 2 * LANES : 3 * LANES]
@@ -443,7 +506,7 @@
         parts = []
         for at in range(0, length, chunk):
             piece = slice(at, at + chunk)
-            scores = dot_over(own_key, scaled[piece], 1, 1) + mask[:, piece]
+            scores = dot_over(own_key, scaled[piece], 1, 1) + masks[b, :, piece]
             probs = jnp.exp(scores - log_total[0, 0, head : head + 1, piece])
             prob_grad = dot_over(own_value, grad[piece], 1, 1)
             row_dot = jnp.sum(probs * prob_grad, axis=0, keepdims=True)
@@ -460,51 +523,112 @@
     qkv_grad[:, 0:LANES] = (jnp.where(first, *query_grads) * SCALE).astype(BF16)
     qkv_grad[:, LANES : 2 * LANES] = (jnp.where(first, *key_grads) * SCALE).astype(BF16)
     qkv_grad[:, 2 * LANES : 3 * LANES] = jnp.where(first, *value_grads).astype(BF16)
-
-
-def attention_specs(length):
-    ids_row = pl.BlockSpec((1, 1, length), lambda b, h: (b, 0, 0))
-    ids_column = pl.BlockSpec((1, length, 1), lambda b, h: (b, 0, 0))
-    qkv = pl.BlockSpec((length, 3 * LANES), lambda b, h: (b, h))
-    one = pl.BlockSpec((length, LANES), lambda b, h: (b, h))
-    log_total = pl.BlockSpec((1, 1, 2, length), lambda b, h: (b, h, 0, 0))
-    return ids_row, ids_column, qkv, one, log_total
-
-
-def attend(qkv, doc_ids):
+    rows = tokens[pl.ds(pl.multiple_of(b * length, length), length), :]
+    rows_grad = qkv_grad[...]
+    part = dot_over(rows, rows_grad, 0, 0)
+    part_sums = jnp.sum(rows_grad.astype(F32), axis=0, keepdims=True)
+    total = refs[-1]
+
+    @pl.when(b == 0)
+    def _():
+        total[...] = part
+        sums[0] = part_sums
+
+    @pl.when(b > 0)
+    def _():
+        total[...] += part
+        sums[0] += part_sums
+
+    @pl.when(b == pl.num_programs(1) - 1)
+    def _():
+        weight_grads[...] = total[...].astype(weight_grads.dtype)
+
+    if finish:
+        finish()
+
+
+def whole(shape):
+    return pl.BlockSpec(shape, lambda h, b: (0,) * len(shape))
+
+
+def attention_specs(count, length):
+    rows = whole((count, 1, length))
+    columns = whole((count, length, 1))
+    tokens = whole((count * length, D))
+    wide = pl.BlockSpec((length, 3 * LANES), lambda h, b: (b, h))
+    one = pl.BlockSpec((length, LANES), lambda h, b: (b, h))
+    log_total = pl.BlockSpec((1, 1, 2, length), lambda h, b: (b, h, 0, 0))
+    weight = pl.BlockSpec((D, 3 * LANES), lambda h, b: (0, h))
+    vector = pl.BlockSpec((1, 1, 3 * LANES), lambda h, b: (h, 0, 0))
+    return rows, columns, tokens, wide, one, log_total, weight, vector
+
+
+def kernel_params(collective_id, count):
+    if not count:
+        return pltpu.CompilerParams(vmem_limit_bytes=60 << 20)
+    return pltpu.CompilerParams(
+        collective_id=collective_id, has_side_effects=True, vmem_limit_bytes=60 << 20
+    )
+
+
+def attend(tokens, doc_ids, weight, bias, blocks, depth, collective_id):
     count, length = doc_ids.shape
-    ids_row, ids_column, wide, one, log_total = attention_specs(length)
+    rows, columns, all_tokens, wide, one, log_total, part, vector = attention_specs(count, length)
+    in_place = pl.BlockSpec(memory_space=pl.ANY)
     return pl.pallas_call(
-        attend_kernel,
-        grid=(count, PAIRS),
-        in_specs=[ids_row, ids_column, wide],
-        out_specs=[one, log_total],
+        functools.partial(attend_kernel, depth, len(blocks), PAIRS * count),
+        grid=(PAIRS, count),
+        in_specs=[rows, columns, all_tokens, part, vector] + [whole(b.shape) for b in blocks],
+        out_specs=[wide, one, log_total] + [in_place] * len(blocks),
         out_shape=[
+            jax.ShapeDtypeStruct((count * length, 3 * D), BF16),
             jax.ShapeDtypeStruct((count * length, D), BF16),
             jax.ShapeDtypeStruct((count, PAIRS, 2, length), F32),
-        ],
-        scratch_shapes=[pltpu.VMEM((length, length), F32)],
+        ]
+        + [jax.ShapeDtypeStruct((depth, 2, 2, 2) + b.shape, b.dtype) for b in blocks],
+        scratch_shapes=[pltpu.VMEM((count, length, length), F32)]
+        + (gather_sems(len(blocks), depth) if blocks else []),
+        compiler_params=kernel_params(collective_id, len(blocks)),
         name="attend",
-    )(doc_ids.reshape(count, 1, length), doc_ids.reshape(count, length, 1), qkv)
-
-
-def attend_back(qkv, doc_ids, attended_grad, totals):
+    )(
+        doc_ids.reshape(count, 1, length),
+        doc_ids.reshape(count, length, 1),
+        tokens,
+        weight,
+        bias.reshape(PAIRS, 1, 3 * LANES),
+        *blocks,
+    )
+
+
+def attend_back(tokens, qkv, doc_ids, attended_grad, totals, dtype, grads, depth, collective_id):
     count, length = doc_ids.shape
-    ids_row, ids_column, wide, one, log_total = attention_specs(length)
+    rows, columns, all_tokens, wide, one, log_total, part, vector = attention_specs(count, length)
+    in_place = pl.BlockSpec(memory_space=pl.ANY)
+    blocks = [g.shape[-2:] for g in grads]
     return pl.pallas_call(
-        attend_back_kernel,
-        grid=(count, PAIRS),
-        in_specs=[ids_row, ids_column, wide, one, log_total],
-        out_specs=wide,
-        out_shape=jax.ShapeDtypeStruct((count * length, 3 * D), BF16),
-        scratch_shapes=[pltpu.VMEM((length, length), F32)],
+        functools.partial(attend_back_kernel, depth, len(grads), PAIRS * count),
+        grid=(PAIRS, count),
+        in_specs=[rows, columns, all_tokens, wide, one, log_total] + [in_place] * len(grads),
+        out_specs=[wide, part, vector] + [whole(shape) for shape in blocks],
+        out_shape=[
+            jax.ShapeDtypeStruct((count * length, 3 * D), BF16),
+            jax.ShapeDtypeStruct((D, 3 * D), dtype),
+            jax.ShapeDtypeStruct((PAIRS, 1, 3 * LANES), F32),
+        ]
+        + [jax.ShapeDtypeStruct(shape, F32) for shape in blocks],
+        scratch_shapes=[pltpu.VMEM((count, length, length), F32)]
+        + (scatter_scratch(grads, depth) if grads else [])
+        + [pltpu.VMEM((D, 3 * LANES), F32)],
+        compiler_params=kernel_params(collective_id, len(grads)),
         name="attend_back",
     )(
         doc_ids.reshape(count, 1, length),
         doc_ids.reshape(count, length, 1),
+        tokens,
         qkv,
         attended_grad,
         totals,
+        *grads,
     )
 
 
@@ -556,8 +680,20 @@
     return dot_over(grad_rows, matrix, 1, 1)
 
 
-def layer_step(tokens, doc_ids, cotangent, weights, grad_type):
-    qkv_weight, proj_weight, up_weight, down_weight, vector = weights
+def layer_step(tokens, doc_ids, cotangent, masters, devices, depth):
+    grad_type = BF16 if depth else F32
+    shape = (depth, 2, 2, 2)
+    blocks, low_vector = lowered_blocks(masters)
+    if depth:
+        rows = low_vector.shape[0] // LANES
+        padded = jnp.pad(low_vector.reshape(rows, LANES), ((0, 32 - rows), (0, 0)))
+        vectors, qkv_weight = gather([padded, blocks[0]], depth, 1)
+        vector = vectors.reshape(devices, 32, LANES)[:, :rows].reshape(-1)
+        qkv_weight = qkv_weight.reshape(D, 3 * D)
+    else:
+        weights = [lax.all_gather(b, "dp", axis=0, tiled=True) for b in blocks]
+        qkv_weight, proj_weight, up_weight, down_weight = weights
+        vector = lax.all_gather(low_vector, "dp", axis=0, tiled=True)
     (
         bias_query,
         bias_value,
@@ -571,8 +707,14 @@
     ) = split_vector(vector.astype(F32))
     bias_all = jnp.concatenate([bias_query, jnp.zeros_like(bias_query), bias_value])
     bias_all = by_pair(bias_all[None])[0]
-    qkv = (times(tokens, qkv_weight) + bias_all).astype(BF16)
-    attended, totals = attend(qkv, doc_ids)
+    riders = blocks[1:] if depth else []
+    qkv, attended, totals, *carried = attend(
+        tokens, doc_ids, qkv_weight, bias_all, riders, depth, 2
+    )
+    if depth:
+        proj_weight, up_weight, down_weight = [
+            c.reshape(-1, width) for c, width in zip(carried, WIDTHS[1:])
+        ]
     hidden = tokens.astype(F32) + times(attended, proj_weight) + bias_proj
     normed, root = normalized(hidden)
     branch = normed * gain_first + shift_first
@@ -600,10 +742,12 @@
     proj_rows = hidden_grad.astype(BF16)
     proj_grad = weight_grad(attended, proj_rows, grad_type)
     attended_grad = back_product(proj_rows, proj_weight).astype(BF16)
-    qkv_rows = attend_back(qkv, doc_ids, attended_grad, totals)
-    qkv_grad = weight_grad(tokens, qkv_rows, grad_type)
-    qkv_sums = by_kind(column_sums(qkv_rows)[None])[0]
+    riders = [g.reshape(*shape, -1, g.shape[1]) for g in (down_grad, up_grad)] if depth else []
+    qkv_rows, qkv_grad, qkv_sums, *summed = attend_back(
+        tokens, qkv, doc_ids, attended_grad, totals, grad_type, riders, depth, 3
+    )
     input_grad = (back_product(qkv_rows, qkv_weight) + hidden_grad).astype(BF16)
+    qkv_sums = by_kind(qkv_sums.reshape(1, -1))[0]
     vector_grad = jnp.concatenate(
         [
             qkv_sums[0:D],
@@ -617,7 +761,21 @@
             shift_second_grad,
         ]
     )
-    return output, input_grad, (qkv_grad, proj_grad, up_grad, down_grad, vector_grad)
+    if depth:
+        padded = jnp.pad(vector_grad.reshape(devices, rows, LANES), ((0, 0), (0, 16 - rows), (0, 0)))
+        last = [g.reshape(*shape, -1, g.shape[1]) for g in (qkv_grad, proj_grad)]
+        owned = scatter([*last, padded.reshape(*shape, 16, LANES)], depth, 4)
+        owned = [owned[0], owned[1], summed[1], summed[0], owned[2][:rows]]
+    else:
+        grads = (qkv_grad, proj_grad, up_grad, down_grad, vector_grad[:, None])
+        owned = [
+            lax.psum_scatter(
+                grad.reshape(devices, -1, grad.shape[-1]), "dp", scatter_dimension=0, tiled=True
+            )[0]
+            for grad in grads
+        ]
+    owned[0] = by_kind(owned[0])
+    return output, input_grad, [own.reshape(-1) for own in owned]
 
 
 def adam_update(master, moment_one, moment_two, grad, rate):
@@ -632,46 +790,19 @@
 WIDTHS = (3 * D, D, FF, D)
 
 
-def gather_weights(masters, devices, depth):
+def lowered_blocks(masters):
     lowered = [master.astype(BF16) for master in masters]
     blocks = [low.reshape(-1, width) for low, width in zip(lowered, WIDTHS)]
     blocks[0] = by_pair(blocks[0])
-    if not depth:
-        flat = [lax.all_gather(block, "dp", axis=0, tiled=True) for block in blocks]
-        return (*flat, lax.all_gather(lowered[4], "dp", axis=0, tiled=True))
-    rows = lowered[4].shape[0] // LANES
-    vector = jnp.pad(lowered[4].reshape(rows, LANES), ((0, 32 - rows), (0, 0)))
-    full = gather([vector, *blocks], depth, 1)
-    matrices = [whole.reshape(-1, width) for whole, width in zip(full[1:], WIDTHS)]
-    return (*matrices, full[0].reshape(devices, 32, LANES)[:, :rows].reshape(-1))
-
-
-def scatter_grads(grads, devices, depth):
-    if not depth:
-        owned = [
-            lax.psum_scatter(
-                grad.reshape(devices, -1, grad.shape[-1]), "dp", scatter_dimension=0, tiled=True
-            )[0]
-            for grad in (*grads[:4], grads[4][None].reshape(-1, 1))
-        ]
-    else:
-        rows = grads[4].shape[0] // devices // LANES
-        vector = jnp.pad(grads[4].reshape(devices, rows, LANES), ((0, 0), (0, 16 - rows), (0, 0)))
-        shape = (depth, 2, 2, 2)
-        blocks = [grad.reshape(*shape, -1, grad.shape[-1]) for grad in grads[:4]]
-        owned = scatter([*reversed(blocks), vector.reshape(*shape, 16, LANES)], depth, 2)
-        owned = [*reversed(owned[:4]), owned[4][:rows]]
-    owned[0] = by_kind(owned[0])
-    return [own.reshape(-1) for own in owned]
+    return blocks, lowered[4]
 
 
 def body(depth, tokens, segment_ids, out_grad, *states):
     devices = lax.axis_size("dp")
     masters = states[0::3]
-    weights = gather_weights(masters, devices, depth)
-    grad_type = BF16 if depth else F32
-    output, input_grad, grads = layer_step(tokens, segment_ids, out_grad, weights, grad_type)
-    owned = scatter_grads(grads, devices, depth)
+    output, input_grad, owned = layer_step(
+        tokens, segment_ids, out_grad, masters, devices, depth
+    )
     outs = [output, input_grad]
     for i in range(5):
         outs += adam_update(*states[3 * i : 3 * i + 3], owned[i], RATES[i])

time: 540 us -> 484 us (0.90)
  Pallas kernels: 328 us -> 301 us
  matrix products: 146 us -> 125 us
    pallas_call x2, Pallas kernels: 68.3 us -> 196 us  [the longest x1 107 us: attend(): pl.pallas_call(functools.partial(attend_kernel, depth, len(blocks), PAIRS...]
    pallas_call x1, Pallas kernels: 124 us -> 43.7 us  [gather(): pl.pallas_call(functools.partial(gather_kernel, depth, count), in_specs=[...]
    pallas_call x1, Pallas kernels: 136 us -> 61.6 us  [scatter(): pl.pallas_call(functools.partial(scatter_kernel, depth, count), in_specs=...]
    dot_general x4 -> x3, matrix products: 50.7 us -> 39.5 us  [times(): return jnp.dot(rows, matrix, preferred_element_type=F32)]
    dot_general x8 -> x7, matrix products: 95.3 us -> 85.3 us  [dot_over(): lax.dot_general(left, right, (((left_dim,), (right_dim,)), ((), ())), pre...]
    reduce_sum x4 -> x3, other arithmetic: 12.3 us -> 8.38 us  [column_sums(): return jnp.sum(rows.astype(F32), axis=0)]
    unnamed x83 -> x79, local copies, waits for them, and re-layouts: 17.6 us -> 15.2 us
where the time goes in v2:
time: 484 us; the launch traced here: 477 us
  Pallas kernels  301 us (62%)
  matrix products  125 us (26%)
  other arithmetic  25.2 us (5%)
  local copies, waits for them, and re-layouts  24 us (5%)
    pallas_call x1, Pallas kernels, attend(): pl.pallas_call(functools.partial(attend_kernel, depth, len(blocks), PAIRS...  107 us
    pallas_call x1, Pallas kernels, attend_back(): pl.pallas_call(functools.partial(attend_back_kernel, depth, len(grads), P...  89 us
    dot_general x7, matrix products, dot_over(): lax.dot_general(left, right, (((left_dim,), (right_dim,)), ((), ())), pre...  85.3 us
    pallas_call x1, Pallas kernels, scatter(): pl.pallas_call(functools.partial(scatter_kernel, depth, count), in_specs=...  61.6 us
    pallas_call x1, Pallas kernels, gather(): pl.pallas_call(functools.partial(gather_kernel, depth, count), in_specs=[...  43.7 us
    dot_general x3, matrix products, times(): return jnp.dot(rows, matrix, preferred_element_type=F32)  39.5 us
    unnamed x79, local copies, waits for them, and re-layouts  15.2 us
    convert_element_type x5, other arithmetic, adam_update(): return (grad, one_new, two_new, master_new, master_new.astype(BF16))  10.2 us

profile of v2, /device:TPU:0, one launch (start us, length us, event | category | flops | bytes accessed | tf_op | source)
XLA Modules:
  0.0 477.0 jit_solution(9288093481326284835)
XLA Ops:
  0.7 0.0 copy-start.20
  0.7 0.7 convert_bitcast_fusion
  1.4 1.3 reshape.177.refs_0_
  2.7 0.6 pad.8.refs_0_
  3.3 0.9 convert_element_type.93
  4.2 0.7 reshape.183.refs_5_
  4.8 1.0 convert_element_type.90
  5.8 0.0 copy-start
  5.9 0.1 copy.53
  6.0 0.8 reshape.180.refs_1_
  6.8 1.1 convert_element_type.94
  7.9 0.8 reshape.184.refs_6_
  8.7 1.1 convert_element_type.95
  9.8 0.8 reshape.185.refs_7_
  10.6 1.0 copy.54.refs_1_
  11.6 3.9 copy.57
  15.6 2.5 copy.52
  18.1 43.7 %gather.1 = (bf16[4,2,2,2,32,128]{5,4,3,2,1,0:T(8,128)(2,1)}, bf16[4,2,2,2,32,3072]{5,4,3,2,1,0:T(8,128)(2,1)}) custom-call(bf16[32,128]{1,0:T(8,128)(2,1)} %pad.8.refs_0_, bf16[32,3072]{1,0:T(8,128)(2,1)} %reshape.180.refs_1_), custom_call_target="tpu_custom_call" | custom-call | tf_op jit(solution)/shard_map/gather/pallas_call | solution.py:229
  61.8 0.8 slice_convert_fusion
  62.7 0.6 copy.55.refs_4_
  63.3 107.1 %attend.1 = (bf16[1024,3072]{1,0:T(8,128)(2,1)}, bf16[1024,1024]{1,0:T(8,128)(2,1)}, f32[2,8,2,512]{3,2,1,0:T(2,128)}, bf16[4,2,2,2,32,1024]{5,4,3,2,1,0:T(8,128...) custom-call(s32[2,1,512]{2,1,0:T(1,128)} %reshape.177.refs_0_, ...), custom_call_target="tpu_custom_call" | custom-call | tf_op jit(solution)/shard_map/attend/pallas_call | solution.py:578
  170.4 4.8 %fusion.39 = (f32[1024]{0:T(1024)S(1)}, f32[1024,1024]{0,1:T(8,128)S(1)}) fusion(f32[1024]{0:T(1024)S(1)} %get-tuple-element.152, bf16[1024,1024]{1,0:T(8,128)(2,1)} %get-tuple-element.45, bf16[1024,1024]{1,0:T(8,128)(2,1)} %bitcast.92, bf16[1024,1024]{0,1:T(8,128)(2,1)S(1)} %copy-done.10), kind=kOutput, calls=%fused_computation.95 | convolution fusion | flops 2151676928 | bytes 10493952 | tf_op jit(solution)/shard_map/dot_general | solution.py:672
  175.3 0.5 multiply_reduce_fusion.3
  175.8 19.8 %multiply_convert_fusion = (bf16[1024,4096]{1,0:T(8,128)(2,1)}, f32[1024,4096]{1,0:T(8,128)}) fusion(f32[4096]{0:T(1024)S(1)} %slice.66, bf16[1024,4096]{1,0:T(8,128)(2,1)} %bitcast.86, f32[1024,1024]{0,1:T(8,128)S(1)} %get-tuple-element.156, f32[1024]{0:T(1024)S(1)} %get-tuple-element.150, f32[1024]{0:T(1024)S(1)} %get-tuple-element.151, ...), kind=kOutput, calls=%fused_computation.8 | convolution fusion | flops 8620343296 | bytes 37781504 | tf_op jit(solution)/shard_map/dot_general | solution.py:672
  195.5 14.9 %fusion.40 = (f32[1024]{0:T(1024)S(1)}, f32[1024,1024]{0,1:T(8,128)S(1)}) fusion(f32[1024]{0:T(1024)S(1)} %get-tuple-element.149, bf16[1024,4096]{1,0:T(8,128)(2,1)} %get-tuple-element.157, bf16[4096,1024]{1,0:T(8,128)(2,1)} %bitcast.88, f32[1024]{0:T(1024)S(1)} %get-tuple-element.150, f32[1024]{0:T(1024)S(1)} %get-tuple-element.151, ...), kind=kOutput, calls=%fused_computation.96 | convolution fusion | flops 8597273600 | bytes 25190400 | tf_op jit(solution)/shard_map/dot_general | solution.py:672
  210.4 0.0 copy-start.1
  210.4 0.5 multiply_reduce_fusion.2
  210.9 1.1 copy-done.1
  212.0 3.3 fusion.12
  215.3 3.7 convert_reduce_fusion.2
  219.0 18.7 %convert_reduce_fusion = (f32[4096]{0:T(1024)S(1)}, bf16[1024,4096]{1,0:T(8,128)(2,1)}) fusion(f32[1024,4096]{1,0:T(8,128)} %get-tuple-element.158, f32[4096]{0:T(1024)S(1)} %slice.66, bf16[1024,1024]{0,1:T(8,128)(2,1)S(1)} %get-tuple-element.143, bf16[4096,1024]{1,0:T(8,128)(2,1)S(1)} %bitcast.91), kind=kOutput, calls=%fused_computation.7 | convolution fusion | flops 8644456448 | bytes 35684352 | tf_op jit(solution)/shard_map/dot_general | solution.py:35
  237.7 16.1 %multiply_reduce_fusion = (f32[1024]{0:T(1024)S(1)}, f32[1024]{0:T(1024)S(1)}, f32[1024]{0:T(1024)S(1)}, f32[1024]{0:T(1024)S(1)}, f32[1024,1024]{0,1:T(8,128)S(1)}) fusion(f32[1024,1024]{0,1:T(8,128)S(1)} %copy-done.3, f32[1024]{0:T(1024)S(1)} %add_rsqrt_fusion.1, f32[1024]{0:T(1024)S(1)} %broadcast_multiply_fusion.5, f32[1024]{0:T(1024)S(1)} %get-tuple-element.151, ...), kind=kOutput, calls=%fused_computation.23 | convolution fusion | flops 8608804864 | bytes 31506432 | tf_op jit(solution)/shard_map/dot_general | solution.py:35
  253.8 14.8 %convolution_convert_fusion.1 = bf16[4096,1024]{1,0:T(8,128)(2,1)} fusion(bf16[1024,4096]{1,0:T(8,128)(2,1)} %get-tuple-element.157, bf16[1024,1024]{0,1:T(8,128)(2,1)S(1)} %get-tuple-element.143), kind=kOutput, calls=%fused_computation.11 | convolution fusion | flops 8594128896 | bytes 18874368 | tf_op jit(solution)/shard_map/dot_general | solution.py:35
  268.7 1.4 convert_reduce_fusion.3
  270.1 16.6 %convolution_convert_fusion = bf16[1024,4096]{1,0:T(8,128)(2,1)} fusion(bf16[1024,4096]{1,0:T(8,128)(2,1)} %get-tuple-element.163, f32[1024,1024]{0,1:T(8,128)S(1)} %copy-done.3, f32[1024]{0:T(1024)S(1)} %get-tuple-element.150, f32[1024]{0:T(1024)S(1)} %get-tuple-element.151, f32[1024]{0:T(1024)S(1)} %add_rsqrt_fusion.1, f32[1024]{0:T(1024)S(1)} %broadcast_multiply_fusion.5), kind=kOutput, calls=%fused_computation.10 | convolution fusion | flops 8599371776 | bytes 20987904 | tf_op jit(solution)/shard_map/dot_general | solution.py:35
  286.7 3.7 convolution_convert_fusion.2
  290.5 3.7 convolution_convert_fusion.3.refs_4_
  294.2 89.0 %attend_back.1 = (bf16[1024,3072]{1,0:T(8,128)(2,1)}, bf16[1024,3072]{1,0:T(8,128)(2,1)}, f32[8,1,384]{2,1,0:T(1,128)}, f32[128,1024]{1,0:T(8,128)}, f32[32,4096]{1,0:T(8,128)}) custom-call(s32[2,1,512]{2,1,0:T(1,128)} %reshape.177.refs_0_, s32[2,512,1]{2,1,0:T(8,128)} %copy.54.refs_1_, bf16[1024,1024]{1,0:T(8,128)(2,1)} %refs_2_.3, ...), custom_call_target="tpu_custom_call" | custom-call | tf_op jit(solution)/shard_map/attend_back/pallas_call | solution.py:608
  383.2 11.6 %add_convert_fusion = bf16[1024,1024]{0,1:T(8,128)(2,1)S(1)} fusion(f32[1024,1024]{0,1:T(8,128)} %copy-done.5, bf16[1024,3072]{1,0:T(8,128)(2,1)} %get-tuple-element.51, bf16[1024,3072]{1,0:T(8,128)(2,1)} %bitcast.65), kind=kOutput, calls=%fused_computation.25 | convolution fusion | flops 6444548096 | bytes 18874368 | tf_op jit(solution)/shard_map/dot_general | solution.py:35
  394.8 0.0 copy-start.21
  394.8 0.0 copy-start.23
  394.8 0.0 copy-start.22
  394.9 2.6 copy.64
  397.6 0.7 pad.9
  398.3 61.6 %scatter.1 = (f32[32,3072]{1,0:T(8,128)}, f32[32,1024]{1,0:T(8,128)}, f32[16,128]{1,0:T(8,128)}) custom-call(bf16[4,2,2,2,32,3072]{5,4,3,2,1,0:T(8,128)(2,1)} %bitcast.66, bf16[4,2,2,2,32,1024]{5,4,3,2,1,0:T(8,128)(2,1)} %bitcast.72, f32[4,2,2,2,16,128]{5,4,3,2,1,0:T(8,128)} %bitcast.75), custom_call_target="tpu_custom_call" | custom-call | tf_op jit(solution)/shard_map/scatter/pallas_call | solution.py:398
  459.9 0.0 copy-start.12
  459.9 0.0 copy-start.19
  459.9 0.0 copy-start.13
  459.9 1.1 copy.68
  461.0 0.0 copy-start.17
  461.1 1.3 fusion.27
  462.4 1.3 reshape.195
  463.7 0.0 copy-start.11
  463.7 1.9 fusion.33
  465.6 1.1 copy.69
  466.8 0.0 copy-start.8
  466.8 0.0 copy-start.7
  466.8 0.0 copy-start.14
  466.8 0.1 copy.70
  466.9 0.0 copy-start.9
  467.0 2.7 fusion.35
  469.7 2.7 fusion.29
  472.4 1.5 fusion.31
  474.0 2.6 copy.63
  (73 shorter events, 0.3 us)
Async XLA Ops:
  0.7 9.9 %copy-start.20 = (s32[2,512]{1,0:T(2,128)S(1)}, s32[2,512]{1,0:T(2,128)}, u32[]{:S(2)}) copy-start(s32[2,512]{1,0:T(2,128)} %param.19) | copy-start | bytes 12292
  5.8 9.7 %copy-start = (bf16[1024,1024]{1,0:T(8,128)(2,1)S(1)}, bf16[1024,1024]{1,0:T(8,128)(2,1)}, u32[]{:S(2)}) copy-start(bf16[1024,1024]{1,0:T(8,128)(2,1)} %refs_2_.3) | copy-start | bytes 6291460
  63.3 107.1 %copy-start.10 = (bf16[1024,1024]{0,1:T(8,128)(2,1)S(1)}, bf16[1024,1024]{0,1:T(8,128)(2,1)}, u32[]{:S(2)}) copy-start(bf16[1024,1024]{0,1:T(8,128)(2,1)} %copy.52) | copy-start | bytes 6291460
  175.2 20.3 %copy-start.2 = (f32[1024,1024]{0,1:T(8,128)}, f32[1024,1024]{0,1:T(8,128)S(1)}, u32[]{:S(2)}) copy-start(f32[1024,1024]{0,1:T(8,128)S(1)} %get-tuple-element.156) | copy-start | bytes 12582916
  210.4 1.6 copy-start.1
  212.0 7.0 %slice-start = ((s8[8388608]{0:T(1024)(128)(4,1)}), s8[4194304]{0:T(1024)(128)(4,1)S(1)}, s32[]{:S(2)}) async-start(s8[8388608]{0:T(1024)(128)(4,1)} %bitcast.89), calls=%async_computation | async-start | bytes 8388608
  215.3 3.7 slice-start.1
  219.0 18.7 %copy-start.3 = (f32[1024,1024]{0,1:T(8,128)S(1)}, f32[1024,1024]{0,1:T(8,128)}, u32[]{:S(2)}) copy-start(f32[1024,1024]{0,1:T(8,128)} %copy-done.2) | copy-start | bytes 12582916
  270.1 20.4 %copy-start.5 = (f32[1024,1024]{0,1:T(8,128)}, f32[1024,1024]{0,1:T(8,128)S(1)}, u32[]{:S(2)}) copy-start(f32[1024,1024]{0,1:T(8,128)S(1)} %get-tuple-element.145) | copy-start | bytes 12582916
  270.1 16.6 %copy-start.29 = (bf16[1024,1024]{1,0:T(8,128)(2,1)S(1)}, bf16[1024,1024]{1,0:T(8,128)(2,1)}, u32[]{:S(2)}) copy-start(bf16[1024,1024]{1,0:T(8,128)(2,1)} %get-tuple-element.45) | copy-start | bytes 6291460
  286.7 3.7 copy-start.28
  394.8 2.6 copy-start.24
  394.8 2.7 copy-start.21
  394.8 2.7 copy-start.23
  394.8 2.7 copy-start.22
  398.3 62.7 %copy-start.25 = (f32[384]{0:T(512)S(1)}, f32[384]{0:T(512)}, u32[]{:S(2)}) copy-start(f32[384]{0:T(512)} %param.33) | copy-start | bytes 4612
  398.3 62.7 %copy-start.26 = (f32[384]{0:T(512)S(1)}, f32[384]{0:T(512)}, u32[]{:S(2)}) copy-start(f32[384]{0:T(512)} %param.35) | copy-start | bytes 4612
  398.3 62.8 %copy-start.27 = (f32[384]{0:T(512)S(1)}, f32[384]{0:T(512)}, u32[]{:S(2)}) copy-start(f32[384]{0:T(512)} %param.34) | copy-start | bytes 4612
  398.3 65.4 %copy-start.16 = (f32[32768]{0:T(1024)S(1)}, f32[32768]{0:T(1024)}, u32[]{:S(2)}) copy-start(f32[32768]{0:T(1024)} %param.24) | copy-start | bytes 393220
  459.9 7.0 %copy-start.18 = (f32[128,1024]{1,0:T(8,128)S(1)}, f32[128,1024]{1,0:T(8,128)}, u32[]{:S(2)}) copy-start(f32[128,1024]{1,0:T(8,128)} %get-tuple-element.57) | copy-start | bytes 1572868
  459.9 7.1 %copy-start.12 = (f32[98304]{0:T(1024)S(1)}, f32[98304]{0:T(1024)}, u32[]{:S(2)}) copy-start(f32[98304]{0:T(1024)} %param.21) | copy-start | bytes 1179652
  459.9 7.1 %copy-start.19 = (f32[98304]{0:T(1024)S(1)}, f32[98304]{0:T(1024)}, u32[]{:S(2)}) copy-start(f32[98304]{0:T(1024)} %param.23) | copy-start | bytes 1179652
  459.9 9.8 %copy-start.6 = (f32[131072]{0:T(1024)S(1)}, f32[131072]{0:T(1024)}, u32[]{:S(2)}) copy-start(f32[131072]{0:T(1024)} %param.30) | copy-start | bytes 1572868
  459.9 9.8 %copy-start.13 = (f32[131072]{0:T(1024)S(1)}, f32[131072]{0:T(1024)}, u32[]{:S(2)}) copy-start(f32[131072]{0:T(1024)} %param.32) | copy-start | bytes 1572868
  461.0 5.9 %copy-start.17 = (f32[4,8,8,128]{3,1,2,0:T(8,128)}, f32[4,8,8,128]{3,1,2,0:T(8,128)S(1)}, u32[]{:S(2)}) copy-start(f32[4,8,8,128]{3,1,2,0:T(8,128)S(1)} %copy.68) | copy-start | bytes 393220
  463.7 8.7 %copy-start.11 = (f32[32,3,8,128]{3,2,1,0:T(8,128)}, f32[32,3,8,128]{3,2,1,0:T(8,128)S(1)}, u32[]{:S(2)}) copy-start(f32[32,3,8,128]{3,2,1,0:T(8,128)S(1)} %copy.62) | copy-start | bytes 1179652
  466.8 7.2 %copy-start.8 = (f32[4,32,8,128]{3,1,2,0:T(8,128)}, f32[4,32,8,128]{3,1,2,0:T(8,128)S(1)}, u32[]{:S(2)}) copy-start(f32[4,32,8,128]{3,1,2,0:T(8,128)S(1)} %copy.69) | copy-start | bytes 1572868
  466.8 5.6 %copy-start.7 = (f32[131072]{0:T(1024)S(1)}, f32[131072]{0:T(1024)}, u32[]{:S(2)}) copy-start(f32[131072]{0:T(1024)} %param.27) | copy-start | bytes 1572868
  466.8 5.6 %copy-start.14 = (f32[131072]{0:T(1024)S(1)}, f32[131072]{0:T(1024)}, u32[]{:S(2)}) copy-start(f32[131072]{0:T(1024)} %param.29) | copy-start | bytes 1572868
  466.8 5.6 %copy-start.15 = (f32[131072]{0:T(1024)S(1)}, f32[131072]{0:T(1024)}, u32[]{:S(2)}) copy-start(f32[131072]{0:T(1024)} %param.28) | copy-start | bytes 1572868
  466.9 7.0 %copy-start.9 = (f32[16,8,8,128]{3,1,2,0:T(8,128)}, f32[16,8,8,128]{3,1,2,0:T(8,128)S(1)}, u32[]{:S(2)}) copy-start(f32[16,8,8,128]{3,1,2,0:T(8,128)S(1)} %copy.70) | copy-start | bytes 1572868
  469.7 4.2 copy-start.4

commit v3 on v2

v3 whole, which is shorter than its diff:
```python
import functools

import jax
import jax.numpy as jnp
from jax import lax
from jax.experimental import pallas as pl
from jax.experimental.pallas import tpu as pltpu
from jax.sharding import PartitionSpec as P

D = 1024
HEADS = 16
HEAD_DIM = 64
FF = 4096
STEP = 3
LANES = 128
PAIRS = HEADS * HEAD_DIM // LANES

NORM_EPS = 1e-05
BETA_FIRST = 0.5
BETA_SECOND = 0.5
ADAM_EPS = 1e-08
WEIGHT_DECAY = 0.01
MASK_FILL = -1000000000.0
RATES = (0.01, 0.03, 0.01, 0.005, 0.05)
SCALE = HEAD_DIM ** (-0.5)
HALF_ROOT = 0.7071067811865476
PDF_TOP = 0.3989422804014327

F32 = jnp.float32
BF16 = jnp.bfloat16
MESH = pl.DeviceIdType.MESH


def dot_over(left, right, left_dim, right_dim):
    return lax.dot_general(
        left, right, (((left_dim,), (right_dim,)), ((), ())), preferred_element_type=F32
    )


def depth_of(mesh):
    devices = list(mesh.devices.flat)
    if len(devices) % 8:
        return 0
    try:
        spots = [(*d.coords, d.core_on_chip) for d in devices]
    except AttributeError:
        return 0
    low = [min(s[i] for s in spots) for i in range(4)]
    depth = len(devices) // 8
    for index, (x, y, z, core) in enumerate(spots):
        spot = (((z - low[2]) * 2 + y - low[1]) * 2 + x - low[0]) * 2 + core - low[3]
        if spot != index:
            return 0
    return depth


class Place:
    def __init__(self, depth):
        me = lax.axis_index("dp")
        self.depth = depth
        self.core = me % 2
        self.x = (me // 2) % 2
        self.y = (me // 4) % 2
        self.z = me // 8

    def index(self, z, y, x, core):
        return ((z * 2 + y) * 2 + x) * 2 + core

    def ahead(self, k):
        return (self.z + k) % self.depth

    def back(self, k):
        return (self.z + self.depth - k) % self.depth

    def twin(self):
        return self.index(self.z, self.y, self.x, 1 - self.core)

    def x_mate(self):
        return self.index(self.z, self.y, 1 - self.x, self.core)

    def y_mate(self):
        return self.index(self.z, 1 - self.y, self.x, self.core)

    def z_mate(self, k):
        return self.index(self.ahead(k), self.y, self.x, self.core)

    def greet(self):
        barrier = pltpu.get_barrier_semaphore()
        mates = [self.twin(), self.x_mate(), self.y_mate()]
        mates += [self.z_mate(k) for k in range(1, self.depth)]
        for mate in mates:
            pl.semaphore_signal(barrier, inc=1, device_id=(mate,), device_id_type=MESH)
        pl.semaphore_wait(barrier, len(mates))


def send(source, target, send_sem, recv_sem, device):
    return pltpu.make_async_remote_copy(
        src_ref=source,
        dst_ref=target,
        send_sem=send_sem,
        recv_sem=recv_sem,
        device_id=(device,),
        device_id_type=MESH,
    )


class Gather:
    BY_Z, BY_X, BY_Y, UPPER, LOWER, OWN, FROM_X, FROM_Y, CROSS = range(9)

    def __init__(self, place, blocks, full, send_sems, recv_sems, local_sems):
        self.place = place
        self.blocks = blocks
        self.full = full
        self.sems = (send_sems, recv_sems)
        self.local_sems = local_sems
        self.depth = place.depth

    def home(self, w):
        p = self.place
        return self.full[w].at[p.z, p.y, p.x, p.core]

    def copy(self, w, k, kind):
        p, full = self.place, self.full[w]
        half = self.blocks[w].shape[0] // 2
        sems = [sem.at[w, k, kind] for sem in self.sems]
        zz = p.back(k)
        if kind == self.BY_Z:
            return send(self.blocks[w], self.home(w), *sems, p.z_mate(k))
        if kind in (self.BY_X, self.BY_Y, self.OWN):
            block = full.at[zz, p.y, p.x, p.core]
            source = self.blocks[w] if k == 0 else block
            mate = {self.BY_X: p.x_mate, self.BY_Y: p.y_mate, self.OWN: p.twin}[kind]()
            return send(source, block, *sems, mate)
        if kind == self.UPPER:
            block = full.at[zz, p.y, 1 - p.x, p.core, pl.ds(0, half)]
            return send(block, block, *sems, p.y_mate())
        if kind == self.LOWER:
            block = full.at[zz, 1 - p.y, p.x, p.core, pl.ds(half, half)]
            return send(block, block, *sems, p.x_mate())
        if kind == self.FROM_X:
            block = full.at[zz, p.y, 1 - p.x, p.core]
        elif kind == self.FROM_Y:
            block = full.at[zz, 1 - p.y, p.x, p.core]
        else:
            block = full.at[zz, 1 - p.y, 1 - p.x, p.core]
        return send(block, block, *sems, p.twin())

    def local(self, w):
        return pltpu.make_async_copy(self.blocks[w], self.home(w), self.local_sems.at[w])

    def start(self, w):
        for k in range(1, self.depth):
            self.copy(w, k, self.BY_Z).start()
        self.local(w).start()

    def spread(self, w, k):
        if k:
            self.copy(w, k, self.BY_Z).wait_recv()
        for kind in (self.BY_X, self.BY_Y, self.OWN):
            self.copy(w, k, kind).start()

    def relay(self, w, k):
        self.copy(w, k, self.BY_X).wait_recv()
        self.copy(w, k, self.UPPER).start()
        self.copy(w, k, self.FROM_X).start()
        self.copy(w, k, self.BY_Y).wait_recv()
        self.copy(w, k, self.LOWER).start()
        self.copy(w, k, self.FROM_Y).start()

    def hand_over(self, w, k):
        self.copy(w, k, self.UPPER).wait_recv()
        self.copy(w, k, self.LOWER).wait_recv()
        self.copy(w, k, self.CROSS).start()

    def receive(self, w, k):
        if k == 0:
            self.local(w).wait()
        for kind in (self.OWN, self.FROM_X, self.FROM_Y, self.CROSS):
            self.copy(w, k, kind).wait_recv()

    def receive_all(self, w):
        for k in range(self.depth):
            self.receive(w, k)

    def sent(self, w):
        for k in range(self.depth):
            for kind in range(9):
                if kind != self.BY_Z or k:
                    self.copy(w, k, kind).wait_send()

    def sent_all(self):
        for w in range(len(self.blocks)):
            self.sent(w)

    def step(self, units, t):
        lag = self.depth
        if t < len(units):
            self.spread(*units[t])
        if 0 <= t - lag < len(units):
            self.relay(*units[t - lag])
        if 0 <= t - 2 * lag < len(units):
            self.hand_over(*units[t - 2 * lag])

    def units(self):
        return [(w, k) for w in range(len(self.blocks)) for k in range(self.depth)]

    def start_all(self):
        for w in range(len(self.blocks)):
            self.start(w)

def gather_sems(count, depth):
    return [
        pltpu.SemaphoreType.DMA((count, depth, 9)),
        pltpu.SemaphoreType.DMA((count, depth, 9)),
        pltpu.SemaphoreType.DMA((count,)),
    ]


class Scatter:
    TWIN, UPPER_Y, LOWER_X, UPPER_X, LOWER_Y, BY_Z = range(6)

    def __init__(self, place, grads, out, bufs, send_sems, recv_sems, local_sems, resident=()):
        self.place = place
        self.resident = resident
        self.grads = grads
        self.out = out
        self.bufs = bufs
        self.sems = (send_sems, recv_sems)
        self.local_sems = local_sems
        self.depth = place.depth
        self.order = list(range(1, self.depth)) + [0]

    def load(self, w, k):
        p = self.place
        return pltpu.make_async_copy(
            self.grads[w].at[p.ahead(k), :, :, p.core],
            self.bufs[w][6].at[k],
            self.local_sems.at[w, k],
        )

    def sums(self, w, k):
        if w in self.resident:
            return self.grads[w].at[self.place.ahead(k), :, :, self.place.core]
        return self.bufs[w][6].at[k]

    def half(self, w):
        return self.grads[w].shape[-2] // 2

    def copy(self, w, k, kind):
        p = self.place
        twin, upper_y, lower_x, upper_x, lower_y, by_z = self.bufs[w][:6]
        sums, half = self.sums(w, k), self.half(w)
        sems = [sem.at[w, k, kind] for sem in self.sems]
        top, bottom = pl.ds(0, half), pl.ds(half, half)
        if kind == self.TWIN:
            source = self.grads[w].at[p.ahead(k), :, :, 1 - p.core]
            return send(source, twin.at[k], *sems, p.twin())
        if kind == self.UPPER_Y:
            return send(sums.at[1 - p.y, :, top], upper_y.at[k], *sems, p.y_mate())
        if kind == self.LOWER_X:
            return send(sums.at[:, 1 - p.x, bottom], lower_x.at[k], *sems, p.x_mate())
        if kind == self.UPPER_X:
            return send(sums.at[p.y, 1 - p.x, top], upper_x.at[k], *sems, p.x_mate())
        if kind == self.LOWER_Y:
            return send(sums.at[1 - p.y, p.x, bottom], lower_y.at[k], *sems, p.y_mate())
        return send(sums.at[p.y, p.x], by_z.at[k], *sems, p.z_mate(k))

    @staticmethod
    def add(target, extra):
        total = target[...].astype(F32) + extra[...].astype(F32)
        target[...] = total.astype(target.dtype)

    def start(self, w):
        for k in self.order:
            self.begin(w, k)

    def begin(self, w, k):
        self.copy(w, k, self.TWIN).start()
        if w not in self.resident:
            self.load(w, k).start()

    def first(self, w, k):
        sums, twin = self.sums(w, k), self.bufs[w][0]
        if w not in self.resident:
            self.load(w, k).wait()
        self.copy(w, k, self.TWIN).wait_recv()

        def body(i, carry):
            self.add(sums.at[i // 2, i % 2], twin.at[k, i // 2, i % 2])
            return carry

        lax.fori_loop(0, 4, body, 0)
        self.copy(w, k, self.UPPER_Y).start()
        self.copy(w, k, self.LOWER_X).start()

    def second(self, w, k):
        p = self.place
        sums, half = self.sums(w, k), self.half(w)
        upper_y, lower_x = self.bufs[w][1:3]
        self.copy(w, k, self.UPPER_Y).wait_recv()
        self.copy(w, k, self.LOWER_X).wait_recv()

        def body(i, carry):
            self.add(sums.at[p.y, i, pl.ds(0, half)], upper_y.at[k, i])
            self.add(sums.at[i, p.x, pl.ds(half, half)], lower_x.at[k, i])
            return carry

        lax.fori_loop(0, 2, body, 0)
        self.copy(w, k, self.UPPER_X).start()
        self.copy(w, k, self.LOWER_Y).start()

    def third(self, w, k):
        p = self.place
        sums, half = self.sums(w, k), self.half(w)
        upper_x, lower_y = self.bufs[w][3:5]
        self.copy(w, k, self.UPPER_X).wait_recv()
        self.copy(w, k, self.LOWER_Y).wait_recv()
        self.add(sums.at[p.y, p.x, pl.ds(0, half)], upper_x.at[k])
        self.add(sums.at[p.y, p.x, pl.ds(half, half)], lower_y.at[k])
        if isinstance(k, int):
            if k:
                self.copy(w, k, self.BY_Z).start()
        else:
            pl.when(k != 0)(lambda: self.copy(w, k, self.BY_Z).start())

    def finish(self, w):
        p = self.place
        by_z = self.bufs[w][5]
        for k in range(1, self.depth):
            self.copy(w, k, self.BY_Z).wait_recv()
        total = self.sums(w, 0)[p.y, p.x].astype(F32)
        for k in range(1, self.depth):
            total = total + by_z[k].astype(F32)
        self.out[w][...] = total
        for k in range(self.depth):
            for kind in range(6):
                if kind != self.BY_Z or k:
                    self.copy(w, k, kind).wait_send()


BUFS = 7


def scatter_scratch(grads, depth, resident=()):
    scratch = []
    for w, grad in enumerate(grads):
        rows, columns = grad.shape[-2:]
        half = rows // 2
        shapes = [(depth, 2, 2, rows, columns)]
        shapes += [(depth, 2, half, columns)] * 2 + [(depth, half, columns)] * 2
        shapes += [(depth, rows, columns)]
        shapes += [(8, LANES) if w in resident else (depth, 2, 2, rows, columns)]
        scratch += [pltpu.VMEM(shape, grad.dtype) for shape in shapes]
    count = len(grads)
    scratch += [pltpu.SemaphoreType.DMA((count, depth, 6))] * 2
    return scratch + [pltpu.SemaphoreType.DMA((count, depth))]


def own_lanes(head):
    lane = lax.broadcasted_iota(jnp.int32, (1, LANES), 1)
    return (lane < HEAD_DIM) == (head == 0)


def fill_masks(ids_row, ids_column, masks):
    for b in range(masks.shape[0]):
        masks[b] = jnp.where(ids_column[b] == ids_row[b], 0.0, MASK_FILL).astype(F32)


def at_step(t, work):
    pl.when(pl.program_id(0) * pl.num_programs(1) + pl.program_id(1) == t)(work)


GROUPS = 4
GROUP_PAIRS = PAIRS // GROUPS
GROUP_WIDTH = 3 * LANES * GROUP_PAIRS


def rows_of(block):
    return block.reshape(-1, block.shape[-1])


def qkv_rows_of(rows, weight, h):
    columns = pl.ds(pl.multiple_of((h % GROUP_PAIRS) * 3 * LANES, 3 * LANES), 3 * LANES)
    if len(weight.shape) == 2:
        return dot_over(rows, weight[:, columns], 1, 0)
    return dot_over(rows, rows_of(weight[:, :, :, :, :, columns]), 1, 0)


def attend_kernel(depth, count, seqs, per, *refs):
    ids_row, ids_column, tokens = refs[:3]
    if depth:
        blocks, refs = refs[3 : 3 + count], refs[3 + count :]
        qkv, attended, log_total, whole_qkv, whole_vector = refs[:5]
        riders, refs = refs[5 : 5 + count - GROUPS], refs[5 + count - GROUPS :]
        masks, bias, groups, refs = refs[0], refs[1], refs[2 : 2 + GROUPS], refs[2 + GROUPS :]
        place = Place(depth)
        side = Gather(place, blocks, [*groups, *riders], *refs[:3])
        out_sems = refs[3]
        units = side.units()

        def out_copy(g):
            columns = pl.ds(0, GROUP_WIDTH)
            target = pl.ds(g * GROUP_WIDTH, GROUP_WIDTH)
            return pltpu.make_async_copy(
                groups[g].at[:, :, :, :, :, columns],
                whole_qkv.at[:, :, :, :, :, target],
                out_sems.at[g],
            )

        vector_copy = pltpu.make_async_copy(
            groups[0].at[:, :, :, :, :, pl.ds(GROUP_WIDTH, LANES)], whole_vector, out_sems.at[GROUPS]
        )

        def open_up():
            place.greet()
            side.start_all()
            for t in range(3 * depth):
                side.step(units, t)
            side.receive_all(0)
            out_copy(0).start()
            vector_copy.start()
            for r in range(2 * PAIRS):
                d, j = r // per, r % per
                spot = (d // 8, d // 4 % 2, d // 2 % 2, d % 2)
                row = groups[0][(*spot, slice(j, j + 1), slice(GROUP_WIDTH, GROUP_WIDTH + LANES))]
                bias[r] = row.astype(F32)

        at_step(0, open_up)
        steps = seqs * GROUP_PAIRS

        def each(work, w):
            for k in range(depth):
                work(w, k)

        def ready(g):
            side.receive_all(g)
            out_copy(g).start()

        steps = seqs * PAIRS
        plan = [[] for _ in range(steps)]

        def put(i, work, *what):
            plan[min(i, steps - 1)].append(functools.partial(work, *what))

        proj, up = GROUPS, GROUPS + 1
        put(1, each, side.spread, 3)
        put(2, each, side.hand_over, 1)
        put(2, each, side.relay, 2)
        put(3, each, side.spread, proj)
        put(steps // GROUPS, ready, 1)
        for k in range(depth):
            put(4 + k, side.spread, up, k)
        put(5, each, side.relay, 3)
        put(6, each, side.hand_over, 2)
        put(7, each, side.relay, proj)
        put(2 * steps // GROUPS, ready, 2)
        put(8, each, side.hand_over, 3)
        put(10, each, side.hand_over, proj)
        put(3 * steps // GROUPS, ready, 3)
        for k in range(depth):
            put(9 + 2 * k, side.relay, up, k)
        put(13, side.hand_over, up, 0)
        for i in range(1, steps):

            def more(i=i):
                for work in plan[i]:
                    work()

            if plan[i]:
                at_step(i, more)
    else:
        weight, bias, qkv, attended, log_total, masks = refs[3:]
    at_step(0, lambda: fill_masks(ids_row, ids_column, masks))
    h, b = pl.program_id(0), pl.program_id(1)
    length = masks.shape[1]
    rows = tokens[pl.ds(pl.multiple_of(b * length, length), length), :]
    if depth:
        shifts = [bias[h], jnp.zeros((1, LANES), F32), bias[PAIRS + h]]
        shift = jnp.concatenate(shifts, axis=1)
        for g in range(GROUPS):

            @pl.when(h // GROUP_PAIRS == g)
            def _():
                qkv[...] = (qkv_rows_of(rows, groups[g], h) + shift).astype(BF16)
    else:
        qkv[...] = (dot_over(rows, weight[...], 1, 0) + bias[0]).astype(BF16)
    query = qkv[:, 0:LANES] * BF16(SCALE)
    key = qkv[:, LANES : 2 * LANES]
    value = qkv[:, 2 * LANES : 3 * LANES]
    chunk = length // 2
    outs = []
    for head in range(2):
        own_key = jnp.where(own_lanes(head), key, BF16(0))
        parts = []
        for at in range(0, length, chunk):
            scores = dot_over(own_key, query[at : at + chunk], 1, 1)
            scores = scores + masks[b, :, at : at + chunk]
            top = jnp.max(scores, axis=0, keepdims=True)
            weights = jnp.exp(scores - top)
            total = jnp.sum(weights, axis=0, keepdims=True)
            log_total[0, 0, head : head + 1, at : at + chunk] = top + jnp.log(total)
            probs = (weights * (1.0 / total)).astype(BF16)
            parts.append(dot_over(probs, value, 0, 0))
        outs.append(jnp.concatenate(parts, axis=0))
    attended[...] = jnp.where(own_lanes(0), outs[0], outs[1]).astype(BF16)
    if depth:

        def close():
            for k in range(1, depth):
                side.hand_over(up, k)
            for w in range(GROUPS, count):
                side.receive_all(w)
            side.sent_all()
            vector_copy.wait()
            for g in range(GROUPS):
                out_copy(g).wait()

        at_step(seqs * PAIRS - 1, close)


def attend_back_kernel(depth, seqs, per_device, *refs):
    ids_row, ids_column, tokens, qkv, attended_grad, log_total, weight, hidden_grad = refs[:8]
    steps = seqs * PAIRS
    i = pl.program_id(0)
    last = pl.num_programs(0) - 1
    spot = jnp.minimum(i, steps - 1)
    h, b = spot // seqs, spot % seqs
    if depth:
        up_grad, proj_grad, vector_part, input_grad = refs[8:12]
        out, refs = refs[12 : 15 + GROUPS], refs[15 + GROUPS :]
        masks, kept, total, sums, vector, *refs = refs
        groups, refs = refs[:GROUPS], refs[GROUPS:]
        grads = [up_grad, proj_grad, *groups, vector]
        count = len(grads)
        bufs = [refs[BUFS * w : BUFS * w + BUFS] for w in range(count)]
        place = Place(depth)
        side = Scatter(place, grads, out, bufs, *refs[BUFS * count :], resident=range(2, count))
        plan = [[] for _ in range(steps + tokens.shape[0] // ROW_BLOCK)]

        def put(at, work, *what):
            plan[min(at, len(plan) - 1)].append(functools.partial(work, *what))

        def each(work, w):
            def body(k, carry):
                work(w, k)
                return carry

            lax.fori_loop(0, depth, body, 0)

        up, proj, vec = 0, 1, count - 1
        put(0, place.greet)
        put(0, side.start, up)
        put(0, side.start, proj)
        for n, k in enumerate(side.order):
            put(1 + 2 * n, side.first, up, k)
            put(4 + 2 * n + n // 2, side.second, up, k)
            put(7 + 2 * n + n // 2, side.third, up, k)
        put(2, each, side.first, proj)
        put(5, each, side.second, proj)
        put(8, each, side.third, proj)
        per = steps // GROUPS
        for g in range(GROUPS):
            at = per * (g + 1)
            put(at, each, side.begin, 2 + g)
            put(at + 1, each, side.first, 2 + g)
            put(at + min(4, GROUPS + 1 - g), each, side.second, 2 + g)
            put(at + min(7, GROUPS + 2 - g), each, side.third, 2 + g)
        rows_each = per_device

        def make_vector():
            vector[...] = vector_part[...]
            for r in range(2 * PAIRS):
                d, j = r // rows_each, r % rows_each
                source = 0 if r < PAIRS else 2 * LANES
                row = sums[r % PAIRS, :, source : source + LANES]
                vector[d // 8, d // 4 % 2, d // 2 % 2, d % 2, j : j + 1, :] = row

        put(steps, make_vector)
        put(steps + 1, each, side.begin, vec)
        put(steps + 2, each, side.first, vec)
        put(steps + 3, each, side.second, vec)
        for at, works in enumerate(plan):

            def run(works=works):
                for work in works:
                    work()

            if works:
                pl.when(i == at)(run)
    else:
        input_grad, weight_grads, sums, masks, kept, total = refs[8:]
    pl.when(i == 0)(lambda: fill_masks(ids_row, ids_column, masks))
    length = qkv.shape[0]
    chunk = length // 2
    wide = pl.ds(pl.multiple_of(h * 3 * LANES, 3 * LANES), 3 * LANES)
    tall = pl.ds(pl.multiple_of(b * length, length), length)

    @pl.when(i < steps)
    def _():
        query = qkv[:, 0:LANES]
        key = qkv[:, LANES : 2 * LANES]
        value = qkv[:, 2 * LANES : 3 * LANES]
        grad = attended_grad[...]
        scaled = query * BF16(SCALE)
        query_grads, key_grads, value_grads = [], [], []
        for head in range(2):
            own_key = jnp.where(own_lanes(head), key, BF16(0))
            own_value = jnp.where(own_lanes(head), value, BF16(0))
            key_grad = value_grad = None
            parts = []
            for at in range(0, length, chunk):
                piece = slice(at, at + chunk)
                scores = dot_over(own_key, scaled[piece], 1, 1) + masks[b, :, piece]
                probs = jnp.exp(scores - log_total[0, 0, head : head + 1, piece])
                prob_grad = dot_over(own_value, grad[piece], 1, 1)
                row_dot = jnp.sum(probs * prob_grad, axis=0, keepdims=True)
                score_grad = (probs * (prob_grad - row_dot)).astype(BF16)
                value_part = dot_over(probs.astype(BF16), grad[piece], 1, 0)
                key_part = dot_over(score_grad, query[piece], 1, 0)
                value_grad = value_part if value_grad is None else value_grad + value_part
                key_grad = key_part if key_grad is None else key_grad + key_part
                parts.append(dot_over(score_grad, key, 0, 0))
            query_grads.append(jnp.concatenate(parts, axis=0))
            key_grads.append(key_grad)
            value_grads.append(value_grad)
        first = own_lanes(0)
        own = [
            (jnp.where(first, *query_grads) * SCALE).astype(BF16),
            (jnp.where(first, *key_grads) * SCALE).astype(BF16),
            jnp.where(first, *value_grads).astype(BF16),
        ]
        rows_grad = jnp.concatenate(own, axis=1)
        kept[tall, wide] = rows_grad
        part = dot_over(tokens[tall, :], rows_grad, 0, 0)
        part_sums = jnp.sum(rows_grad.astype(F32), axis=0, keepdims=True)

        @pl.when(b == 0)
        def _():
            total[...] = part
            sums[h] = part_sums

        @pl.when(b > 0)
        def _():
            total[...] += part
            sums[h] += part_sums

        @pl.when(b == seqs - 1)
        def _():
            if depth:
                where = (h % GROUP_PAIRS) * 3 * LANES
                columns = pl.ds(pl.multiple_of(where, 3 * LANES), 3 * LANES)
                for g in range(GROUPS):

                    @pl.when(h // GROUP_PAIRS == g)
                    def _():
                        shape = groups[g].shape[:5] + (3 * LANES,)
                        groups[g][:, :, :, :, :, columns] = total[...].astype(BF16).reshape(shape)
            else:
                weight_grads[...] = total[...]

    @pl.when(i >= steps)
    def _():
        at = pl.multiple_of((i - steps) * ROW_BLOCK, ROW_BLOCK)
        back = dot_over(kept[pl.ds(at, ROW_BLOCK), :], weight[...], 1, 1)
        input_grad[...] = (back + hidden_grad[...]).astype(BF16)

    if depth:

        @pl.when(i == last)
        def _():
            each(side.third, vec)
            for w in range(count):
                side.finish(w)


def whole(shape):
    return pl.BlockSpec(shape, lambda h, b: (0,) * len(shape))


def attention_specs(count, length):
    rows = whole((count, 1, length))
    columns = whole((count, length, 1))
    tokens = whole((count * length, D))
    wide = pl.BlockSpec((length, 3 * LANES), lambda h, b: (b, h))
    one = pl.BlockSpec((length, LANES), lambda h, b: (b, h))
    log_total = pl.BlockSpec((1, 1, 2, length), lambda h, b: (b, h, 0, 0))
    weight = pl.BlockSpec((D, 3 * LANES), lambda h, b: (0, h))
    vector = pl.BlockSpec((1, 1, 3 * LANES), lambda h, b: (h, 0, 0))
    return rows, columns, tokens, wide, one, log_total, weight, vector


def kernel_params(collective_id, remote, limit=60 << 20):
    if not remote:
        return pltpu.CompilerParams(vmem_limit_bytes=limit)
    return pltpu.CompilerParams(
        collective_id=collective_id, has_side_effects=True, vmem_limit_bytes=limit
    )


def attend(tokens, doc_ids, weight, bias, blocks, per, depth, collective_id):
    count, length = doc_ids.shape
    rows, columns, all_tokens, wide, one, log_total, part, vector = attention_specs(count, length)
    in_place = pl.BlockSpec(memory_space=pl.ANY)
    out_shape = [
        jax.ShapeDtypeStruct((count * length, 3 * D), BF16),
        jax.ShapeDtypeStruct((count * length, D), BF16),
        jax.ShapeDtypeStruct((count, PAIRS, 2, length), F32),
    ]
    out_specs = [wide, one, log_total]
    in_specs = [rows, columns, all_tokens]
    scratch = [pltpu.VMEM((count, length, length), F32)]
    grid3 = (depth, 2, 2, 2)
    if depth:
        in_specs += [whole(b.shape) for b in blocks]
        tall = blocks[0].shape[0]
        shapes = [(*grid3, tall, 3 * D), (*grid3, tall, LANES)]
        shapes += [grid3 + b.shape for b in blocks[GROUPS:]]
        out_shape += [jax.ShapeDtypeStruct(shape, BF16) for shape in shapes]
        out_specs += [in_place] * len(shapes)
        scratch += [pltpu.VMEM((2 * PAIRS, 1, LANES), F32)]
        scratch += [pltpu.VMEM(grid3 + b.shape, BF16) for b in blocks[:GROUPS]]
        scratch += gather_sems(len(blocks), depth) + [pltpu.SemaphoreType.DMA((GROUPS + 1,))]
        operands = blocks
    else:
        in_specs += [part, vector]
        operands = [weight, bias.reshape(PAIRS, 1, 3 * LANES)]
    return pl.pallas_call(
        functools.partial(attend_kernel, depth, len(blocks), count, per),
        grid=(PAIRS, count),
        in_specs=in_specs,
        out_specs=out_specs,
        out_shape=out_shape,
        scratch_shapes=scratch,
        compiler_params=kernel_params(collective_id, len(blocks)),
        name="attend",
    )(
        doc_ids.reshape(count, 1, length),
        doc_ids.reshape(count, length, 1),
        tokens,
        *operands,
    )


def attend_back(
    tokens, qkv, doc_ids, attended_grad, totals, weight, hidden_grad, grads, per_device, depth, collective_id
):
    seqs, length = doc_ids.shape
    steps = seqs * PAIRS
    blocks = seqs * length // ROW_BLOCK

    def h(i):
        return jnp.minimum(i, steps - 1) // seqs

    def b(i):
        return jnp.minimum(i, steps - 1) % seqs

    def late(i):
        return jnp.maximum(i - steps, 0)

    def once(shape):
        return pl.BlockSpec(shape, lambda i: (0,) * len(shape), pipeline_mode=pl.Buffered(1))

    in_place = pl.BlockSpec(memory_space=pl.ANY)
    in_specs = [
        once((seqs, 1, length)),
        once((seqs, length, 1)),
        once((seqs * length, D)),
        pl.BlockSpec((length, 3 * LANES), lambda i: (b(i), h(i))),
        pl.BlockSpec((length, LANES), lambda i: (b(i), h(i))),
        pl.BlockSpec((1, 1, 2, length), lambda i: (b(i), h(i), 0, 0)),
        once((D, 3 * D)),
        pl.BlockSpec((ROW_BLOCK, D), lambda i: (late(i), 0)),
    ]
    out_specs = [pl.BlockSpec((ROW_BLOCK, D), lambda i: (late(i), 0))]
    out_shape = [jax.ShapeDtypeStruct((seqs * length, D), BF16)]
    scratch = [
        pltpu.VMEM((seqs, length, length), F32),
        pltpu.VMEM((seqs * length, 3 * D), BF16),
        pltpu.VMEM((D, 3 * LANES), F32),
    ]
    if depth:
        up_grad, proj_grad, vector = grads
        tall = up_grad.shape[-2]
        group = jax.ShapeDtypeStruct((depth, 2, 2, 2, tall, GROUP_WIDTH), BF16)
        moved = [up_grad, proj_grad, *([group] * GROUPS), vector]
        in_specs += [in_place, in_place, flat(vector.shape)]
        out_specs += [flat(m.shape[-2:]) for m in moved]
        out_shape += [jax.ShapeDtypeStruct(m.shape[-2:], F32) for m in moved]
        scratch += [pltpu.VMEM((PAIRS, 1, 3 * LANES), F32), pltpu.VMEM(vector.shape, F32)]
        scratch += [pltpu.VMEM(group.shape, BF16)] * GROUPS
        scratch += scatter_scratch(moved, depth, resident=range(2, len(moved)))
    else:
        out_specs += [
            pl.BlockSpec((D, 3 * LANES), lambda i: (0, h(i))),
            flat((PAIRS, 1, 3 * LANES)),
        ]
        out_shape += [
            jax.ShapeDtypeStruct((D, 3 * D), F32),
            jax.ShapeDtypeStruct((PAIRS, 1, 3 * LANES), F32),
        ]
    return pl.pallas_call(
        functools.partial(attend_back_kernel, depth, seqs, per_device),
        grid=(steps + blocks,),
        in_specs=in_specs,
        out_specs=out_specs,
        out_shape=out_shape,
        scratch_shapes=scratch,
        compiler_params=kernel_params(collective_id, depth, 63 << 20),
        name="attend_back",
    )(
        doc_ids.reshape(seqs, 1, length),
        doc_ids.reshape(seqs, length, 1),
        tokens,
        qkv,
        attended_grad,
        totals,
        weight,
        hidden_grad,
        *grads,
    )


TILE = 512
ROW_CHUNK = 256


def widen_kernel(depth, tiles, *refs):
    low, up_weight, up_bias, normed, scales, block = refs[:6]
    activated, slope, second_in, whole_down = refs[6:10]
    kept, down, out_sems, *sems = refs[10:]
    place = Place(depth)
    side = Gather(place, [block], [down], *sems)
    units = side.units()
    i = pl.program_id(0)
    per = tiles // depth

    def out_copy(k):
        zz = place.back(k)
        return pltpu.make_async_copy(down.at[zz], whole_down.at[zz], out_sems.at[k])

    def step_of(t, work):
        pl.when(i == t)(work)

    def open_up():
        place.greet()
        side.start_all()

    step_of(0, open_up)
    for t in range(tiles):
        step_of(t, functools.partial(side.step, units, t))

    @pl.when(i < tiles)
    def _():
        for at in range(0, low.shape[0], ROW_CHUNK):
            rows = slice(at, at + ROW_CHUNK)
            upward = dot_over(low[rows, :], up_weight[...], 1, 0) + up_bias[...]
            cdf = 0.5 * (1.0 + lax.erf(upward * HALF_ROOT))
            value = (upward * cdf).astype(BF16)
            activated[rows, :] = value
            kept[i, rows, :] = value
            slope[rows, :] = cdf + upward * (PDF_TOP * jnp.exp(-0.5 * upward * upward))

    for k in range(depth):

        def layer(k=k):
            if tiles + k < len(units) + 2 * depth:
                side.step(units, tiles + k)
            side.receive(0, k)
            out_copy(k).start()
            zz = place.back(k)
            for at in range(0, low.shape[0], ROW_CHUNK):
                rows = slice(at, at + ROW_CHUNK)
                if k == 0:
                    total = normed[rows, :] * scales[0:1, :] + scales[1:2, :] + scales[2:3, :]
                else:
                    total = second_in[rows, :]
                for n in range(per):
                    tile = kept[zz * per + n, rows, :]
                    weight = rows_of(down[zz, n * 2 // per : (n + 1) * 2 // per])
                    total = total + dot_over(tile, weight, 1, 0)
                second_in[rows, :] = total

        step_of(tiles + k, layer)

    def close():
        for t in range(tiles + depth, len(units) + 2 * depth):
            side.step(units, t)
        side.sent_all()
        for k in range(depth):
            out_copy(k).wait()

    step_of(tiles + depth - 1, close)


def flat(shape):
    return pl.BlockSpec(shape, lambda i: (0,) * len(shape))


def widen(low, up_weight, up_bias, normed, scales, block, depth, collective_id):
    count = low.shape[0]
    tiles = FF // TILE
    last = tiles - 1
    tile = pl.BlockSpec((count, TILE), lambda i: (0, jnp.minimum(i, last)))
    spread = (depth, 2, 2, 2) + block.shape
    return pl.pallas_call(
        functools.partial(widen_kernel, depth, tiles),
        grid=(tiles + depth,),
        in_specs=[
            flat(low.shape),
            pl.BlockSpec((D, TILE), lambda i: (0, jnp.minimum(i, last))),
            pl.BlockSpec((1, TILE), lambda i: (0, jnp.minimum(i, last))),
            flat(normed.shape),
            flat(scales.shape),
            flat(block.shape),
        ],
        out_specs=[tile, tile, flat((count, D)), pl.BlockSpec(memory_space=pl.ANY)],
        out_shape=[
            jax.ShapeDtypeStruct((count, FF), BF16),
            jax.ShapeDtypeStruct((count, FF), F32),
            jax.ShapeDtypeStruct((count, D), F32),
            jax.ShapeDtypeStruct(spread, BF16),
        ],
        scratch_shapes=[
            pltpu.VMEM((tiles, count, TILE), BF16),
            pltpu.VMEM(spread, BF16),
            pltpu.SemaphoreType.DMA((depth,)),
            *gather_sems(1, depth),
        ],
        compiler_params=kernel_params(collective_id, 1),
        name="widen",
    )(low, up_weight, up_bias[None], normed, scales, block)


def widen_back_kernel(depth, tiles, *refs):
    rows_grad, activated, slope, down_weight, low_turned, up_weight = refs[:6]
    up_grad, branch_grad, sums, down_out = refs[6:10]
    kept, down_grad, total, *rest = refs[10:]
    place = Place(depth)
    side = Scatter(place, [down_grad], [down_out], [rest[:BUFS]], *rest[BUFS:], resident=(0,))
    i = pl.program_id(0)
    per = tiles // depth

    def step_of(t, work):
        pl.when(i == t)(work)

    step_of(0, place.greet)
    for zz in range(depth):
        k = (zz + depth - place.z) % depth
        ready = (zz + 1) * per
        step_of(ready, functools.partial(side.begin, 0, k))
        step_of(ready + 1, functools.partial(side.first, 0, k))
        step_of(ready + 3, functools.partial(side.second, 0, k))
        step_of(ready + 5, functools.partial(side.third, 0, k))

    @pl.when(i < tiles)
    def _():
        for at in range(0, rows_grad.shape[0], ROW_CHUNK):
            rows = slice(at, at + ROW_CHUNK)
            back = dot_over(rows_grad[rows, :], down_weight[...], 1, 1)
            kept[i, rows, :] = (back * slope[rows, :]).astype(BF16)
        sums[0] = jnp.sum(kept[i].astype(F32), axis=0, keepdims=True)
        grad = dot_over(activated[...], rows_grad[...], 0, 0).astype(BF16)
        blocks = TILE // down_grad.shape[4]
        grad = grad.reshape(1, blocks // 4, 2, 2, down_grad.shape[4], D)[0]
        part = pl.ds((i % per) * (blocks // 4), blocks // 4)
        down_grad[i // per, part] = grad

    @pl.when(i >= tiles)
    def _():
        tile = kept[i - tiles]
        up_grad[...] = dot_over(low_turned[...], tile, 1, 0).astype(BF16)
        for at in range(0, rows_grad.shape[0], ROW_CHUNK):
            rows = slice(at, at + ROW_CHUNK)
            part = dot_over(tile[rows, :], up_weight[...], 1, 1)

            @pl.when(i == tiles)
            def _():
                total[rows, :] = part

            @pl.when(i > tiles)
            def _():
                total[rows, :] += part

    @pl.when(i == 2 * tiles - 1)
    def _():
        branch_grad[...] = total[...]
        side.finish(0)


def widen_back(rows_grad, activated, slope, down_weight, low_turned, up_weight, depth, collective_id):
    count = rows_grad.shape[0]
    tiles = FF // TILE
    last = tiles - 1

    def early(i):
        return jnp.minimum(i, last)

    def late(i):
        return jnp.maximum(i - tiles, 0)

    shares = 8 * depth
    spread = jax.ShapeDtypeStruct((depth, 2, 2, 2, FF // shares, D), BF16)
    return pl.pallas_call(
        functools.partial(widen_back_kernel, depth, tiles),
        grid=(2 * tiles,),
        in_specs=[
            flat(rows_grad.shape),
            pl.BlockSpec((count, TILE), lambda i: (0, early(i))),
            pl.BlockSpec((count, TILE), lambda i: (0, early(i))),
            pl.BlockSpec((TILE, D), lambda i: (early(i), 0)),
            flat(low_turned.shape),
            pl.BlockSpec((D, TILE), lambda i: (0, late(i))),
        ],
        out_specs=[
            pl.BlockSpec((D, TILE), lambda i: (0, late(i))),
            flat((count, D)),
            pl.BlockSpec((1, 1, TILE), lambda i: (early(i), 0, 0)),
            flat(spread.shape[-2:]),
        ],
        out_shape=[
            jax.ShapeDtypeStruct((D, FF), BF16),
            jax.ShapeDtypeStruct((count, D), F32),
            jax.ShapeDtypeStruct((tiles, 1, TILE), F32),
            jax.ShapeDtypeStruct(spread.shape[-2:], F32),
        ],
        scratch_shapes=[
            pltpu.VMEM((tiles, count, TILE), BF16),
            pltpu.VMEM(spread.shape, BF16),
            pltpu.VMEM((count, D), F32),
            *scatter_scratch([spread], depth, resident=(0,)),
        ],
        compiler_params=kernel_params(collective_id, 1),
        name="widen_back",
    )(rows_grad, activated, slope, down_weight, low_turned, up_weight)


ROW_BLOCK = 256


def mean_of(rows):
    return jnp.sum(rows, axis=-1, keepdims=True) * (1.0 / D)


def normalized(hidden):
    center = hidden - mean_of(hidden)
    root = lax.rsqrt(mean_of(center * center) + NORM_EPS)
    return center * root, root


def norm_back(grad, normed, root, gain):
    scaled = grad * gain
    return root * (scaled - mean_of(scaled) - normed * mean_of(scaled * normed))


def add_sums(sums, *rows):
    new = [jnp.sum(r.astype(F32), axis=0, keepdims=True) for r in rows]

    @pl.when(pl.program_id(0) == 0)
    def _():
        sums[...] = jnp.zeros_like(sums)

    for j, n in enumerate(new):
        sums[j : j + 1, :] += n


def project_kernel(attended, tokens, weight, scales, normed, root, low, turned):
    hidden = dot_over(attended[...], weight[...], 1, 0)
    hidden = tokens[...].astype(F32) + hidden + scales[0:1, :]
    normed[...], root[...] = normalized(hidden)
    branch = normed[...] * scales[1:2, :] + scales[2:3, :]
    low[...] = branch.astype(BF16)
    turned[...] = branch.T.astype(BF16)


def output_kernel(second_in, cotangent, scales, output, rows, grad, sums):
    normed, root = normalized(second_in[...])
    output[...] = (normed * scales[0:1, :] + scales[1:2, :]).astype(BF16)
    upstream = cotangent[...].astype(F32)
    grad[...] = norm_back(upstream, normed, root, scales[0:1, :])
    rows[...] = grad[...].astype(BF16)
    add_sums(sums, upstream * normed, upstream, rows[...])


def project_back_kernel(
    branch_grad, second_grad, normed, root, attended, weight, scales, grad, back, weight_grads, sums, total
):
    upstream = branch_grad[...] + second_grad[...]
    grad[...] = norm_back(upstream, normed[...], root[...], scales[0:1, :])
    rows = grad[...].astype(BF16)
    back[...] = dot_over(rows, weight[...], 1, 1).astype(BF16)
    add_sums(sums, upstream * normed[...], upstream, rows)
    part = dot_over(attended[...], rows, 0, 0)

    @pl.when(pl.program_id(0) == 0)
    def _():
        total[...] = part

    @pl.when(pl.program_id(0) > 0)
    def _():
        total[...] += part

    @pl.when(pl.program_id(0) == pl.num_programs(0) - 1)
    def _():
        weight_grads[...] = total[...].astype(weight_grads.dtype)


def row_block(width=D):
    return pl.BlockSpec((ROW_BLOCK, width), lambda i: (i, 0))


def row_call(kernel, count, in_specs, out_specs, outs, scratch=()):
    return pl.pallas_call(
        kernel,
        grid=(count // ROW_BLOCK,),
        in_specs=in_specs,
        out_specs=out_specs,
        out_shape=[jax.ShapeDtypeStruct(shape, dtype) for shape, dtype in outs],
        scratch_shapes=list(scratch),
        compiler_params=pltpu.CompilerParams(vmem_limit_bytes=60 << 20),
        name=kernel.__name__,
    )


SUMS = (8, D)


def project(attended, tokens, weight, scales):
    count = tokens.shape[0]
    block, matrix = row_block(), flat((D, D))
    turned = pl.BlockSpec((D, ROW_BLOCK), lambda i: (0, i))
    outs = [((count, D), F32), ((count, 1), F32), ((count, D), BF16), ((D, count), BF16)]
    return row_call(
        project_kernel,
        count,
        [block, block, matrix, flat(scales.shape)],
        [block, row_block(1), block, turned],
        outs,
    )(attended, tokens, weight, scales)


def output_and_grad(second_in, cotangent, scales):
    count = second_in.shape[0]
    block = row_block()
    shape = (count, D)
    return row_call(
        output_kernel,
        count,
        [block, block, flat(scales.shape)],
        [block, block, block, flat(SUMS)],
        [(shape, BF16), (shape, BF16), (shape, F32), (SUMS, F32)],
    )(second_in, cotangent, scales)


def project_back(branch_grad, second_grad, normed, root, attended, weight, scales, dtype):
    count = attended.shape[0]
    block, matrix = row_block(), flat((D, D))
    shape = (count, D)
    return row_call(
        project_back_kernel,
        count,
        [block, block, block, row_block(1), block, matrix, flat(scales.shape)],
        [block, block, matrix, flat(SUMS)],
        [(shape, F32), (shape, BF16), ((D, D), dtype), (SUMS, F32)],
        [pltpu.VMEM((D, D), F32)],
    )(branch_grad, second_grad, normed, root, attended, weight, scales)


def split_vector(vector):
    sizes = (D, D, D, D, D, FF, D, D, D)
    parts, at = [], 0
    for size in sizes:
        parts.append(vector[at : at + size])
        at += size
    return parts


def by_pair(columns):
    rows = columns.shape[0]
    return columns.reshape(rows, 3, PAIRS, LANES).swapaxes(1, 2).reshape(rows, 3 * D)


def by_kind(columns):
    rows = columns.shape[0]
    return columns.reshape(rows, PAIRS, 3, LANES).swapaxes(1, 2).reshape(rows, 3 * D)


def stacked(*vectors):
    return jnp.pad(jnp.stack(vectors), ((0, 8 - len(vectors)), (0, 0)))


def column_sums(rows):
    return jnp.sum(rows.astype(F32), axis=0)


def times(rows, matrix):
    return jnp.dot(rows, matrix, preferred_element_type=F32)


def weight_grad(left_rows, right_rows, dtype):
    return dot_over(left_rows, right_rows, 0, 0).astype(dtype)


def back_product(grad_rows, matrix):
    return dot_over(grad_rows, matrix, 1, 1)


def layer_step(tokens, doc_ids, cotangent, masters, devices, depth):
    grad_type = BF16 if depth else F32
    shape = (depth, 2, 2, 2)
    blocks, low_vector = lowered_blocks(masters)
    rows = low_vector.shape[0] // LANES
    if depth:
        tall = blocks[0].shape[0]
        padded = jnp.pad(low_vector.reshape(rows, LANES), ((0, tall - rows), (0, 0)))
        first = [blocks[0][:, g * GROUP_WIDTH : (g + 1) * GROUP_WIDTH] for g in range(GROUPS)]
        first[0] = jnp.concatenate([first[0], padded], axis=1)
        qkv, attended, totals, qkv_weight, vectors, proj_weight, up_weight = attend(
            tokens, doc_ids, None, None, first + blocks[1:3], rows, depth, 1
        )
        vector = vectors.reshape(devices, tall, LANES)[:, :rows].reshape(-1)
        qkv_weight, proj_weight, up_weight = map(rows_of, (qkv_weight, proj_weight, up_weight))
    else:
        weights = [lax.all_gather(b, "dp", axis=0, tiled=True) for b in blocks]
        qkv_weight, proj_weight, up_weight, down_weight = weights
        vector = lax.all_gather(low_vector, "dp", axis=0, tiled=True)
    (
        bias_query,
        bias_value,
        bias_proj,
        gain_first,
        shift_first,
        bias_up,
        bias_down,
        gain_second,
        shift_second,
    ) = split_vector(vector.astype(F32))
    if not depth:
        bias_all = jnp.concatenate([bias_query, jnp.zeros_like(bias_query), bias_value])
        bias_all = by_pair(bias_all[None])[0]
        qkv, attended, totals = attend(tokens, doc_ids, qkv_weight, bias_all, [], 0, 0, 0)
    normed, root, branch_low, low_turned = project(
        attended, tokens, proj_weight, stacked(bias_proj, gain_first, shift_first)
    )
    if depth:
        activated, slope, second_in, down_weight = widen(
            branch_low,
            up_weight,
            bias_up,
            normed,
            stacked(gain_first, shift_first, bias_down),
            blocks[3],
            depth,
            2,
        )
        down_weight = rows_of(down_weight)
    else:
        upward = times(branch_low, up_weight) + bias_up
        cdf = 0.5 * (1.0 + lax.erf(upward * HALF_ROOT))
        activated = (upward * cdf).astype(BF16)
        slope = cdf + upward * (PDF_TOP * jnp.exp(-0.5 * upward * upward))
        branch = normed * gain_first + shift_first
        second_in = branch + times(activated, down_weight) + bias_down
    output, down_rows, second_grad, second_sums = output_and_grad(
        second_in, cotangent, stacked(gain_second, shift_second)
    )
    if depth:
        up_grad, branch_grad, bias_up_grad, down_owned = widen_back(
            down_rows, activated, slope, down_weight, low_turned, up_weight, depth, 3
        )
        bias_up_grad = bias_up_grad.reshape(-1)
    else:
        down_grad = weight_grad(activated, down_rows, F32)
        up_rows = (back_product(down_rows, down_weight) * slope).astype(BF16)
        bias_up_grad = column_sums(up_rows)
        up_grad = weight_grad(branch_low, up_rows, F32)
        branch_grad = back_product(up_rows, up_weight)
    hidden_grad, attended_grad, proj_grad, first_sums = project_back(
        branch_grad,
        second_grad,
        normed,
        root,
        attended,
        proj_weight,
        stacked(gain_first),
        grad_type,
    )
    known = [
        first_sums[2],
        first_sums[0],
        first_sums[1],
        bias_up_grad,
        second_sums[2],
        second_sums[0],
        second_sums[1],
    ]
    riders = []
    if depth:
        vector_part = jnp.concatenate([jnp.zeros((2 * D,), F32), *known])
        vector_part = vector_part.reshape(devices, rows, LANES)
        vector_part = jnp.pad(vector_part, ((0, 0), (0, 16 - rows), (0, 0)))
        riders = [g.reshape(*shape, -1, g.shape[1]) for g in (up_grad, proj_grad)]
        riders += [vector_part.reshape(*shape, 16, LANES)]
    input_grad, *summed = attend_back(
        tokens,
        qkv,
        doc_ids,
        attended_grad,
        totals,
        qkv_weight,
        hidden_grad,
        riders,
        rows,
        depth,
        4,
    )
    if depth:
        up_owned, proj_owned, *qkv_owned, vector_owned = summed
        owned = [jnp.concatenate(qkv_owned, axis=1), proj_owned, up_owned, down_owned]
        owned += [vector_owned[:rows]]
    else:
        qkv_grad, qkv_sums = summed
        qkv_sums = by_kind(qkv_sums.reshape(1, -1))[0]
        vector_grad = jnp.concatenate([qkv_sums[0:D], qkv_sums[2 * D : 3 * D], *known])
        grads = (qkv_grad, proj_grad, up_grad, down_grad, vector_grad[:, None])
        owned = [
            lax.psum_scatter(
                grad.reshape(devices, -1, grad.shape[-1]), "dp", scatter_dimension=0, tiled=True
            )[0]
            for grad in grads
        ]
    owned[0] = by_kind(owned[0])
    return output, input_grad, [own.reshape(-1) for own in owned]


def adam_update(master, moment_one, moment_two, grad, rate):
    one_new = BETA_FIRST * moment_one + (1.0 - BETA_FIRST) * grad
    two_new = BETA_SECOND * moment_two + (1.0 - BETA_SECOND) * grad * grad
    one_hat = one_new / (1.0 - BETA_FIRST**STEP)
    two_hat = two_new / (1.0 - BETA_SECOND**STEP)
    master_new = master - rate * (one_hat / (jnp.sqrt(two_hat) + ADAM_EPS) + WEIGHT_DECAY * master)
    return (grad, one_new, two_new, master_new, master_new.astype(BF16))


WIDTHS = (3 * D, D, FF, D)


def lowered_blocks(masters):
    lowered = [master.astype(BF16) for master in masters]
    blocks = [low.reshape(-1, width) for low, width in zip(lowered, WIDTHS)]
    blocks[0] = by_pair(blocks[0])
    return blocks, lowered[4]


def body(depth, tokens, segment_ids, out_grad, *states):
    devices = lax.axis_size("dp")
    masters = states[0::3]
    output, input_grad, owned = layer_step(
        tokens, segment_ids, out_grad, masters, devices, depth
    )
    outs = [output, input_grad]
    for i in range(5):
        outs += adam_update(*states[3 * i : 3 * i + 3], owned[i], RATES[i])
    return tuple(outs)


def solution(mesh):
    rows = P("dp", None)
    flat = P("dp")
    return jax.shard_map(
        functools.partial(body, depth_of(mesh)),
        mesh=mesh,
        in_specs=(rows,) * 3 + (flat,) * 15,
        out_specs=(rows,) * 2 + (flat,) * 25,
        check_vma=False,
    )
```

time: 484 us -> 419 us (0.87)
  matrix products: 125 us -> 0 us
  Pallas kernels: 301 us -> 381 us
  other arithmetic: 25.2 us -> 15.5 us
  local copies, waits for them, and re-layouts: 24 us -> 14.5 us
    dot_general x10 -> x0, matrix products: 125 us -> none  [the longest x7 85.3 us: dot_over(): lax.dot_general(left, right, (((left_dim,), (right_dim,)), ((), ())), pre...]
    pallas_call x4 -> x7, Pallas kernels: 301 us -> 381 us  [the longest x1 105 us: attend(): pl.pallas_call(functools.partial(attend_kernel, depth, len(blocks), count...]
    unnamed x79 -> x49, local copies, waits for them, and re-layouts: 15.2 us -> 4.83 us
    reduce_sum x5 -> x0, other arithmetic: 9.34 us -> none  [the longest x3 8.38 us: column_sums(): return jnp.sum(rows.astype(F32), axis=0)]
    convert_element_type x5 -> x4, other arithmetic: 10.2 us -> 8.99 us  [adam_update(): return (grad, one_new, two_new, master_new, master_new.astype(BF16))]
where the time goes in v3:
time: 419 us; the launch traced here: 412 us
  Pallas kernels  381 us (91%)
  other arithmetic  15.5 us (4%)
  local copies, waits for them, and re-layouts  14.5 us (3%)
    pallas_call x1, Pallas kernels, attend(): pl.pallas_call(functools.partial(attend_kernel, depth, len(blocks), count...  105 us
    pallas_call x1, Pallas kernels, attend_back(): pl.pallas_call(functools.partial(attend_back_kernel, depth, seqs, per_dev...  104 us
    pallas_call x1, Pallas kernels, widen_back(): pl.pallas_call(functools.partial(widen_back_kernel, depth, tiles), grid=(...  76.8 us
    pallas_call x1, Pallas kernels, widen(): pl.pallas_call(functools.partial(widen_kernel, depth, tiles), grid=(tiles...  63 us
    pallas_call x1, Pallas kernels, project_back(): row_call(project_back_kernel, count, [block, block, block, row_block(1),...  15 us
    convert_element_type x4, other arithmetic, adam_update(): return (grad, one_new, two_new, master_new, master_new.astype(BF16))  8.99 us
    pallas_call x1, Pallas kernels, project(): row_call(project_kernel, count, [block, block, matrix, flat(scales.shape)...  8.64 us

profile of v3, /device:TPU:0, one launch (start us, length us, event | category | flops | bytes accessed | tf_op | source)
XLA Modules:
  0.0 412.2 jit_solution(17141510464643938952)
XLA Ops:
  0.7 1.0 convert_element_type.47
  1.7 0.1 copy.45
  1.8 0.2 reshape.127
  2.0 0.7 fusion.17
  2.6 0.7 convert_bitcast_fusion
  3.3 0.6 fusion.5.refs_3_
  3.9 1.7 copy.46.refs_1_
  5.7 1.3 reshape.125.refs_0_
  6.9 1.1 convert_element_type.50
  8.0 0.8 reshape.130.refs_8_
  8.8 0.9 convert_element_type.49
  9.7 0.7 reshape.129.refs_7_
  10.4 105.5 %attend.1 = (bf16[1024,3072]{1,0:T(8,128)(2,1)}, bf16[1024,1024]{1,0:T(8,128)(2,1)}, f32[2,8,2,512]{3,2,1,0:T(2,128)}, bf16[4,2,2,2,32,3072]{5,4,3,2,1,0:T(8,128...) custom-call(s32[2,1,512]{2,1,0:T(1,128)} %reshape.125.refs_0_, ...), custom_call_target="tpu_custom_call" | custom-call | tf_op jit(solution)/shard_map/attend/pallas_call | solution.py:727
  115.9 0.8 slice_convert_fusion
  116.8 0.7 select_maximum_fusion.1
  117.4 8.6 %project_kernel.1 = (f32[1024,1024]{1,0:T(8,128)}, f32[1024,1]{1,0:T(8,128)}, bf16[1024,1024]{1,0:T(8,128)(2,1)}, bf16[1024,1024]{1,0:T(8,128)(2,1)}) custom-call(bf16[1024,1024]{1,0:T(8,128)(2,1)} %get-tuple-element.62.attended, bf16[1024,1024]{1,0:T(8,128)(2,1)} %refs_2_.3, bf16[1024,1024]{1,0:T(8,128)(2,1)} %bitcast.41, f32[8,1024]{1,0:T(8,128)} %get-tuple-element.135.scales), custom_call_target="tpu_custom_call" | custom-call | tf_op jit(solution)/shard_map/project_kernel/pallas_call | solution.py:1132
  126.1 0.6 slice.84
  126.7 0.0 copy-done.2
  126.7 0.8 reshape.134.refs_5_
  127.5 63.0 %widen.1 = (bf16[1024,4096]{1,0:T(8,128)(2,1)}, f32[1024,4096]{1,0:T(8,128)}, f32[1024,1024]{1,0:T(8,128)}, bf16[4,2,2,2,128,1024]{5,4,3,2,1,0:T(8,128)(2,1)}) custom-call(bf16[1024,1024]{1,0:T(8,128)(2,1)} %get-tuple-element.65.refs_0_, bf16[1024,4096]{1,0:T(8,128)(2,1)} %bitcast.39, f32[1,4096]{1,0:T(1,128)} %bitcast.61, ...), custom_call_target="tpu_custom_call" | custom-call | tf_op jit(solution)/shard_map/widen/pallas_call | solution.py:905
  190.5 0.6 select_maximum_fusion.scales
  191.1 8.1 %output_kernel.1 = (bf16[1024,1024]{1,0:T(8,128)(2,1)}, bf16[1024,1024]{1,0:T(8,128)(2,1)}, f32[1024,1024]{1,0:T(8,128)}, f32[8,1024]{1,0:T(8,128)}) custom-call(f32[1024,1024]{1,0:T(8,128)} %get-tuple-element.68.second_in, bf16[1024,1024]{1,0:T(8,128)(2,1)} %cotangent.1, f32[8,1024]{1,0:T(8,128)} %select_maximum_fusion.scales), custom_call_target="tpu_custom_call" | custom-call | tf_op jit(solution)/shard_map/output_kernel/pallas_call | solution.py:1145
  199.2 76.8 %widen_back.1 = (bf16[1024,4096]{1,0:T(8,128)(2,1)}, f32[1024,1024]{1,0:T(8,128)}, f32[8,1,512]{2,1,0:T(1,128)}, f32[128,1024]{1,0:T(8,128)}) custom-call(bf16[1024,1024]{1,0:T(8,128)(2,1)} %get-tuple-element.71.refs_0_, bf16[1024,4096]{1,0:T(8,128)(2,1)} %get-tuple-element.72.refs_1_, f32[1024,4096]{1,0:T(8,128)} %get-tuple-element.73.refs_2_, ...), custom_call_target="tpu_custom_call" | custom-call | tf_op jit(solution)/shard_map/widen_back/pallas_call | solution.py:1003
  276.0 0.0 copy-start.15
  276.0 15.0 %project_back_kernel.1 = (f32[1024,1024]{1,0:T(8,128)}, bf16[1024,1024]{1,0:T(8,128)(2,1)}, bf16[1024,1024]{1,0:T(8,128)(2,1)}, f32[8,1024]{1,0:T(8,128)}) custom-call(f32[1024,1024]{1,0:T(8,128)} %get-tuple-element.76.branch_grad, f32[1024,1024]{1,0:T(8,128)} %get-tuple-element.77.second_grad, f32[1024,1024]{1,0:T(8,128)} %get-tuple-element.67.refs_3_.normed, ...), custom_call_target="tpu_custom_call" | custom-call | tf_op jit(solution)/shard_map/project_back_kernel/pallas_call | solution.py:1158
  291.0 0.9 fusion.20
  291.9 0.0 copy-done.15
  291.9 0.9 fusion.19
  292.9 0.7 pad.28
  293.6 103.7 %attend_back.1 = (bf16[1024,1024]{1,0:T(8,128)(2,1)}, f32[32,4096]{1,0:T(8,128)}, f32[32,1024]{1,0:T(8,128)}, f32[32,768]{1,0:T(8,128)}, f32[32,768]{1,0:T(8,128...) custom-call(s32[2,1,512]{2,1,0:T(1,128)} %reshape.125.refs_0_, s32[2,512,1]{2,1,0:T(8,128)} %copy.46.refs_1_, ...), custom_call_target="tpu_custom_call" | custom-call | tf_op jit(solution)/shard_map/attend_back/pallas_call | solution.py:801
  397.4 1.1 copy.50
  398.5 0.0 copy-start.3
  398.5 1.3 copy.51
  399.8 0.0 copy-start.4
  399.9 0.0 copy-start.11
  399.9 0.0 copy-start.12
  399.9 0.0 copy-start.13
  399.9 0.0 copy-start.14
  399.9 0.0 copy-done.1
  399.9 0.0 copy-start.6
  399.9 4.1 fusion.9
  404.0 0.0 copy-done.3
  404.0 0.0 copy-start.16
  404.0 0.0 copy-start.17
  404.0 0.0 copy-start.18
  404.0 0.0 copy-start
  404.0 0.0 copy-done.4
  404.0 0.0 copy-done.11
  404.1 0.0 copy-done.12
  404.1 0.0 copy-done.13
  404.1 0.0 copy-done.14
  404.1 0.3 reshape.142
  404.4 0.0 copy-start.9
  404.4 0.0 copy-start.10
  404.5 0.0 copy-start.5
  404.5 0.0 copy-done.6
  404.5 2.8 fusion.15
  407.3 0.9 copy.49
  408.2 0.0 copy-start.8
  408.3 0.8 fusion.13
  409.1 0.0 copy-done.17
  409.1 1.3 fusion.7
  410.4 1.3 copy.60
  411.7 0.0 copy-done.8
  (24 shorter events, 0.2 us)
Async XLA Ops:
  10.4 116.3 %copy-start.2 = (f32[131072]{0:T(1024)S(1)}, f32[131072]{0:T(1024)}, u32[]{:S(2)}) copy-start(f32[131072]{0:T(1024)} %param.30) | copy-start | bytes 1572868
  276.0 15.9 %copy-start.15 = (f32[8,1,512]{2,1,0:T(1,128)S(1)}, f32[8,1,512]{2,1,0:T(1,128)}, u32[]{:S(2)}) copy-start(f32[8,1,512]{2,1,0:T(1,128)} %get-tuple-element.86) | copy-start | bytes 49156
  293.6 106.3 %copy-start.1 = (f32[131072]{0:T(1024)S(1)}, f32[131072]{0:T(1024)}, u32[]{:S(2)}) copy-start(f32[131072]{0:T(1024)} %param.27) | copy-start | bytes 1572868
  398.5 5.5 %copy-start.3 = (f32[4,32,8,128]{3,1,2,0:T(8,128)}, f32[4,32,8,128]{3,1,2,0:T(8,128)S(1)}, u32[]{:S(2)}) copy-start(f32[4,32,8,128]{3,1,2,0:T(8,128)S(1)} %copy.50) | copy-start | bytes 1572868
  399.8 4.2 %copy-start.4 = (f32[16,8,8,128]{3,1,2,0:T(8,128)}, f32[16,8,8,128]{3,1,2,0:T(8,128)S(1)}, u32[]{:S(2)}) copy-start(f32[16,8,8,128]{3,1,2,0:T(8,128)S(1)} %copy.51) | copy-start | bytes 1572868
  399.9 4.2 %copy-start.11 = (f32[32,768]{1,0:T(8,128)S(1)}, f32[32,768]{1,0:T(8,128)}, u32[]{:S(2)}) copy-start(f32[32,768]{1,0:T(8,128)} %get-tuple-element.89) | copy-start | bytes 294916
  399.9 4.2 %copy-start.12 = (f32[32,768]{1,0:T(8,128)S(1)}, f32[32,768]{1,0:T(8,128)}, u32[]{:S(2)}) copy-start(f32[32,768]{1,0:T(8,128)} %get-tuple-element.90) | copy-start | bytes 294916
  399.9 4.2 %copy-start.13 = (f32[32,768]{1,0:T(8,128)S(1)}, f32[32,768]{1,0:T(8,128)}, u32[]{:S(2)}) copy-start(f32[32,768]{1,0:T(8,128)} %get-tuple-element.91) | copy-start | bytes 294916
  399.9 4.2 %copy-start.14 = (f32[32,768]{1,0:T(8,128)S(1)}, f32[32,768]{1,0:T(8,128)}, u32[]{:S(2)}) copy-start(f32[32,768]{1,0:T(8,128)} %get-tuple-element.92) | copy-start | bytes 294916
  399.9 4.6 %copy-start.6 = (f32[98304]{0:T(1024)S(1)}, f32[98304]{0:T(1024)}, u32[]{:S(2)}) copy-start(f32[98304]{0:T(1024)} %param.21) | copy-start | bytes 1179652
  404.0 4.3 %copy-start.7 = (f32[32768]{0:T(1024)S(1)}, f32[32768]{0:T(1024)}, u32[]{:S(2)}) copy-start(f32[32768]{0:T(1024)} %param.24) | copy-start | bytes 393220
  404.0 5.1 %copy-start.16 = (f32[384]{0:T(512)S(1)}, f32[384]{0:T(512)}, u32[]{:S(2)}) copy-start(f32[384]{0:T(512)} %param.33) | copy-start | bytes 4612
  404.0 5.1 %copy-start.17 = (f32[384]{0:T(512)S(1)}, f32[384]{0:T(512)}, u32[]{:S(2)}) copy-start(f32[384]{0:T(512)} %param.35) | copy-start | bytes 4612
  404.0 5.1 %copy-start.18 = (f32[384]{0:T(512)S(1)}, f32[384]{0:T(512)}, u32[]{:S(2)}) copy-start(f32[384]{0:T(512)} %param.34) | copy-start | bytes 4612
  404.0 6.4 %copy-start = (bf16[1024,1024]{1,0:T(8,128)(2,1)S(1)}, bf16[1024,1024]{1,0:T(8,128)(2,1)}, u32[]{:S(2)}) copy-start(bf16[1024,1024]{1,0:T(8,128)(2,1)} %get-tuple-element.169) | copy-start | bytes 6291460
  404.4 3.9 copy-start.9
  404.4 3.9 copy-start.10
  404.5 7.3 %copy-start.5 = (f32[32,3,8,128]{3,2,1,0:T(8,128)}, f32[32,3,8,128]{3,2,1,0:T(8,128)S(1)}, u32[]{:S(2)}) copy-start(f32[32,3,8,128]{3,2,1,0:T(8,128)S(1)} %copy.48) | copy-start | bytes 1179652
  408.2 3.5 copy-start.8

commit v4 on v3

--- a/solution.py
+++ b/solution.py
@@ -37,6 +37,9 @@
     )
 
 
+PLANNED_DEPTH = 4
+
+
 def depth_of(mesh):
     devices = list(mesh.devices.flat)
     if len(devices) % 8:
@@ -47,6 +50,8 @@
         return 0
     low = [min(s[i] for s in spots) for i in range(4)]
     depth = len(devices) // 8
+    if depth != PLANNED_DEPTH:
+        return 0
     for index, (x, y, z, core) in enumerate(spots):
         spot = (((z - low[2]) * 2 + y - low[1]) * 2 + x - low[0]) * 2 + core - low[3]
         if spot != index:
@@ -448,18 +453,17 @@
         put(2, each, side.relay, 2)
         put(3, each, side.spread, proj)
         put(steps // GROUPS, ready, 1)
-        for k in range(depth):
-            put(4 + k, side.spread, up, k)
         put(5, each, side.relay, 3)
         put(6, each, side.hand_over, 2)
         put(7, each, side.relay, proj)
         put(2 * steps // GROUPS, ready, 2)
         put(8, each, side.hand_over, 3)
-        put(10, each, side.hand_over, proj)
+        put(9, each, side.hand_over, proj)
         put(3 * steps // GROUPS, ready, 3)
         for k in range(depth):
-            put(9 + 2 * k, side.relay, up, k)
-        put(13, side.hand_over, up, 0)
+            put(4 + k, side.spread, up, k)
+            put(8 + k, side.relay, up, k)
+            put(11 + k, side.hand_over, up, k)
         for i in range(1, steps):
 
             def more(i=i):
@@ -506,8 +510,6 @@
     if depth:
 
         def close():
-            for k in range(1, depth):
-                side.hand_over(up, k)
             for w in range(GROUPS, count):
                 side.receive_all(w)
             side.sent_all()
@@ -756,9 +758,6 @@
 
     def late(i):
         return jnp.maximum(i - steps, 0)
-
-    def once(shape):
-        return pl.BlockSpec(shape, lambda i: (0,) * len(shape), pipeline_mode=pl.Buffered(1))
 
     in_place = pl.BlockSpec(memory_space=pl.ANY)
     in_specs = [
@@ -825,35 +824,68 @@
 
 
 def widen_kernel(depth, tiles, *refs):
-    low, up_weight, up_bias, normed, scales, block = refs[:6]
-    activated, slope, second_in, whole_down = refs[6:10]
-    kept, down, out_sems, *sems = refs[10:]
+    low, up_weight, up_bias, normed, scales = refs[:5]
+    blocks = refs[5:7]
+    activated, slope, second_in, whole_up, whole_down = refs[7:12]
+    kept, tile_weight, late_up, down, out_sems, *sems = refs[12:]
     place = Place(depth)
-    side = Gather(place, [block], [down], *sems)
-    units = side.units()
+    side = Gather(place, blocks, [late_up, down], *sems)
     i = pl.program_id(0)
     per = tiles // depth
+    half = tiles // 2
 
     def out_copy(k):
         zz = place.back(k)
         return pltpu.make_async_copy(down.at[zz], whole_down.at[zz], out_sems.at[k])
 
-    def step_of(t, work):
-        pl.when(i == t)(work)
-
-    def open_up():
-        place.greet()
-        side.start_all()
-
-    step_of(0, open_up)
-    for t in range(tiles):
-        step_of(t, functools.partial(side.step, units, t))
+    up_copy = pltpu.make_async_copy(late_up, whole_up, out_sems.at[depth])
+    plan = [[] for _ in range(tiles + depth)]
+
+    def put(at, work, *what):
+        plan[min(at, len(plan) - 1)].append(functools.partial(work, *what))
+
+    put(0, place.greet)
+    put(0, side.start_all)
+    for k in range(depth):
+        put(min(k, half - 1), side.spread, 0, k)
+        put(min(k + 2, half), side.relay, 0, k)
+    put(half, side.spread, 1, 0)
+    put(half, side.spread, 1, 1)
+    for k in range(depth):
+        put(half, side.hand_over, 0, k)
+    put(half, side.receive_all, 0)
+    put(half, up_copy.start)
+    put(half + 1, side.relay, 1, 0)
+    for k in range(2, depth):
+        put(half + 2 * k - 2, side.spread, 1, k)
+    for k in range(1, depth - 1):
+        put(half + 1 + 2 * k, side.relay, 1, k)
+    put(tiles + depth - 2, side.relay, 1, depth - 1)
+    for k in range(depth):
+        put(tiles + k, side.hand_over, 1, k)
+    for at, works in enumerate(plan):
+
+        def run(works=works):
+            for work in works:
+                work()
+
+        if works:
+            pl.when(i == at)(run)
+
+    @pl.when(i < half)
+    def _():
+        tile_weight[...] = up_weight[...]
+
+    @pl.when((i >= half) & (i < tiles))
+    def _():
+        columns = pl.ds(pl.multiple_of((i - half) * TILE, TILE), TILE)
+        tile_weight[...] = rows_of(late_up[:, :, :, :, :, columns])
 
     @pl.when(i < tiles)
     def _():
         for at in range(0, low.shape[0], ROW_CHUNK):
             rows = slice(at, at + ROW_CHUNK)
-            upward = dot_over(low[rows, :], up_weight[...], 1, 0) + up_bias[...]
+            upward = dot_over(low[rows, :], tile_weight[...], 1, 0) + up_bias[...]
             cdf = 0.5 * (1.0 + lax.erf(upward * HALF_ROOT))
             value = (upward * cdf).astype(BF16)
             activated[rows, :] = value
@@ -863,9 +895,7 @@
     for k in range(depth):
 
         def layer(k=k):
-            if tiles + k < len(units) + 2 * depth:
-                side.step(units, tiles + k)
-            side.receive(0, k)
+            side.receive(1, k)
             out_copy(k).start()
             zz = place.back(k)
             for at in range(0, low.shape[0], ROW_CHUNK):
@@ -880,61 +910,70 @@
                     total = total + dot_over(tile, weight, 1, 0)
                 second_in[rows, :] = total
 
-        step_of(tiles + k, layer)
-
-    def close():
-        for t in range(tiles + depth, len(units) + 2 * depth):
-            side.step(units, t)
+        pl.when(i == tiles + k)(layer)
+
+    @pl.when(i == tiles + depth - 1)
+    def _():
         side.sent_all()
+        up_copy.wait()
         for k in range(depth):
             out_copy(k).wait()
 
-    step_of(tiles + depth - 1, close)
-
 
 def flat(shape):
     return pl.BlockSpec(shape, lambda i: (0,) * len(shape))
 
 
-def widen(low, up_weight, up_bias, normed, scales, block, depth, collective_id):
+def once(shape):
+    return pl.BlockSpec(shape, lambda i: (0,) * len(shape), pipeline_mode=pl.Buffered(1))
+
+
+def widen(low, up_weight, up_bias, normed, scales, blocks, depth, collective_id):
     count = low.shape[0]
     tiles = FF // TILE
-    last = tiles - 1
+    last, half = tiles - 1, tiles // 2
     tile = pl.BlockSpec((count, TILE), lambda i: (0, jnp.minimum(i, last)))
-    spread = (depth, 2, 2, 2) + block.shape
+    spread = [(depth, 2, 2, 2) + block.shape for block in blocks]
+    in_place = pl.BlockSpec(memory_space=pl.ANY)
     return pl.pallas_call(
         functools.partial(widen_kernel, depth, tiles),
         grid=(tiles + depth,),
         in_specs=[
-            flat(low.shape),
-            pl.BlockSpec((D, TILE), lambda i: (0, jnp.minimum(i, last))),
+            once(low.shape),
+            pl.BlockSpec((D, TILE), lambda i: (0, jnp.minimum(i, half - 1))),
             pl.BlockSpec((1, TILE), lambda i: (0, jnp.minimum(i, last))),
-            flat(normed.shape),
-            flat(scales.shape),
-            flat(block.shape),
+            once(normed.shape),
+            once(scales.shape),
+            *[once(block.shape) for block in blocks],
         ],
-        out_specs=[tile, tile, flat((count, D)), pl.BlockSpec(memory_space=pl.ANY)],
+        out_specs=[tile, tile, flat((count, D)), in_place, in_place],
         out_shape=[
             jax.ShapeDtypeStruct((count, FF), BF16),
             jax.ShapeDtypeStruct((count, FF), F32),
             jax.ShapeDtypeStruct((count, D), F32),
-            jax.ShapeDtypeStruct(spread, BF16),
+            *[jax.ShapeDtypeStruct(shape, BF16) for shape in spread],
         ],
         scratch_shapes=[
             pltpu.VMEM((tiles, count, TILE), BF16),
-            pltpu.VMEM(spread, BF16),
-            pltpu.SemaphoreType.DMA((depth,)),
-            *gather_sems(1, depth),
+            pltpu.VMEM((D, TILE), BF16),
+            *[pltpu.VMEM(shape, BF16) for shape in spread],
+            pltpu.SemaphoreType.DMA((depth + 1,)),
+            *gather_sems(2, depth),
         ],
         compiler_params=kernel_params(collective_id, 1),
         name="widen",
-    )(low, up_weight, up_bias[None], normed, scales, block)
+    )(low, up_weight, up_bias[None], normed, scales, *blocks)
+
+
+def early_tile(i, tiles, depth):
+    ahead = (lax.axis_index("dp") // 8 + 1) * (tiles // depth)
+    return (jnp.minimum(i, tiles - 1) + ahead) % tiles
 
 
 def widen_back_kernel(depth, tiles, *refs):
-    rows_grad, activated, slope, down_weight, low_turned, up_weight = refs[:6]
-    up_grad, branch_grad, sums, down_out = refs[6:10]
-    kept, down_grad, total, *rest = refs[10:]
+    rows_grad, activated, slope, down_weight, low_turned, up_early, up_late = refs[:7]
+    up_grad, branch_grad, sums, down_out = refs[7:11]
+    kept, down_grad, total, *rest = refs[11:]
     place = Place(depth)
     side = Scatter(place, [down_grad], [down_out], [rest[:BUFS]], *rest[BUFS:], resident=(0,))
     i = pl.program_id(0)
@@ -944,9 +983,9 @@
         pl.when(i == t)(work)
 
     step_of(0, place.greet)
-    for zz in range(depth):
-        k = (zz + depth - place.z) % depth
-        ready = (zz + 1) * per
+    now = early_tile(i, tiles, depth)
+    for n, k in enumerate(side.order):
+        ready = (n + 1) * per
         step_of(ready, functools.partial(side.begin, 0, k))
         step_of(ready + 1, functools.partial(side.first, 0, k))
         step_of(ready + 3, functools.partial(side.second, 0, k))
@@ -957,21 +996,22 @@
         for at in range(0, rows_grad.shape[0], ROW_CHUNK):
             rows = slice(at, at + ROW_CHUNK)
             back = dot_over(rows_grad[rows, :], down_weight[...], 1, 1)
-            kept[i, rows, :] = (back * slope[rows, :]).astype(BF16)
-        sums[0] = jnp.sum(kept[i].astype(F32), axis=0, keepdims=True)
+            kept[now, rows, :] = (back * slope[rows, :]).astype(BF16)
+        sums[0] = jnp.sum(kept[now].astype(F32), axis=0, keepdims=True)
         grad = dot_over(activated[...], rows_grad[...], 0, 0).astype(BF16)
         blocks = TILE // down_grad.shape[4]
         grad = grad.reshape(1, blocks // 4, 2, 2, down_grad.shape[4], D)[0]
-        part = pl.ds((i % per) * (blocks // 4), blocks // 4)
-        down_grad[i // per, part] = grad
+        part = pl.ds((now % per) * (blocks // 4), blocks // 4)
+        down_grad[now // per, part] = grad
 
     @pl.when(i >= tiles)
     def _():
         tile = kept[i - tiles]
         up_grad[...] = dot_over(low_turned[...], tile, 1, 0).astype(BF16)
+        up_weight = jnp.where(i - tiles < tiles // 2, up_early[...], up_late[...])
         for at in range(0, rows_grad.shape[0], ROW_CHUNK):
             rows = slice(at, at + ROW_CHUNK)
-            part = dot_over(tile[rows, :], up_weight[...], 1, 1)
+            part = dot_over(tile[rows, :], up_weight, 1, 1)
 
             @pl.when(i == tiles)
             def _():
@@ -987,13 +1027,16 @@
         side.finish(0)
 
 
-def widen_back(rows_grad, activated, slope, down_weight, low_turned, up_weight, depth, collective_id):
+def widen_back(
+    rows_grad, activated, slope, down_weight, low_turned, up_early, up_late, depth, collective_id
+):
     count = rows_grad.shape[0]
     tiles = FF // TILE
-    last = tiles - 1
+
+    half = tiles // 2
 
     def early(i):
-        return jnp.minimum(i, last)
+        return early_tile(i, tiles, depth)
 
     def late(i):
         return jnp.maximum(i - tiles, 0)
@@ -1004,12 +1047,13 @@
         functools.partial(widen_back_kernel, depth, tiles),
         grid=(2 * tiles,),
         in_specs=[
-            flat(rows_grad.shape),
+            once(rows_grad.shape),
             pl.BlockSpec((count, TILE), lambda i: (0, early(i))),
             pl.BlockSpec((count, TILE), lambda i: (0, early(i))),
             pl.BlockSpec((TILE, D), lambda i: (early(i), 0)),
-            flat(low_turned.shape),
-            pl.BlockSpec((D, TILE), lambda i: (0, late(i))),
+            once(low_turned.shape),
+            pl.BlockSpec((D, TILE), lambda i: (0, jnp.minimum(late(i), half - 1))),
+            pl.BlockSpec((D, TILE), lambda i: (0, jnp.maximum(late(i) - half, 0))),
         ],
         out_specs=[
             pl.BlockSpec((D, TILE), lambda i: (0, late(i))),
@@ -1031,7 +1075,7 @@
         ],
         compiler_params=kernel_params(collective_id, 1),
         name="widen_back",
-    )(rows_grad, activated, slope, down_weight, low_turned, up_weight)
+    )(rows_grad, activated, slope, down_weight, low_turned, up_early, up_late)
 
 
 ROW_BLOCK = 256
@@ -1214,8 +1258,9 @@
         padded = jnp.pad(low_vector.reshape(rows, LANES), ((0, tall - rows), (0, 0)))
         first = [blocks[0][:, g * GROUP_WIDTH : (g + 1) * GROUP_WIDTH] for g in range(GROUPS)]
         first[0] = jnp.concatenate([first[0], padded], axis=1)
+        up_blocks = [blocks[2][:, : FF // 2], blocks[2][:, FF // 2 :]]
         qkv, attended, totals, qkv_weight, vectors, proj_weight, up_weight = attend(
-            tokens, doc_ids, None, None, first + blocks[1:3], rows, depth, 1
+            tokens, doc_ids, None, None, [*first, blocks[1], up_blocks[0]], rows, depth, 1
         )
         vector = vectors.reshape(devices, tall, LANES)[:, :rows].reshape(-1)
         qkv_weight, proj_weight, up_weight = map(rows_of, (qkv_weight, proj_weight, up_weight))
@@ -1242,17 +1287,17 @@
         attended, tokens, proj_weight, stacked(bias_proj, gain_first, shift_first)
     )
     if depth:
-        activated, slope, second_in, down_weight = widen(
+        activated, slope, second_in, up_late, down_weight = widen(
             branch_low,
             up_weight,
             bias_up,
             normed,
             stacked(gain_first, shift_first, bias_down),
-            blocks[3],
+            [up_blocks[1], blocks[3]],
             depth,
             2,
         )
-        down_weight = rows_of(down_weight)
+        up_late, down_weight = rows_of(up_late), rows_of(down_weight)
     else:
         upward = times(branch_low, up_weight) + bias_up
         cdf = 0.5 * (1.0 + lax.erf(upward * HALF_ROOT))
@@ -1265,7 +1310,15 @@
     )
     if depth:
         up_grad, branch_grad, bias_up_grad, down_owned = widen_back(
-            down_rows, activated, slope, down_weight, low_turned, up_weight, depth, 3
+            down_rows,
+            activated,
+            slope,
+            down_weight,
+            low_turned,
+            up_weight,
+            up_late,
+            depth,
+            3,
         )
         bias_up_grad = bias_up_grad.reshape(-1)
     else:

time: 419 us -> 407 us (0.971)
  Pallas kernels: 381 us -> 371 us
    pallas_call x1, Pallas kernels: 105 us -> 85.2 us  [attend(): pl.pallas_call(functools.partial(attend_kernel, depth, len(blocks), count...]
    pallas_call x1, Pallas kernels: 63 us -> 73.4 us  [widen(): pl.pallas_call(functools.partial(widen_kernel, depth, tiles), grid=(tiles...]
where the time goes in v4:
time: 407 us; the launch traced here: 401 us
  Pallas kernels  371 us (91%)
  other arithmetic  14.6 us (4%)
  local copies, waits for them, and re-layouts  13.8 us (3%)
    pallas_call x1, Pallas kernels, attend_back(): pl.pallas_call(functools.partial(attend_back_kernel, depth, seqs, per_dev...  100 us
    pallas_call x1, Pallas kernels, attend(): pl.pallas_call(functools.partial(attend_kernel, depth, len(blocks), count...  85.2 us
    pallas_call x1, Pallas kernels, widen_back(): pl.pallas_call(functools.partial(widen_back_kernel, depth, tiles), grid=(...  80.4 us
    pallas_call x1, Pallas kernels, widen(): pl.pallas_call(functools.partial(widen_kernel, depth, tiles), grid=(tiles...  73.4 us
    pallas_call x1, Pallas kernels, project_back(): row_call(project_back_kernel, count, [block, block, block, row_block(1),...  14.9 us
    convert_element_type x4, other arithmetic, adam_update(): return (grad, one_new, two_new, master_new, master_new.astype(BF16))  8.96 us
    pallas_call x1, Pallas kernels, project(): row_call(project_kernel, count, [block, block, matrix, flat(scales.shape)...  8.63 us

profile of v4, /device:TPU:0, one launch (start us, length us, event | category | flops | bytes accessed | tf_op | source)
XLA Modules:
  0.0 401.0 jit_solution(4423574513908035271)
XLA Ops:
  0.7 0.0 copy-start.15
  0.7 0.0 copy-start.7
  0.7 1.1 convert_element_type.47
  1.7 0.1 copy.45
  1.9 0.2 reshape.130
  2.0 0.7 fusion.18
  2.7 0.7 convert_bitcast_fusion
  3.4 0.6 fusion.5.refs_3_
  4.0 1.1 convert_element_type.50
  5.1 0.1 reshape.133
  5.2 0.7 fusion.17
  5.9 1.7 copy.46.refs_1_
  7.6 0.0 copy-done.15
  7.6 0.6 reshape.128.refs_0_
  8.2 0.0 copy-done.7
  8.2 0.7 reshape.132.refs_7_
  8.9 85.2 %attend.1 = (bf16[1024,3072]{1,0:T(8,128)(2,1)}, bf16[1024,1024]{1,0:T(8,128)(2,1)}, f32[2,8,2,512]{3,2,1,0:T(2,128)}, bf16[4,2,2,2,32,3072]{5,4,3,2,1,0:T(8,128...) custom-call(s32[2,1,512]{2,1,0:T(1,128)} %reshape.128.refs_0_, ...), custom_call_target="tpu_custom_call" | custom-call | tf_op jit(solution)/shard_map/attend/pallas_call | solution.py:729
  94.1 0.8 slice_convert_fusion
  95.0 0.7 select_maximum_fusion.1
  95.7 8.6 %project_kernel.1 = (f32[1024,1024]{1,0:T(8,128)}, f32[1024,1]{1,0:T(8,128)}, bf16[1024,1024]{1,0:T(8,128)(2,1)}, bf16[1024,1024]{1,0:T(8,128)(2,1)}) custom-call(bf16[1024,1024]{1,0:T(8,128)(2,1)} %get-tuple-element.63.attended, bf16[1024,1024]{1,0:T(8,128)(2,1)} %refs_2_.3, bf16[1024,1024]{1,0:T(8,128)(2,1)} %bitcast.42, f32[8,1024]{1,0:T(8,128)} %get-tuple-element.139.scales), custom_call_target="tpu_custom_call" | custom-call | tf_op jit(solution)/shard_map/project_kernel/pallas_call | solution.py:1176
  104.3 0.6 slice.93
  104.9 0.0 copy-done.2
  104.9 0.8 reshape.137.refs_6_
  105.8 73.4 %widen.1 = (bf16[1024,4096]{1,0:T(8,128)(2,1)}, f32[1024,4096]{1,0:T(8,128)}, f32[1024,1024]{1,0:T(8,128)}, bf16[4,2,2,2,32,2048]{5,4,3,2,1,0:T(8,128)(2,1)}, bf16[4,2,2,2,128,1024]{5,4,3,2,1,0:T(8,128)(2,1)}) custom-call(bf16[1024,1024]{1,0:T(8,128)(2,1)} %get-tuple-element.66.refs_0_, bf16[1024,2048]{1,0:T(8,128)(2,1)} %bitcast.40, f32[1,4096]{1,0:T(1,128)} %bitcast.63, ...), custom_call_target="tpu_custom_call" | custom-call | tf_op jit(solution)/shard_map/widen/pallas_call | solution.py:938
  179.2 0.6 select_maximum_fusion.scales
  179.8 8.0 %output_kernel.1 = (bf16[1024,1024]{1,0:T(8,128)(2,1)}, bf16[1024,1024]{1,0:T(8,128)(2,1)}, f32[1024,1024]{1,0:T(8,128)}, f32[8,1024]{1,0:T(8,128)}) custom-call(f32[1024,1024]{1,0:T(8,128)} %get-tuple-element.69.second_in, bf16[1024,1024]{1,0:T(8,128)(2,1)} %cotangent.1, f32[8,1024]{1,0:T(8,128)} %select_maximum_fusion.scales), custom_call_target="tpu_custom_call" | custom-call | tf_op jit(solution)/shard_map/output_kernel/pallas_call | solution.py:1189
  187.8 80.4 %widen_back.1 = (bf16[1024,4096]{1,0:T(8,128)(2,1)}, f32[1024,1024]{1,0:T(8,128)}, f32[8,1,512]{2,1,0:T(1,128)}, f32[128,1024]{1,0:T(8,128)}) custom-call(bf16[1024,1024]{1,0:T(8,128)(2,1)} %get-tuple-element.72.refs_0_, bf16[1024,4096]{1,0:T(8,128)(2,1)} %get-tuple-element.73.refs_1_, f32[1024,4096]{1,0:T(8,128)} %get-tuple-element.74.refs_2_, ...), custom_call_target="tpu_custom_call" | custom-call | tf_op jit(solution)/shard_map/widen_back/pallas_call | solution.py:1046
  268.2 0.0 copy-start.16
  268.2 14.9 %project_back_kernel.1 = (f32[1024,1024]{1,0:T(8,128)}, bf16[1024,1024]{1,0:T(8,128)(2,1)}, bf16[1024,1024]{1,0:T(8,128)(2,1)}, f32[8,1024]{1,0:T(8,128)}) custom-call(f32[1024,1024]{1,0:T(8,128)} %get-tuple-element.78.branch_grad, f32[1024,1024]{1,0:T(8,128)} %get-tuple-element.79.second_grad, f32[1024,1024]{1,0:T(8,128)} %get-tuple-element.68.refs_3_.normed, ...), custom_call_target="tpu_custom_call" | custom-call | tf_op jit(solution)/shard_map/project_back_kernel/pallas_call | solution.py:1202
  283.2 0.9 fusion.21
  284.1 0.0 copy-done.16
  284.1 0.9 fusion.20
  285.1 0.7 pad.28
  285.8 100.4 %attend_back.1 = (bf16[1024,1024]{1,0:T(8,128)(2,1)}, f32[32,4096]{1,0:T(8,128)}, f32[32,1024]{1,0:T(8,128)}, f32[32,768]{1,0:T(8,128)}, f32[32,768]{1,0:T(8,128...) custom-call(s32[2,1,512]{2,1,0:T(1,128)} %reshape.128.refs_0_, s32[2,512,1]{2,1,0:T(8,128)} %copy.46.refs_1_, ...), custom_call_target="tpu_custom_call" | custom-call | tf_op jit(solution)/shard_map/attend_back/pallas_call | solution.py:800
  386.3 1.1 copy.50
  387.4 0.0 copy-start.3
  387.4 1.3 copy.51
  388.7 0.0 copy-start.4
  388.8 0.0 copy-start.11
  388.8 0.0 copy-start.12
  388.8 0.0 copy-start.13
  388.8 0.0 copy-start.14
  388.8 0.0 copy-done.1
  388.8 0.0 copy-start.6
  388.8 4.1 %fusion.9 = (bf16[131072]{0:T(1024)(128)(2,1)}, f32[131072]{0:T(1024)}, f32[131072]{0:T(1024)}, f32[131072]{0:T(1024)}, bf16[131072]{0:T(1024)(128)(2,1)}, /*ind...) fusion(f32[131072]{0:T(1024)} %param.30, f32[131072]{0:T(1024)S(1)} %bitcast.52, f32[131072]{0:T(1024)} %param.32, ...), kind=kLoop, calls=%fused_computation.43 | loop fusion | flops 3932160 | bytes 7864320 | tf_op jit(solution)/shard_map/convert_element_type | solution.py:1394
  392.9 0.0 copy-done.3
  392.9 0.0 copy-start.18
  392.9 0.0 copy-start.19
  392.9 0.0 copy-start
  393.0 0.3 reshape.146
  393.3 0.0 copy-start.9
  393.3 0.0 copy-start.10
  393.4 0.0 copy-start.5
  393.4 2.8 fusion.15
  396.2 0.9 copy.49
  397.1 0.0 copy-start.8
  397.1 0.0 copy-done.9
  397.1 0.0 copy-done.10
  397.1 0.8 fusion.13
  398.0 0.0 copy-done.19
  398.0 1.3 fusion.7
  399.3 0.0 copy-done
  399.3 1.3 copy.60
  400.6 0.0 copy-done.8
  (27 shorter events, 0.2 us)
Async XLA Ops:
  0.7 7.0 %copy-start.15 = (s32[2,512]{1,0:T(2,128)S(1)}, s32[2,512]{1,0:T(2,128)}, u32[]{:S(2)}) copy-start(s32[2,512]{1,0:T(2,128)} %param.19) | copy-start | bytes 12292
  0.7 7.5 %copy-start.7 = (f32[32768]{0:T(1024)S(1)}, f32[32768]{0:T(1024)}, u32[]{:S(2)}) copy-start(f32[32768]{0:T(1024)} %param.24) | copy-start | bytes 393220
  8.9 96.0 %copy-start.2 = (f32[131072]{0:T(1024)S(1)}, f32[131072]{0:T(1024)}, u32[]{:S(2)}) copy-start(f32[131072]{0:T(1024)} %param.30) | copy-start | bytes 1572868
  268.2 15.9 %copy-start.16 = (f32[8,1,512]{2,1,0:T(1,128)S(1)}, f32[8,1,512]{2,1,0:T(1,128)}, u32[]{:S(2)}) copy-start(f32[8,1,512]{2,1,0:T(1,128)} %get-tuple-element.88) | copy-start | bytes 49156
  285.8 103.0 %copy-start.1 = (f32[131072]{0:T(1024)S(1)}, f32[131072]{0:T(1024)}, u32[]{:S(2)}) copy-start(f32[131072]{0:T(1024)} %param.27) | copy-start | bytes 1572868
  387.4 5.5 %copy-start.3 = (f32[4,32,8,128]{3,1,2,0:T(8,128)}, f32[4,32,8,128]{3,1,2,0:T(8,128)S(1)}, u32[]{:S(2)}) copy-start(f32[4,32,8,128]{3,1,2,0:T(8,128)S(1)} %copy.50) | copy-start | bytes 1572868
  388.7 4.2 %copy-start.4 = (f32[16,8,8,128]{3,1,2,0:T(8,128)}, f32[16,8,8,128]{3,1,2,0:T(8,128)S(1)}, u32[]{:S(2)}) copy-start(f32[16,8,8,128]{3,1,2,0:T(8,128)S(1)} %copy.51) | copy-start | bytes 1572868
  388.8 4.2 %copy-start.11 = (f32[32,768]{1,0:T(8,128)S(1)}, f32[32,768]{1,0:T(8,128)}, u32[]{:S(2)}) copy-start(f32[32,768]{1,0:T(8,128)} %get-tuple-element.91) | copy-start | bytes 294916
  388.8 4.2 %copy-start.12 = (f32[32,768]{1,0:T(8,128)S(1)}, f32[32,768]{1,0:T(8,128)}, u32[]{:S(2)}) copy-start(f32[32,768]{1,0:T(8,128)} %get-tuple-element.92) | copy-start | bytes 294916
  388.8 4.2 %copy-start.13 = (f32[32,768]{1,0:T(8,128)S(1)}, f32[32,768]{1,0:T(8,128)}, u32[]{:S(2)}) copy-start(f32[32,768]{1,0:T(8,128)} %get-tuple-element.93) | copy-start | bytes 294916
  388.8 4.2 %copy-start.14 = (f32[32,768]{1,0:T(8,128)S(1)}, f32[32,768]{1,0:T(8,128)}, u32[]{:S(2)}) copy-start(f32[32,768]{1,0:T(8,128)} %get-tuple-element.94) | copy-start | bytes 294916
  388.8 4.6 %copy-start.6 = (f32[98304]{0:T(1024)S(1)}, f32[98304]{0:T(1024)}, u32[]{:S(2)}) copy-start(f32[98304]{0:T(1024)} %param.21) | copy-start | bytes 1179652
  392.9 5.1 %copy-start.17 = (f32[384]{0:T(512)S(1)}, f32[384]{0:T(512)}, u32[]{:S(2)}) copy-start(f32[384]{0:T(512)} %param.33) | copy-start | bytes 4612
  392.9 5.1 %copy-start.18 = (f32[384]{0:T(512)S(1)}, f32[384]{0:T(512)}, u32[]{:S(2)}) copy-start(f32[384]{0:T(512)} %param.35) | copy-start | bytes 4612
  392.9 5.1 %copy-start.19 = (f32[384]{0:T(512)S(1)}, f32[384]{0:T(512)}, u32[]{:S(2)}) copy-start(f32[384]{0:T(512)} %param.34) | copy-start | bytes 4612
  392.9 6.3 %copy-start = (bf16[1024,1024]{1,0:T(8,128)(2,1)S(1)}, bf16[1024,1024]{1,0:T(8,128)(2,1)}, u32[]{:S(2)}) copy-start(bf16[1024,1024]{1,0:T(8,128)(2,1)} %get-tuple-element.173) | copy-start | bytes 6291460
  393.3 3.8 copy-start.9
  393.3 3.8 copy-start.10
  393.4 7.2 %copy-start.5 = (f32[32,3,8,128]{3,2,1,0:T(8,128)}, f32[32,3,8,128]{3,2,1,0:T(8,128)S(1)}, u32[]{:S(2)}) copy-start(f32[32,3,8,128]{3,2,1,0:T(8,128)S(1)} %copy.48) | copy-start | bytes 1179652
  397.1 3.5 copy-start.8

commit v5 on v4

--- a/solution.py
+++ b/solution.py
@@ -272,8 +272,7 @@
 
     @staticmethod
     def add(target, extra):
-        total = target[...].astype(F32) + extra[...].astype(F32)
-        target[...] = total.astype(target.dtype)
+        target[...] = target[...] + extra[...]
 
     def start(self, w):
         for k in self.order:
@@ -384,20 +383,16 @@
     return block.reshape(-1, block.shape[-1])
 
 
-def qkv_rows_of(rows, weight, h):
-    columns = pl.ds(pl.multiple_of((h % GROUP_PAIRS) * 3 * LANES, 3 * LANES), 3 * LANES)
-    if len(weight.shape) == 2:
-        return dot_over(rows, weight[:, columns], 1, 0)
-    return dot_over(rows, rows_of(weight[:, :, :, :, :, columns]), 1, 0)
-
-
 def attend_kernel(depth, count, seqs, per, *refs):
     ids_row, ids_column, tokens = refs[:3]
     if depth:
         blocks, refs = refs[3 : 3 + count], refs[3 + count :]
         qkv, attended, log_total, whole_qkv, whole_vector = refs[:5]
         riders, refs = refs[5 : 5 + count - GROUPS], refs[5 + count - GROUPS :]
-        masks, bias, groups, refs = refs[0], refs[1], refs[2 : 2 + GROUPS], refs[2 + GROUPS :]
+        masks, bias, store, refs = refs[0], refs[1], refs[2], refs[3:]
+        groups = [
+            store.at[g, :, :, :, :, :, pl.ds(0, blocks[g].shape[1])] for g in range(GROUPS)
+        ]
         place = Place(depth)
         side = Gather(place, blocks, [*groups, *riders], *refs[:3])
         out_sems = refs[3]
@@ -427,7 +422,7 @@
             for r in range(2 * PAIRS):
                 d, j = r // per, r % per
                 spot = (d // 8, d // 4 % 2, d // 2 % 2, d % 2)
-                row = groups[0][(*spot, slice(j, j + 1), slice(GROUP_WIDTH, GROUP_WIDTH + LANES))]
+                row = store[(0, *spot, slice(j, j + 1), slice(GROUP_WIDTH, GROUP_WIDTH + LANES))]
                 bias[r] = row.astype(F32)
 
         at_step(0, open_up)
@@ -481,11 +476,9 @@
     if depth:
         shifts = [bias[h], jnp.zeros((1, LANES), F32), bias[PAIRS + h]]
         shift = jnp.concatenate(shifts, axis=1)
-        for g in range(GROUPS):
-
-            @pl.when(h // GROUP_PAIRS == g)
-            def _():
-                qkv[...] = (qkv_rows_of(rows, groups[g], h) + shift).astype(BF16)
+        columns = pl.ds(pl.multiple_of((h % GROUP_PAIRS) * 3 * LANES, 3 * LANES), 3 * LANES)
+        weight = rows_of(store[h // GROUP_PAIRS, :, :, :, :, :, columns])
+        qkv[...] = (dot_over(rows, weight, 1, 0) + shift).astype(BF16)
     else:
         qkv[...] = (dot_over(rows, weight[...], 1, 0) + bias[0]).astype(BF16)
     query = qkv[:, 0:LANES] * BF16(SCALE)
@@ -593,7 +586,7 @@
         input_grad, weight_grads, sums, masks, kept, total = refs[8:]
     pl.when(i == 0)(lambda: fill_masks(ids_row, ids_column, masks))
     length = qkv.shape[0]
-    chunk = length // 2
+    chunk = length
     wide = pl.ds(pl.multiple_of(h * 3 * LANES, 3 * LANES), 3 * LANES)
     tall = pl.ds(pl.multiple_of(b * length, length), length)
 
@@ -720,7 +713,7 @@
         out_shape += [jax.ShapeDtypeStruct(shape, BF16) for shape in shapes]
         out_specs += [in_place] * len(shapes)
         scratch += [pltpu.VMEM((2 * PAIRS, 1, LANES), F32)]
-        scratch += [pltpu.VMEM(grid3 + b.shape, BF16) for b in blocks[:GROUPS]]
+        scratch += [pltpu.VMEM((GROUPS, *grid3, *blocks[0].shape), BF16)]
         scratch += gather_sems(len(blocks), depth) + [pltpu.SemaphoreType.DMA((GROUPS + 1,))]
         operands = blocks
     else:

time: 407 us -> 395 us (0.971); the launches traced: 401 us -> 394 us
  Pallas kernels: 371 us -> 365 us
    pallas_call x1, Pallas kernels: 85.2 us -> 80.6 us  [attend(): pl.pallas_call(functools.partial(attend_kernel, depth, len(blocks), count...]
where the time goes in v5:
time: 395 us; the launch traced here: 394 us
  Pallas kernels  365 us (92%)
  other arithmetic  14.6 us (4%)
  local copies, waits for them, and re-layouts  13.8 us (3%)
    pallas_call x1, Pallas kernels, attend_back(): pl.pallas_call(functools.partial(attend_back_kernel, depth, seqs, per_dev...  98.4 us
    pallas_call x1, Pallas kernels, attend(): pl.pallas_call(functools.partial(attend_kernel, depth, len(blocks), count...  80.6 us
    pallas_call x1, Pallas kernels, widen_back(): pl.pallas_call(functools.partial(widen_back_kernel, depth, tiles), grid=(...  80.4 us
    pallas_call x1, Pallas kernels, widen(): pl.pallas_call(functools.partial(widen_kernel, depth, tiles), grid=(tiles...  73.7 us
    pallas_call x1, Pallas kernels, project_back(): row_call(project_back_kernel, count, [block, block, block, row_block(1),...  14.9 us
    convert_element_type x4, other arithmetic, adam_update(): return (grad, one_new, two_new, master_new, master_new.astype(BF16))  8.96 us
    pallas_call x1, Pallas kernels, project(): row_call(project_kernel, count, [block, block, matrix, flat(scales.shape)...  8.63 us
    pallas_call x1, Pallas kernels, output_and_grad(): row_call(output_kernel, count, [block, block, flat(scales.shape)], [block...  8.04 us

profile of v5, /device:TPU:0, one launch (start us, length us, event | category | flops | bytes accessed | tf_op | source)
XLA Modules:
  0.0 394.2 jit_solution(15294827288366197628)
XLA Ops:
  0.7 0.0 copy-start.15
  0.7 0.0 copy-start.7
  0.7 1.1 convert_element_type.47
  1.7 0.1 copy.45
  1.9 0.2 reshape.130
  2.0 0.7 fusion.18
  2.7 0.7 convert_bitcast_fusion
  3.4 0.6 fusion.5.refs_3_
  4.0 1.1 convert_element_type.50
  5.1 0.1 reshape.133
  5.2 0.7 fusion.17
  5.9 1.7 copy.46.refs_1_
  7.6 0.0 copy-done.15
  7.6 0.6 reshape.128.refs_0_
  8.2 0.0 copy-done.7
  8.2 0.7 reshape.132.refs_7_
  8.9 80.6 %attend.1 = (bf16[1024,3072]{1,0:T(8,128)(2,1)}, bf16[1024,1024]{1,0:T(8,128)(2,1)}, f32[2,8,2,512]{3,2,1,0:T(2,128)}, bf16[4,2,2,2,32,3072]{5,4,3,2,1,0:T(8,128...) custom-call(s32[2,1,512]{2,1,0:T(1,128)} %reshape.128.refs_0_, ...), custom_call_target="tpu_custom_call" | custom-call | tf_op jit(solution)/shard_map/attend/pallas_call | solution.py:722
  89.5 0.8 slice_convert_fusion
  90.4 0.7 select_maximum_fusion.1
  91.1 8.6 %project_kernel.1 = (f32[1024,1024]{1,0:T(8,128)}, f32[1024,1]{1,0:T(8,128)}, bf16[1024,1024]{1,0:T(8,128)(2,1)}, bf16[1024,1024]{1,0:T(8,128)(2,1)}) custom-call(bf16[1024,1024]{1,0:T(8,128)(2,1)} %get-tuple-element.63.attended, bf16[1024,1024]{1,0:T(8,128)(2,1)} %refs_2_.3, bf16[1024,1024]{1,0:T(8,128)(2,1)} %bitcast.42, f32[8,1024]{1,0:T(8,128)} %get-tuple-element.139.scales), custom_call_target="tpu_custom_call" | custom-call | tf_op jit(solution)/shard_map/project_kernel/pallas_call | solution.py:1169
  99.7 0.6 slice.93
  100.3 0.0 copy-done.2
  100.3 0.8 reshape.137.refs_6_
  101.1 73.7 %widen.1 = (bf16[1024,4096]{1,0:T(8,128)(2,1)}, f32[1024,4096]{1,0:T(8,128)}, f32[1024,1024]{1,0:T(8,128)}, bf16[4,2,2,2,32,2048]{5,4,3,2,1,0:T(8,128)(2,1)}, bf16[4,2,2,2,128,1024]{5,4,3,2,1,0:T(8,128)(2,1)}) custom-call(bf16[1024,1024]{1,0:T(8,128)(2,1)} %get-tuple-element.66.refs_0_, bf16[1024,2048]{1,0:T(8,128)(2,1)} %bitcast.40, f32[1,4096]{1,0:T(1,128)} %bitcast.63, ...), custom_call_target="tpu_custom_call" | custom-call | tf_op jit(solution)/shard_map/widen/pallas_call | solution.py:931
  174.8 0.6 select_maximum_fusion.scales
  175.5 8.0 %output_kernel.1 = (bf16[1024,1024]{1,0:T(8,128)(2,1)}, bf16[1024,1024]{1,0:T(8,128)(2,1)}, f32[1024,1024]{1,0:T(8,128)}, f32[8,1024]{1,0:T(8,128)}) custom-call(f32[1024,1024]{1,0:T(8,128)} %get-tuple-element.69.second_in, bf16[1024,1024]{1,0:T(8,128)(2,1)} %cotangent.1, f32[8,1024]{1,0:T(8,128)} %select_maximum_fusion.scales), custom_call_target="tpu_custom_call" | custom-call | tf_op jit(solution)/shard_map/output_kernel/pallas_call | solution.py:1182
  183.5 80.4 %widen_back.1 = (bf16[1024,4096]{1,0:T(8,128)(2,1)}, f32[1024,1024]{1,0:T(8,128)}, f32[8,1,512]{2,1,0:T(1,128)}, f32[128,1024]{1,0:T(8,128)}) custom-call(bf16[1024,1024]{1,0:T(8,128)(2,1)} %get-tuple-element.72.refs_0_, bf16[1024,4096]{1,0:T(8,128)(2,1)} %get-tuple-element.73.refs_1_, f32[1024,4096]{1,0:T(8,128)} %get-tuple-element.74.refs_2_, ...), custom_call_target="tpu_custom_call" | custom-call | tf_op jit(solution)/shard_map/widen_back/pallas_call | solution.py:1039
  263.9 0.0 copy-start.16
  263.9 14.9 %project_back_kernel.1 = (f32[1024,1024]{1,0:T(8,128)}, bf16[1024,1024]{1,0:T(8,128)(2,1)}, bf16[1024,1024]{1,0:T(8,128)(2,1)}, f32[8,1024]{1,0:T(8,128)}) custom-call(f32[1024,1024]{1,0:T(8,128)} %get-tuple-element.78.branch_grad, f32[1024,1024]{1,0:T(8,128)} %get-tuple-element.79.second_grad, f32[1024,1024]{1,0:T(8,128)} %get-tuple-element.68.refs_3_.normed, ...), custom_call_target="tpu_custom_call" | custom-call | tf_op jit(solution)/shard_map/project_back_kernel/pallas_call | solution.py:1195
  278.8 0.9 fusion.21
  279.7 0.0 copy-done.16
  279.8 0.9 fusion.20
  280.7 0.7 pad.28
  281.4 98.4 %attend_back.1 = (bf16[1024,1024]{1,0:T(8,128)(2,1)}, f32[32,4096]{1,0:T(8,128)}, f32[32,1024]{1,0:T(8,128)}, f32[32,768]{1,0:T(8,128)}, f32[32,768]{1,0:T(8,128...) custom-call(s32[2,1,512]{2,1,0:T(1,128)} %reshape.128.refs_0_, s32[2,512,1]{2,1,0:T(8,128)} %copy.46.refs_1_, ...), custom_call_target="tpu_custom_call" | custom-call | tf_op jit(solution)/shard_map/attend_back/pallas_call | solution.py:793
  379.8 1.1 copy.50
  381.0 0.0 copy-start.3
  381.0 1.3 copy.51
  382.3 0.0 copy-start.4
  382.3 0.0 copy-start.11
  382.3 0.0 copy-start.12
  382.3 0.0 copy-start.13
  382.4 0.0 copy-start.14
  382.4 0.0 copy-done.1
  382.4 0.0 copy-start.6
  382.4 4.1 %fusion.9 = (bf16[131072]{0:T(1024)(128)(2,1)}, f32[131072]{0:T(1024)}, f32[131072]{0:T(1024)}, f32[131072]{0:T(1024)}, bf16[131072]{0:T(1024)(128)(2,1)}, /*ind...) fusion(f32[131072]{0:T(1024)} %param.30, f32[131072]{0:T(1024)S(1)} %bitcast.52, f32[131072]{0:T(1024)} %param.32, ...), kind=kLoop, calls=%fused_computation.43 | loop fusion | flops 3932160 | bytes 7864320 | tf_op jit(solution)/shard_map/convert_element_type | solution.py:1387
  386.5 0.0 copy-done.3
  386.5 0.0 copy-start.18
  386.5 0.0 copy-start.19
  386.5 0.0 copy-start
  386.5 0.0 copy-done.4
  386.6 0.3 reshape.146
  386.9 0.0 copy-start.9
  386.9 0.0 copy-start.10
  386.9 0.0 copy-start.5
  387.0 2.8 fusion.15
  389.7 0.9 copy.49
  390.7 0.0 copy-start.8
  390.7 0.0 copy-done.9
  390.7 0.0 copy-done.10
  390.7 0.8 fusion.13
  391.5 0.0 copy-done.19
  391.5 1.3 fusion.7
  392.8 0.0 copy-done
  392.8 1.3 copy.60
  (27 shorter events, 0.2 us)
Async XLA Ops:
  0.7 7.0 %copy-start.15 = (s32[2,512]{1,0:T(2,128)S(1)}, s32[2,512]{1,0:T(2,128)}, u32[]{:S(2)}) copy-start(s32[2,512]{1,0:T(2,128)} %param.19) | copy-start | bytes 12292
  0.7 7.5 %copy-start.7 = (f32[32768]{0:T(1024)S(1)}, f32[32768]{0:T(1024)}, u32[]{:S(2)}) copy-start(f32[32768]{0:T(1024)} %param.24) | copy-start | bytes 393220
  8.9 91.4 %copy-start.2 = (f32[131072]{0:T(1024)S(1)}, f32[131072]{0:T(1024)}, u32[]{:S(2)}) copy-start(f32[131072]{0:T(1024)} %param.30) | copy-start | bytes 1572868
  263.9 15.9 %copy-start.16 = (f32[8,1,512]{2,1,0:T(1,128)S(1)}, f32[8,1,512]{2,1,0:T(1,128)}, u32[]{:S(2)}) copy-start(f32[8,1,512]{2,1,0:T(1,128)} %get-tuple-element.88) | copy-start | bytes 49156
  281.4 100.9 %copy-start.1 = (f32[131072]{0:T(1024)S(1)}, f32[131072]{0:T(1024)}, u32[]{:S(2)}) copy-start(f32[131072]{0:T(1024)} %param.27) | copy-start | bytes 1572868
  381.0 5.5 %copy-start.3 = (f32[4,32,8,128]{3,1,2,0:T(8,128)}, f32[4,32,8,128]{3,1,2,0:T(8,128)S(1)}, u32[]{:S(2)}) copy-start(f32[4,32,8,128]{3,1,2,0:T(8,128)S(1)} %copy.50) | copy-start | bytes 1572868
  382.3 4.2 %copy-start.4 = (f32[16,8,8,128]{3,1,2,0:T(8,128)}, f32[16,8,8,128]{3,1,2,0:T(8,128)S(1)}, u32[]{:S(2)}) copy-start(f32[16,8,8,128]{3,1,2,0:T(8,128)S(1)} %copy.51) | copy-start | bytes 1572868
  382.3 4.2 %copy-start.11 = (f32[32,768]{1,0:T(8,128)S(1)}, f32[32,768]{1,0:T(8,128)}, u32[]{:S(2)}) copy-start(f32[32,768]{1,0:T(8,128)} %get-tuple-element.91) | copy-start | bytes 294916
  382.3 4.2 %copy-start.12 = (f32[32,768]{1,0:T(8,128)S(1)}, f32[32,768]{1,0:T(8,128)}, u32[]{:S(2)}) copy-start(f32[32,768]{1,0:T(8,128)} %get-tuple-element.92) | copy-start | bytes 294916
  382.3 4.2 %copy-start.13 = (f32[32,768]{1,0:T(8,128)S(1)}, f32[32,768]{1,0:T(8,128)}, u32[]{:S(2)}) copy-start(f32[32,768]{1,0:T(8,128)} %get-tuple-element.93) | copy-start | bytes 294916
  382.4 4.2 %copy-start.14 = (f32[32,768]{1,0:T(8,128)S(1)}, f32[32,768]{1,0:T(8,128)}, u32[]{:S(2)}) copy-start(f32[32,768]{1,0:T(8,128)} %get-tuple-element.94) | copy-start | bytes 294916
  382.4 4.6 %copy-start.6 = (f32[98304]{0:T(1024)S(1)}, f32[98304]{0:T(1024)}, u32[]{:S(2)}) copy-start(f32[98304]{0:T(1024)} %param.21) | copy-start | bytes 1179652
  386.5 5.1 %copy-start.17 = (f32[384]{0:T(512)S(1)}, f32[384]{0:T(512)}, u32[]{:S(2)}) copy-start(f32[384]{0:T(512)} %param.33) | copy-start | bytes 4612
  386.5 5.1 %copy-start.18 = (f32[384]{0:T(512)S(1)}, f32[384]{0:T(512)}, u32[]{:S(2)}) copy-start(f32[384]{0:T(512)} %param.35) | copy-start | bytes 4612
  386.5 5.1 %copy-start.19 = (f32[384]{0:T(512)S(1)}, f32[384]{0:T(512)}, u32[]{:S(2)}) copy-start(f32[384]{0:T(512)} %param.34) | copy-start | bytes 4612
  386.5 6.3 %copy-start = (bf16[1024,1024]{1,0:T(8,128)(2,1)S(1)}, bf16[1024,1024]{1,0:T(8,128)(2,1)}, u32[]{:S(2)}) copy-start(bf16[1024,1024]{1,0:T(8,128)(2,1)} %get-tuple-element.173) | copy-start | bytes 6291460
  386.9 3.8 copy-start.9
  386.9 3.8 copy-start.10
  386.9 7.2 %copy-start.5 = (f32[32,3,8,128]{3,2,1,0:T(8,128)}, f32[32,3,8,128]{3,2,1,0:T(8,128)S(1)}, u32[]{:S(2)}) copy-start(f32[32,3,8,128]{3,2,1,0:T(8,128)S(1)} %copy.48) | copy-start | bytes 1179652
  390.7 3.5 copy-start.8

commit v6 on v5

--- a/solution.py
+++ b/solution.py
@@ -548,18 +548,18 @@
         put(0, side.start, proj)
         for n, k in enumerate(side.order):
             put(1 + 2 * n, side.first, up, k)
-            put(4 + 2 * n + n // 2, side.second, up, k)
-            put(7 + 2 * n + n // 2, side.third, up, k)
+            put(4 + 2 * n + (n + 1) // 2, side.second, up, k)
+            put(8 + 2 * n + (n + 1) // 2, side.third, up, k)
         put(2, each, side.first, proj)
-        put(5, each, side.second, proj)
-        put(8, each, side.third, proj)
+        put(7, each, side.second, proj)
+        put(12, each, side.third, proj)
         per = steps // GROUPS
         for g in range(GROUPS):
             at = per * (g + 1)
             put(at, each, side.begin, 2 + g)
             put(at + 1, each, side.first, 2 + g)
-            put(at + min(4, GROUPS + 1 - g), each, side.second, 2 + g)
-            put(at + min(7, GROUPS + 2 - g), each, side.third, 2 + g)
+            put(at + (7, 6, 4, 2)[g], each, side.second, 2 + g)
+            put(at + (10, 8, 5, 3)[g], each, side.third, 2 + g)
         rows_each = per_device
 
         def make_vector():

time: 395 us -> 391 us (0.990)
  Pallas kernels: 365 us -> 361 us
    pallas_call x1, Pallas kernels: 98.4 us -> 94.4 us  [attend_back(): pl.pallas_call(functools.partial(attend_back_kernel, depth, seqs, per_dev...]
where the time goes in v6:
time: 391 us; the launch traced here: 390 us
  Pallas kernels  361 us (92%)
  other arithmetic  14.6 us (4%)
  local copies, waits for them, and re-layouts  13.8 us (4%)
    pallas_call x1, Pallas kernels, attend_back(): pl.pallas_call(functools.partial(attend_back_kernel, depth, seqs, per_dev...  94.4 us
    pallas_call x1, Pallas kernels, attend(): pl.pallas_call(functools.partial(attend_kernel, depth, len(blocks), count...  80.6 us
    pallas_call x1, Pallas kernels, widen_back(): pl.pallas_call(functools.partial(widen_back_kernel, depth, tiles), grid=(...  80.4 us
    pallas_call x1, Pallas kernels, widen(): pl.pallas_call(functools.partial(widen_kernel, depth, tiles), grid=(tiles...  73.7 us
    pallas_call x1, Pallas kernels, project_back(): row_call(project_back_kernel, count, [block, block, block, row_block(1),...  14.9 us
    convert_element_type x4, other arithmetic, adam_update(): return (grad, one_new, two_new, master_new, master_new.astype(BF16))  8.96 us
    pallas_call x1, Pallas kernels, project(): row_call(project_kernel, count, [block, block, matrix, flat(scales.shape)...  8.63 us
    pallas_call x1, Pallas kernels, output_and_grad(): row_call(output_kernel, count, [block, block, flat(scales.shape)], [block...  8.04 us

profile of v6, /device:TPU:0, one launch (start us, length us, event | category | flops | bytes accessed | tf_op | source)
XLA Modules:
  0.0 390.2 jit_solution(3163851462803309640)
XLA Ops:
  0.7 0.0 copy-start.15
  0.7 0.0 copy-start.7
  0.7 1.1 convert_element_type.47
  1.7 0.1 copy.45
  1.9 0.2 reshape.130
  2.0 0.7 fusion.18
  2.7 0.7 convert_bitcast_fusion
  3.4 0.6 fusion.5.refs_3_
  4.0 1.1 convert_element_type.50
  5.1 0.1 reshape.133
  5.2 0.7 fusion.17
  5.9 1.7 copy.46.refs_1_
  7.6 0.0 copy-done.15
  7.6 0.6 reshape.128.refs_0_
  8.2 0.0 copy-done.7
  8.2 0.7 reshape.132.refs_7_
  8.9 80.6 %attend.1 = (bf16[1024,3072]{1,0:T(8,128)(2,1)}, bf16[1024,1024]{1,0:T(8,128)(2,1)}, f32[2,8,2,512]{3,2,1,0:T(2,128)}, bf16[4,2,2,2,32,3072]{5,4,3,2,1,0:T(8,128...) custom-call(s32[2,1,512]{2,1,0:T(1,128)} %reshape.128.refs_0_, ...), custom_call_target="tpu_custom_call" | custom-call | tf_op jit(solution)/shard_map/attend/pallas_call | solution.py:722
  89.5 0.8 slice_convert_fusion
  90.4 0.7 select_maximum_fusion.1
  91.1 8.6 %project_kernel.1 = (f32[1024,1024]{1,0:T(8,128)}, f32[1024,1]{1,0:T(8,128)}, bf16[1024,1024]{1,0:T(8,128)(2,1)}, bf16[1024,1024]{1,0:T(8,128)(2,1)}) custom-call(bf16[1024,1024]{1,0:T(8,128)(2,1)} %get-tuple-element.63.attended, bf16[1024,1024]{1,0:T(8,128)(2,1)} %refs_2_.3, bf16[1024,1024]{1,0:T(8,128)(2,1)} %bitcast.42, f32[8,1024]{1,0:T(8,128)} %get-tuple-element.139.scales), custom_call_target="tpu_custom_call" | custom-call | tf_op jit(solution)/shard_map/project_kernel/pallas_call | solution.py:1169
  99.7 0.6 slice.93
  100.3 0.0 copy-done.2
  100.3 0.8 reshape.137.refs_6_
  101.1 73.7 %widen.1 = (bf16[1024,4096]{1,0:T(8,128)(2,1)}, f32[1024,4096]{1,0:T(8,128)}, f32[1024,1024]{1,0:T(8,128)}, bf16[4,2,2,2,32,2048]{5,4,3,2,1,0:T(8,128)(2,1)}, bf16[4,2,2,2,128,1024]{5,4,3,2,1,0:T(8,128)(2,1)}) custom-call(bf16[1024,1024]{1,0:T(8,128)(2,1)} %get-tuple-element.66.refs_0_, bf16[1024,2048]{1,0:T(8,128)(2,1)} %bitcast.40, f32[1,4096]{1,0:T(1,128)} %bitcast.63, ...), custom_call_target="tpu_custom_call" | custom-call | tf_op jit(solution)/shard_map/widen/pallas_call | solution.py:931
  174.8 0.6 select_maximum_fusion.scales
  175.5 8.0 %output_kernel.1 = (bf16[1024,1024]{1,0:T(8,128)(2,1)}, bf16[1024,1024]{1,0:T(8,128)(2,1)}, f32[1024,1024]{1,0:T(8,128)}, f32[8,1024]{1,0:T(8,128)}) custom-call(f32[1024,1024]{1,0:T(8,128)} %get-tuple-element.69.second_in, bf16[1024,1024]{1,0:T(8,128)(2,1)} %cotangent.1, f32[8,1024]{1,0:T(8,128)} %select_maximum_fusion.scales), custom_call_target="tpu_custom_call" | custom-call | tf_op jit(solution)/shard_map/output_kernel/pallas_call | solution.py:1182
  183.5 80.4 %widen_back.1 = (bf16[1024,4096]{1,0:T(8,128)(2,1)}, f32[1024,1024]{1,0:T(8,128)}, f32[8,1,512]{2,1,0:T(1,128)}, f32[128,1024]{1,0:T(8,128)}) custom-call(bf16[1024,1024]{1,0:T(8,128)(2,1)} %get-tuple-element.72.refs_0_, bf16[1024,4096]{1,0:T(8,128)(2,1)} %get-tuple-element.73.refs_1_, f32[1024,4096]{1,0:T(8,128)} %get-tuple-element.74.refs_2_, ...), custom_call_target="tpu_custom_call" | custom-call | tf_op jit(solution)/shard_map/widen_back/pallas_call | solution.py:1039
  263.9 0.0 copy-start.16
  263.9 14.9 %project_back_kernel.1 = (f32[1024,1024]{1,0:T(8,128)}, bf16[1024,1024]{1,0:T(8,128)(2,1)}, bf16[1024,1024]{1,0:T(8,128)(2,1)}, f32[8,1024]{1,0:T(8,128)}) custom-call(f32[1024,1024]{1,0:T(8,128)} %get-tuple-element.78.branch_grad, f32[1024,1024]{1,0:T(8,128)} %get-tuple-element.79.second_grad, f32[1024,1024]{1,0:T(8,128)} %get-tuple-element.68.refs_3_.normed, ...), custom_call_target="tpu_custom_call" | custom-call | tf_op jit(solution)/shard_map/project_back_kernel/pallas_call | solution.py:1195
  278.8 0.9 fusion.21
  279.7 0.0 copy-done.16
  279.8 0.9 fusion.20
  280.7 0.7 pad.28
  281.4 94.4 %attend_back.1 = (bf16[1024,1024]{1,0:T(8,128)(2,1)}, f32[32,4096]{1,0:T(8,128)}, f32[32,1024]{1,0:T(8,128)}, f32[32,768]{1,0:T(8,128)}, f32[32,768]{1,0:T(8,128...) custom-call(s32[2,1,512]{2,1,0:T(1,128)} %reshape.128.refs_0_, s32[2,512,1]{2,1,0:T(8,128)} %copy.46.refs_1_, ...), custom_call_target="tpu_custom_call" | custom-call | tf_op jit(solution)/shard_map/attend_back/pallas_call | solution.py:793
  375.9 1.1 copy.50
  377.0 0.0 copy-start.3
  377.0 1.3 copy.51
  378.3 0.0 copy-start.4
  378.3 0.0 copy-start.11
  378.4 0.0 copy-start.12
  378.4 0.0 copy-start.13
  378.4 0.0 copy-start.6
  378.4 4.1 %fusion.9 = (bf16[131072]{0:T(1024)(128)(2,1)}, f32[131072]{0:T(1024)}, f32[131072]{0:T(1024)}, f32[131072]{0:T(1024)}, bf16[131072]{0:T(1024)(128)(2,1)}, /*ind...) fusion(f32[131072]{0:T(1024)} %param.30, f32[131072]{0:T(1024)S(1)} %bitcast.52, f32[131072]{0:T(1024)} %param.32, ...), kind=kLoop, calls=%fused_computation.43 | loop fusion | flops 3932160 | bytes 7864320 | tf_op jit(solution)/shard_map/convert_element_type | solution.py:1387
  382.5 0.0 copy-done.3
  382.5 0.0 copy-start.18
  382.5 0.0 copy-start.19
  382.5 0.0 copy-start
  382.5 0.0 copy-done.4
  382.5 0.0 copy-done.11
  382.5 0.0 copy-done.12
  382.6 0.0 copy-done.13
  382.6 0.0 copy-done.14
  382.6 0.3 reshape.146
  382.9 0.0 copy-start.9
  382.9 0.0 copy-start.10
  383.0 0.0 copy-start.5
  383.0 2.8 fusion.15
  385.8 0.9 copy.49
  386.7 0.0 copy-start.8
  386.7 0.8 fusion.13
  387.6 0.0 copy-done.17
  387.6 1.3 fusion.7
  388.9 1.3 copy.60
  390.2 0.0 copy-done.8
  (27 shorter events, 0.2 us)
Async XLA Ops:
  0.7 7.0 %copy-start.15 = (s32[2,512]{1,0:T(2,128)S(1)}, s32[2,512]{1,0:T(2,128)}, u32[]{:S(2)}) copy-start(s32[2,512]{1,0:T(2,128)} %param.19) | copy-start | bytes 12292
  0.7 7.5 %copy-start.7 = (f32[32768]{0:T(1024)S(1)}, f32[32768]{0:T(1024)}, u32[]{:S(2)}) copy-start(f32[32768]{0:T(1024)} %param.24) | copy-start | bytes 393220
  8.9 91.4 %copy-start.2 = (f32[131072]{0:T(1024)S(1)}, f32[131072]{0:T(1024)}, u32[]{:S(2)}) copy-start(f32[131072]{0:T(1024)} %param.30) | copy-start | bytes 1572868
  263.9 15.9 %copy-start.16 = (f32[8,1,512]{2,1,0:T(1,128)S(1)}, f32[8,1,512]{2,1,0:T(1,128)}, u32[]{:S(2)}) copy-start(f32[8,1,512]{2,1,0:T(1,128)} %get-tuple-element.88) | copy-start | bytes 49156
  281.4 97.0 %copy-start.1 = (f32[131072]{0:T(1024)S(1)}, f32[131072]{0:T(1024)}, u32[]{:S(2)}) copy-start(f32[131072]{0:T(1024)} %param.27) | copy-start | bytes 1572868
  377.0 5.5 %copy-start.3 = (f32[4,32,8,128]{3,1,2,0:T(8,128)}, f32[4,32,8,128]{3,1,2,0:T(8,128)S(1)}, u32[]{:S(2)}) copy-start(f32[4,32,8,128]{3,1,2,0:T(8,128)S(1)} %copy.50) | copy-start | bytes 1572868
  378.3 4.2 %copy-start.4 = (f32[16,8,8,128]{3,1,2,0:T(8,128)}, f32[16,8,8,128]{3,1,2,0:T(8,128)S(1)}, u32[]{:S(2)}) copy-start(f32[16,8,8,128]{3,1,2,0:T(8,128)S(1)} %copy.51) | copy-start | bytes 1572868
  378.3 4.2 %copy-start.11 = (f32[32,768]{1,0:T(8,128)S(1)}, f32[32,768]{1,0:T(8,128)}, u32[]{:S(2)}) copy-start(f32[32,768]{1,0:T(8,128)} %get-tuple-element.91) | copy-start | bytes 294916
  378.4 4.2 %copy-start.12 = (f32[32,768]{1,0:T(8,128)S(1)}, f32[32,768]{1,0:T(8,128)}, u32[]{:S(2)}) copy-start(f32[32,768]{1,0:T(8,128)} %get-tuple-element.92) | copy-start | bytes 294916
  378.4 4.2 %copy-start.13 = (f32[32,768]{1,0:T(8,128)S(1)}, f32[32,768]{1,0:T(8,128)}, u32[]{:S(2)}) copy-start(f32[32,768]{1,0:T(8,128)} %get-tuple-element.93) | copy-start | bytes 294916
  378.4 4.2 %copy-start.14 = (f32[32,768]{1,0:T(8,128)S(1)}, f32[32,768]{1,0:T(8,128)}, u32[]{:S(2)}) copy-start(f32[32,768]{1,0:T(8,128)} %get-tuple-element.94) | copy-start | bytes 294916
  378.4 4.6 %copy-start.6 = (f32[98304]{0:T(1024)S(1)}, f32[98304]{0:T(1024)}, u32[]{:S(2)}) copy-start(f32[98304]{0:T(1024)} %param.21) | copy-start | bytes 1179652
  382.5 5.1 %copy-start.17 = (f32[384]{0:T(512)S(1)}, f32[384]{0:T(512)}, u32[]{:S(2)}) copy-start(f32[384]{0:T(512)} %param.33) | copy-start | bytes 4612
  382.5 5.1 %copy-start.18 = (f32[384]{0:T(512)S(1)}, f32[384]{0:T(512)}, u32[]{:S(2)}) copy-start(f32[384]{0:T(512)} %param.35) | copy-start | bytes 4612
  382.5 5.1 %copy-start.19 = (f32[384]{0:T(512)S(1)}, f32[384]{0:T(512)}, u32[]{:S(2)}) copy-start(f32[384]{0:T(512)} %param.34) | copy-start | bytes 4612
  382.5 6.3 %copy-start = (bf16[1024,1024]{1,0:T(8,128)(2,1)S(1)}, bf16[1024,1024]{1,0:T(8,128)(2,1)}, u32[]{:S(2)}) copy-start(bf16[1024,1024]{1,0:T(8,128)(2,1)} %get-tuple-element.173) | copy-start | bytes 6291460
  382.9 3.8 copy-start.9
  382.9 3.8 copy-start.10
  383.0 7.2 %copy-start.5 = (f32[32,3,8,128]{3,2,1,0:T(8,128)}, f32[32,3,8,128]{3,2,1,0:T(8,128)S(1)}, u32[]{:S(2)}) copy-start(f32[32,3,8,128]{3,2,1,0:T(8,128)S(1)} %copy.48) | copy-start | bytes 1179652
  386.7 3.5 copy-start.8
